TPU v7x, 512 devices: a 4x2x32 block of a 4x8x32 slice. The times are simulated.
512 devices in a mesh: groups: 2 (over y), tm: 128 (over z, x), space: 2 (over core).
Axes of the slice: x: 4, y: 2, z: 32, core: 2. Of those that a mesh axis runs over, the one named last changes fastest.
The devices are a block of a 4x8x32 slice.
Arguments:
- iterate: float32 [256, 16, 16, 128], P(('groups', 'tm'), 'space'), parts along dimension 0, may hold values from -0.7 to 1.3
- source: float32 [256, 16, 16, 128], P(('groups', 'tm'), 'space'), parts along dimension 0, may hold values from -6 to 6
- diffusivity: float32 [32, 16, 128], P(('groups', 'space')), parts along dimension 0, may hold values from 0.1 to 1
Outputs:
- new_iterate: float32 [256, 16, 16, 128], P(('groups', 'tm'), 'space'), parts along dimension 0
- new_residual: float32 [256, 16, 16, 128], P(('groups', 'tm'), 'space'), parts along dimension 0
There are 2 independent parts, one for each index of `groups`. A program takes and returns all parts, laid end to end along the dimension named above; each array names one. Nothing has to cross between parts.
All inputs are finite; a program needn't handle non-finite values.
Results may differ from a plain program's by a relative error of at most 0.0019.
Values sent between devices are 32-bit elements; how exact they have to be, the bound alone decides.
No kernel may reach another device: no remote copies, remote signals or barrier semaphores. Data moves between devices by JAX's collectives and lax.ppermute only.
A program may use at most 64 MiB of HBM per device.

v0:
```python
import math

import jax
import jax.numpy as jnp
from jax import lax
from jax.sharding import Mesh
from jax.sharding import PartitionSpec as P

SWEEPS = 6
TM_SPACE = ("tm_0", "tm_1", "space")
TM = ("tm_0", "tm_1")
GROUPS_TM = ("groups", "tm_0", "tm_1")


frac_order = 0.3
step_length = 0.01
gamma_factor = 0.9086387328532904


def with_halo(value, sides, width):
    for axis, dim in sides:
        peers, length = (lax.axis_size(axis), value.shape[dim])
        up = [(i, (i + 1) % peers) for i in range(peers - 1)]
        down = [(j, i) for i, j in up]
        last = lax.slice_in_dim(value, length - width, length, axis=dim)
        first = lax.slice_in_dim(value, 0, width, axis=dim)
        before = lax.ppermute(last, axis, up)
        after = lax.ppermute(first, axis, down)
        value = jnp.concatenate([before, value, after], axis=dim)
    return value


def by_axis(value, axes):
    for axis in axes:
        value = lax.psum(value, axis)
    return value


def history_weights(lags):
    scale = 1.0 / (step_length**frac_order * gamma_factor)
    power = 1.0 - frac_order
    safe = jnp.maximum(lags, 0.0)
    upper = (safe + 1.0) ** power - safe**power
    lower = jnp.where(safe >= 1.0, safe**power - jnp.maximum(safe - 1.0, 0.0) ** power, 0.0)
    return jnp.where(lags >= 0.0, (upper - lower) * scale, 0.0)


def circulant_spectrum(freqs, total):
    lags = jnp.arange(total, dtype=jnp.int32)
    first = jnp.where(lags < total // 2, history_weights(lags.astype(jnp.float32)), 0.0)
    phase = (freqs[:, None] * lags[None, :] % total).astype(jnp.float32) * (2.0 * math.pi / total)
    real_part = jnp.sum(first[None, :] * jnp.cos(phase), axis=1)
    imag_part = -jnp.sum(first[None, :] * jnp.sin(phase), axis=1)
    return (real_part, imag_part)


def fourier_tables(total):
    index = jnp.arange(total, dtype=jnp.int32)
    phase = (index[:, None] * index[None, :] % total).astype(jnp.float32) * (2.0 * math.pi / total)
    return (jnp.cos(phase), jnp.sin(phase))


def neighbour_sum(padded):
    inner = padded[..., 1:-1, :, :]
    result = padded[..., 2:, :, :] + padded[..., :-2, :, :]
    along_y = jnp.pad(inner, [(0, 0)] * (inner.ndim - 2) + [(1, 1), (0, 0)])
    result = result + along_y[..., 2:, :] + along_y[..., :-2, :]
    along_x = jnp.pad(inner, [(0, 0)] * (inner.ndim - 1) + [(1, 1)])
    return result + along_x[..., 2:] + along_x[..., :-2]


def jacobi_step(
    spec_re, spec_im, sol_re, sol_im, stiff_re, stiff_im, lam_re, lam_im, inv_re, inv_im
):
    res_re = spec_re - (lam_re * sol_re - lam_im * sol_im) - stiff_re
    res_im = spec_im - (lam_re * sol_im + lam_im * sol_re) - stiff_im
    return (
        sol_re + (res_re * inv_re - res_im * inv_im),
        sol_im + (res_re * inv_im + res_im * inv_re),
    )


def stiffness_pair(sol_re, sol_im, diffusivity):
    stacked = jnp.stack([sol_re, sol_im])
    padded = with_halo(stacked, (("space", 2),), 1)
    stiff = diffusivity * (6.0 * stacked - neighbour_sum(padded))
    return (stiff[0], stiff[1])


def time_product(matrix, field):
    return jnp.dot(matrix, field, precision=lax.Precision.HIGHEST)


def inner_products(residual, image):
    return (by_axis(jnp.sum(residual * image), TM_SPACE), by_axis(jnp.sum(image * image), TM_SPACE))


def on_device(iterate, source, diffusivity):
    steps_here = iterate.shape[0]
    slab_shape = iterate.shape
    cells = slab_shape[1] * slab_shape[2] * slab_shape[3]
    total = steps_here * lax.axis_size(TM)
    my_times = lax.axis_index(TM) * steps_here + jnp.arange(steps_here, dtype=jnp.int32)
    times = jnp.arange(total, dtype=jnp.int32)
    toeplitz = history_weights((times[:, None] - times[None, :]).astype(jnp.float32))
    cos_table, sin_table = fourier_tables(total)
    padded = with_halo(iterate, (("space", 1),), 1)
    stiff_iter = diffusivity * (6.0 * iterate - neighbour_sum(padded))
    flat_iter = iterate.reshape(steps_here, cells)
    flat_source = source.reshape(steps_here, cells)
    flat_stiff = stiff_iter.reshape(steps_here, cells)
    iter_cols, source_cols, stiff_cols = (
        lax.all_to_all(flat_iter, TM, split_axis=1, concat_axis=0, tiled=True),
        lax.all_to_all(flat_source, TM, split_axis=1, concat_axis=0, tiled=True),
        lax.all_to_all(flat_stiff, TM, split_axis=1, concat_axis=0, tiled=True),
    )
    residual = source_cols - time_product(toeplitz, iter_cols) - stiff_cols
    spec_re = time_product(cos_table, residual)
    spec_im = -time_product(sin_table, residual)
    spec_re, spec_im = (
        lax.all_to_all(spec_re, TM, split_axis=0, concat_axis=1, tiled=True),
        lax.all_to_all(spec_im, TM, split_axis=0, concat_axis=1, tiled=True),
    )
    spec_re = spec_re.reshape(slab_shape)
    spec_im = spec_im.reshape(slab_shape)
    lam_re, lam_im = circulant_spectrum(my_times, total)
    lam_re = lam_re[:, None, None, None]
    lam_im = lam_im[:, None, None, None]
    diag_re = lam_re + 6.0 * diffusivity
    denom = diag_re * diag_re + lam_im * lam_im
    inv_re = diag_re / denom
    inv_im = -lam_im / denom
    sol_re = spec_re * inv_re - spec_im * inv_im
    sol_im = spec_re * inv_im + spec_im * inv_re
    for sweep in range(SWEEPS - 1):
        stiff_re, stiff_im = stiffness_pair(sol_re, sol_im, diffusivity)
        sol_re, sol_im = jacobi_step(
            spec_re, spec_im, sol_re, sol_im, stiff_re, stiff_im, lam_re, lam_im, inv_re, inv_im
        )
    sol_re, sol_im = (
        lax.all_to_all(
            sol_re.reshape(steps_here, cells), TM, split_axis=1, concat_axis=0, tiled=True
        ),
        lax.all_to_all(
            sol_im.reshape(steps_here, cells), TM, split_axis=1, concat_axis=0, tiled=True
        ),
    )
    correction = (time_product(cos_table, sol_re) - time_product(sin_table, sol_im)) / total
    history_term = time_product(toeplitz, correction)
    correction_slab, history_slab, residual_here = (
        lax.all_to_all(correction, TM, split_axis=0, concat_axis=1, tiled=True),
        lax.all_to_all(history_term, TM, split_axis=0, concat_axis=1, tiled=True),
        lax.all_to_all(residual, TM, split_axis=0, concat_axis=1, tiled=True),
    )
    correction_slab = correction_slab.reshape(slab_shape)
    residual_here = residual_here.reshape(slab_shape)
    padded_corr = with_halo(correction_slab, (("space", 1),), 1)
    stiff_corr = diffusivity * (6.0 * correction_slab - neighbour_sum(padded_corr))
    image = history_slab.reshape(slab_shape) + stiff_corr
    inner_ri, inner_ii = inner_products(residual_here, image)
    step = inner_ri / inner_ii
    return (iterate + step * correction_slab, residual_here - step * image)


def solution(mesh):
    split = Mesh(
        mesh.devices.reshape(mesh.shape["groups"], 32, 4, mesh.shape["space"]),
        ("groups", "tm_0", "tm_1", "space"),
    )
    placed = (
        P(GROUPS_TM, "space", None, None),
        P(GROUPS_TM, "space", None, None),
        P(("groups", "space"), None, None),
    )
    return jax.shard_map(
        on_device,
        mesh=split,
        in_specs=placed,
        out_specs=(P(GROUPS_TM, "space", None, None), P(GROUPS_TM, "space", None, None)),
        check_vma=False,
    )
```

profile of v0, /device:TPU:33, one launch (start us, length us, event | category | flops | bytes accessed | tf_op | source)
XLA Modules:
  0.0 483.4 jit_solution(9495237298354544404)
XLA Ops:
  0.6 74.0 %all_to_all.145 = f32[1,128,128]{2,0,1:T(1,128)S(1)} all-to-all(f32[1,128,128]{2,0,1:T(1,128)} %bitcast.339), channel_id=1, replica_groups=mesh['groups'=2,'tm_0'=32,'tm_1'=4,'space'=2] {'tm_0','tm_1'}, dimensions={1} | all-to-all | bytes 131072 | tf_op jit(solution)/shard_map/all_to_all | solution.py:114
  74.6 12.1 %all-to-all-start.1 = ((f32[1,128,128]{2,0,1:T(1,128)}), f32[1,128,128]{2,0,1:T(1,128)S(1)}, u32[]{:S(2)}, u32[]{:S(2)}) async-start(f32[1,128,128]{2,0,1:T(1,128)} %bitcast.2), calls=%async_computation.1 | async-start | bytes 131072 | tf_op jit(solution)/shard_map/all_to_all | solution.py:113
  87.5 3.8 collective-permute-start
  91.3 1.3 collective-permute-start.1
  92.7 1.8 collective-permute-done.1
  95.7 11.2 %all-to-all-done.1 = f32[1,128,128]{2,0,1:T(1,128)S(1)} async-done(((f32[1,128,128]{2,0,1:T(1,128)}), f32[1,128,128]{2,0,1:T(1,128)S(1)}, u32[]{:S(2)}, u32[]{:S(2)}) %all-to-all-start.1) | async-done | bytes 65568 | tf_op jit(solution)/shard_map/all_to_all | solution.py:113
  106.9 37.1 %all_to_all.146 = f32[1,128,128]{2,0,1:T(1,128)S(1)} all-to-all(f32[1,128,128]{2,0,1:T(1,128)S(1)} %bitcast.337), channel_id=1, replica_groups=mesh['groups'=2,'tm_0'=32,'tm_1'=4,'space'=2] {'tm_0','tm_1'}, dimensions={1} | all-to-all | bytes 131072 | tf_op jit(solution)/shard_map/all_to_all | solution.py:115
  145.0 1.9 convolution_negate_fusion
  147.0 11.9 %all-to-all-start.5 = ((f32[128,1,128]{2,1,0:T(1,128)}), f32[128,1,128]{2,1,0:T(1,128)S(1)}, u32[]{:S(2)}, u32[]{:S(2)}) async-start(f32[128,1,128]{2,1,0:T(1,128)} %bitcast.14), calls=%async_computation.5 | async-start | bytes 131072 | tf_op jit(solution)/shard_map/all_to_all | solution.py:122
  158.9 1.9 fusion.79
  160.8 18.5 %all-to-all-done.5 = f32[128,1,128]{2,1,0:T(1,128)S(1)} async-done(((f32[128,1,128]{2,1,0:T(1,128)}), f32[128,1,128]{2,1,0:T(1,128)S(1)}, u32[]{:S(2)}, u32[]{:S(2)}) %all-to-all-start.5) | async-done | bytes 65568 | tf_op jit(solution)/shard_map/all_to_all | solution.py:122
  179.3 11.0 %all-to-all-start.4 = ((f32[128,1,128]{2,1,0:T(1,128)}), f32[128,1,128]{2,1,0:T(1,128)S(1)}, u32[]{:S(2)}, u32[]{:S(2)}) async-start(f32[128,1,128]{2,1,0:T(1,128)} %bitcast.11), calls=%async_computation.4 | async-start | bytes 131072 | tf_op jit(solution)/shard_map/all_to_all | solution.py:121
  193.0 17.9 %all-to-all-done.4 = f32[128,1,128]{2,1,0:T(1,128)S(1)} async-done(((f32[128,1,128]{2,1,0:T(1,128)}), f32[128,1,128]{2,1,0:T(1,128)S(1)}, u32[]{:S(2)}, u32[]{:S(2)}) %all-to-all-start.4) | async-done | bytes 65568 | tf_op jit(solution)/shard_map/all_to_all | solution.py:121
  210.9 1.4 fusion.68
  212.2 5.5 %collective-permute-start.2 = (f32[2,1,1,16,128]{4,3,2,1,0:T(8,128)S(1)}, f32[2,1,1,16,128]{4,3,2,1,0:T(8,128)S(1)}, u32[]{:S(2)}, u32[]{:S(2)}) collective-permute-start(f32[2,1,1,16,128]{4,3,2,1,0:T(8,128)S(1)} %get-tuple-element.31), channel_id=1, source_target_pairs={{1,0},{3,2},{5,4},{7,6},{9,8},{11,10},{13,12},{15,14},{17,16},{19,... | collective-permute-start | bytes 49160 | tf_op jit(solution)/shard_map/ppermute | solution.py:28
  217.7 1.3 collective-permute-start.3
  219.1 1.8 collective-permute-done.3
  221.0 1.4 subtract_add_fusion.4
  222.4 2.1 collective-permute-start.4
  224.5 1.3 collective-permute-start.5
  225.9 1.8 collective-permute-done.5
  227.8 1.4 subtract_add_fusion.3
  229.2 2.1 collective-permute-start.6
  232.6 1.8 collective-permute-done.7
  234.6 1.4 fusion.94
  236.0 2.1 collective-permute-start.8
  238.1 1.3 collective-permute-start.9
  239.4 1.8 collective-permute-done.9
  241.3 1.4 add_add_fusion.1
  242.8 2.1 collective-permute-start.10
  244.9 1.3 collective-permute-start.11
  246.2 1.8 collective-permute-done.11
  248.1 1.4 add_add_fusion
  249.5 30.8 %all_to_all.147 = f32[1,128,128]{2,0,1:T(1,128)S(1)} all-to-all(f32[1,128,128]{2,0,1:T(1,128)S(1)} %bitcast.336), channel_id=1, replica_groups=mesh['groups'=2,'tm_0'=32,'tm_1'=4,'space'=2] {'tm_0','tm_1'}, dimensions={1} | all-to-all | bytes 131072 | tf_op jit(solution)/shard_map/all_to_all | solution.py:141
  280.3 32.0 %all_to_all.148 = f32[1,128,128]{2,0,1:T(1,128)S(1)} all-to-all(f32[1,128,128]{2,0,1:T(1,128)S(1)} %bitcast.335), channel_id=1, replica_groups=mesh['groups'=2,'tm_0'=32,'tm_1'=4,'space'=2] {'tm_0','tm_1'}, dimensions={1} | all-to-all | bytes 131072 | tf_op jit(solution)/shard_map/all_to_all | solution.py:144
  312.4 11.2 %all-to-all-start.3 = ((f32[128,1,128]{2,1,0:T(1,128)}), f32[128,1,128]{2,1,0:T(1,128)S(1)}, u32[]{:S(2)}, u32[]{:S(2)}) async-start(f32[128,1,128]{2,1,0:T(1,128)} %bitcast.8), calls=%async_computation.3 | async-start | bytes 131072 | tf_op jit(solution)/shard_map/all_to_all | solution.py:153
  325.1 19.0 %all-to-all-done.3 = f32[128,1,128]{2,1,0:T(1,128)S(1)} async-done(((f32[128,1,128]{2,1,0:T(1,128)}), f32[128,1,128]{2,1,0:T(1,128)S(1)}, u32[]{:S(2)}, u32[]{:S(2)}) %all-to-all-start.3) | async-done | bytes 65568 | tf_op jit(solution)/shard_map/all_to_all | solution.py:153
  344.1 10.2 %all-to-all-start.9 = ((f32[128,1,128]{2,1,0:T(1,128)}), f32[128,1,128]{2,1,0:T(1,128)S(1)}, u32[]{:S(2)}, u32[]{:S(2)}) async-start(f32[128,1,128]{2,1,0:T(1,128)} %bitcast.44), calls=%async_computation.9 | async-start | bytes 131072 | tf_op jit(solution)/shard_map/all_to_all | solution.py:151
  354.2 1.8 fusion.83
  356.1 18.7 %all-to-all-done.9 = f32[128,1,128]{2,1,0:T(1,128)S(1)} async-done(((f32[128,1,128]{2,1,0:T(1,128)}), f32[128,1,128]{2,1,0:T(1,128)S(1)}, u32[]{:S(2)}, u32[]{:S(2)}) %all-to-all-start.9) | async-done | bytes 65568 | tf_op jit(solution)/shard_map/all_to_all | solution.py:151
  374.8 10.1 %all-to-all-start.8 = ((f32[128,1,128]{2,1,0:T(1,128)}), f32[128,1,128]{2,1,0:T(1,128)S(1)}, u32[]{:S(2)}, u32[]{:S(2)}) async-start(f32[128,1,128]{2,1,0:T(1,128)} %bitcast.41), calls=%async_computation.8 | async-start | bytes 131072 | tf_op jit(solution)/shard_map/all_to_all | solution.py:152
  384.9 7.1 %collective-permute-start.12 = (f32[1,1,16,128]{3,2,1,0:T(8,128)S(1)}, f32[1,1,16,128]{3,2,1,0:T(8,128)S(1)}, u32[]{:S(2)}, u32[]{:S(2)}) collective-permute-start(f32[1,1,16,128]{3,2,1,0:T(8,128)S(1)} %get-tuple-element.33), channel_id=1, source_target_pairs={{1,0},{3,2},{5,4},{7,6},{9,8},{11,10},{13,12},{15,14},{17,16},{19,... | collective-permute-start | bytes 24584 | tf_op jit(solution)/shard_map/ppermute | solution.py:28
  392.0 1.3 collective-permute-start.13
  393.3 12.1 %all-to-all-done.8 = f32[128,1,128]{2,1,0:T(1,128)S(1)} async-done(((f32[128,1,128]{2,1,0:T(1,128)}), f32[128,1,128]{2,1,0:T(1,128)S(1)}, u32[]{:S(2)}, u32[]{:S(2)}) %all-to-all-start.8) | async-done | bytes 65568 | tf_op jit(solution)/shard_map/all_to_all | solution.py:152
  406.1 40.7 %all-reduce.14 = (f32[]{:T(128)}, f32[]{:T(128)}) all-reduce(f32[]{:T(128)} %get-tuple-element.3, f32[]{:T(128)} %get-tuple-element.2), channel_id=1, replica_groups=mesh['groups'=2,'tm_0'=32,'tm_1'=4,'space'=2] {'tm_0'}, use_global_device_ids=true, to_apply=%region_3.4 | all-reduce | flops 2 | bytes 16 | tf_op jit(solution)/shard_map/psum | solution.py:35
  446.8 7.8 %all-reduce.15 = (f32[]{:T(128)}, f32[]{:T(128)}) all-reduce(f32[]{:T(128)} %get-tuple-element.4, f32[]{:T(128)} %get-tuple-element.5), channel_id=1, replica_groups=mesh['groups'=2,'tm_0'=32,'tm_1'=4,'space'=2] {'tm_1'}, use_global_device_ids=true, to_apply=%region_4.5 | all-reduce | flops 2 | bytes 16 | tf_op jit(solution)/shard_map/psum | solution.py:35
  454.6 25.0 %all-reduce.16 = (f32[]{:T(128)}, f32[]{:T(128)}) all-reduce(f32[]{:T(128)} %get-tuple-element.6, f32[]{:T(128)} %get-tuple-element.7), channel_id=1, replica_groups=mesh['groups'=2,'tm_0'=32,'tm_1'=4,'space'=2] {'space'}, use_global_device_ids=true, to_apply=%region_5.6 | all-reduce | flops 2 | bytes 16 | tf_op jit(solution)/shard_map/psum | solution.py:35
  480.9 1.5 multiply_add_fusion
  (35 shorter events, 8.7 us)
Async XLA Ops:
  74.6 19.8 %copy-start = (f32[8,16,128]{2,1,0:T(8,128)S(1)}, f32[8,16,128]{2,1,0:T(8,128)}, u32[]{:S(2)}) copy-start(f32[8,16,128]{2,1,0:T(8,128)} %param.5) | copy-start | bytes 196612
  74.6 32.3 %all-to-all-start.1 = ((f32[1,128,128]{2,0,1:T(1,128)}), f32[1,128,128]{2,0,1:T(1,128)S(1)}, u32[]{:S(2)}, u32[]{:S(2)}) async-start(f32[1,128,128]{2,0,1:T(1,128)} %bitcast.2), calls=%async_computation.1 | async-start | bytes 131072 | tf_op jit(solution)/shard_map/all_to_all | solution.py:113
  87.5 5.2 %collective-permute-start = (f32[1,1,16,128]{3,2,1,0:T(8,128)S(1)}, f32[1,1,16,128]{3,2,1,0:T(8,128)S(1)}, u32[]{:S(2)}, u32[]{:S(2)}) collective-permute-start(f32[1,1,16,128]{3,2,1,0:T(8,128)S(1)} %get-tuple-element.35), channel_id=1, source_target_pairs={{1,0},{3,2},{5,4},{7,6},{9,8},{11,10},{13,12},{15,14},{17,16},{19,... | collective-permute-start | bytes 24584 | tf_op jit(solution)/shard_map/ppermute | solution.py:28
  91.3 3.1 collective-permute-start.1
  147.0 32.3 %all-to-all-start.5 = ((f32[128,1,128]{2,1,0:T(1,128)}), f32[128,1,128]{2,1,0:T(1,128)S(1)}, u32[]{:S(2)}, u32[]{:S(2)}) async-start(f32[128,1,128]{2,1,0:T(1,128)} %bitcast.14), calls=%async_computation.5 | async-start | bytes 131072 | tf_op jit(solution)/shard_map/all_to_all | solution.py:122
  179.3 31.6 %all-to-all-start.4 = ((f32[128,1,128]{2,1,0:T(1,128)}), f32[128,1,128]{2,1,0:T(1,128)S(1)}, u32[]{:S(2)}, u32[]{:S(2)}) async-start(f32[128,1,128]{2,1,0:T(1,128)} %bitcast.11), calls=%async_computation.4 | async-start | bytes 131072 | tf_op jit(solution)/shard_map/all_to_all | solution.py:121
  212.2 6.8 %collective-permute-start.2 = (f32[2,1,1,16,128]{4,3,2,1,0:T(8,128)S(1)}, f32[2,1,1,16,128]{4,3,2,1,0:T(8,128)S(1)}, u32[]{:S(2)}, u32[]{:S(2)}) collective-permute-start(f32[2,1,1,16,128]{4,3,2,1,0:T(8,128)S(1)} %get-tuple-element.31), channel_id=1, source_target_pairs={{1,0},{3,2},{5,4},{7,6},{9,8},{11,10},{13,12},{15,14},{17,16},{19,... | collective-permute-start | bytes 49160 | tf_op jit(solution)/shard_map/ppermute | solution.py:28
  217.7 3.1 collective-permute-start.3
  222.4 3.4 collective-permute-start.4
  224.5 3.1 collective-permute-start.5
  229.2 3.4 collective-permute-start.6
  231.3 3.1 collective-permute-start.7
  236.0 3.4 collective-permute-start.8
  238.1 3.1 collective-permute-start.9
  242.8 3.4 collective-permute-start.10
  244.9 3.1 collective-permute-start.11
  312.4 31.7 %all-to-all-start.3 = ((f32[128,1,128]{2,1,0:T(1,128)}), f32[128,1,128]{2,1,0:T(1,128)S(1)}, u32[]{:S(2)}, u32[]{:S(2)}) async-start(f32[128,1,128]{2,1,0:T(1,128)} %bitcast.8), calls=%async_computation.3 | async-start | bytes 131072 | tf_op jit(solution)/shard_map/all_to_all | solution.py:153
  344.1 30.7 %all-to-all-start.9 = ((f32[128,1,128]{2,1,0:T(1,128)}), f32[128,1,128]{2,1,0:T(1,128)S(1)}, u32[]{:S(2)}, u32[]{:S(2)}) async-start(f32[128,1,128]{2,1,0:T(1,128)} %bitcast.44), calls=%async_computation.9 | async-start | bytes 131072 | tf_op jit(solution)/shard_map/all_to_all | solution.py:151
  374.8 30.6 %all-to-all-start.8 = ((f32[128,1,128]{2,1,0:T(1,128)}), f32[128,1,128]{2,1,0:T(1,128)S(1)}, u32[]{:S(2)}, u32[]{:S(2)}) async-start(f32[128,1,128]{2,1,0:T(1,128)} %bitcast.41), calls=%async_computation.8 | async-start | bytes 131072 | tf_op jit(solution)/shard_map/all_to_all | solution.py:152
  384.9 20.5 %collective-permute-start.12 = (f32[1,1,16,128]{3,2,1,0:T(8,128)S(1)}, f32[1,1,16,128]{3,2,1,0:T(8,128)S(1)}, u32[]{:S(2)}, u32[]{:S(2)}) collective-permute-start(f32[1,1,16,128]{3,2,1,0:T(8,128)S(1)} %get-tuple-element.33), channel_id=1, source_target_pairs={{1,0},{3,2},{5,4},{7,6},{9,8},{11,10},{13,12},{15,14},{17,16},{19,... | collective-permute-start | bytes 24584 | tf_op jit(solution)/shard_map/ppermute | solution.py:28
  392.0 13.4 %collective-permute-start.13 = (f32[1,1,16,128]{3,2,1,0:T(8,128)S(1)}, f32[1,1,16,128]{3,2,1,0:T(8,128)S(1)}, u32[]{:S(2)}, u32[]{:S(2)}) collective-permute-start(f32[1,1,16,128]{3,2,1,0:T(8,128)S(1)} %get-tuple-element.34), channel_id=1, source_target_pairs={{0,1},{2,3},{4,5},{6,7},{8,9},{10,11},{12,13},{14,15},{16,17},{18,... | collective-permute-start | bytes 24584 | tf_op jit(solution)/shard_map/ppermute | solution.py:27
where the time goes:
time: 493 us; the launch traced here: 483 us
  blocking collectives  247 us (50%)
  waiting for transfers between devices  108 us (22%)
  starting transfers between devices  100 us (20%)
  other arithmetic  14 us (3%)
  matrix products  8.19 us (2%)
    all_to_all x1, blocking collectives, on_device(): lax.all_to_all(flat_source, TM, split_axis=1, concat_axis=0, tiled=True)  74 us
    psum x3, blocking collectives, by_axis(): value = lax.psum(value, axis)  73.4 us
    all_to_all x1, blocking collectives, on_device(): lax.all_to_all(flat_stiff, TM, split_axis=1, concat_axis=0, tiled=True)  37.1 us
    all_to_all x1, blocking collectives, on_device(): lax.all_to_all(sol_im.reshape(steps_here, cells), TM, split_axis=1, conca...  32 us
    all_to_all x1, blocking collectives, on_device(): lax.all_to_all(sol_re.reshape(steps_here, cells), TM, split_axis=1, conca...  30.8 us
    ppermute x7, starting transfers between devices, with_halo(): after = lax.ppermute(first, axis, down)  24.8 us
    all_to_all x1, waiting for transfers between devices, on_device(): lax.all_to_all(residual, TM, split_axis=0, concat_axis=1, tiled=True)  19 us
    all_to_all x1, waiting for transfers between devices, on_device(): lax.all_to_all(correction, TM, split_axis=0, concat_axis=1, tiled=True)  18.7 us
  transfers between devices with their start and end apart: 20, of which 12 were waited for; matrix products, arithmetic and copies ran while one was open for 2% of the time, Pallas kernels for 0%

commit v1 on v0

v1 whole, which is shorter than its diff:
```python
import math

import jax
import jax.numpy as jnp
import numpy as np
from jax import lax
from jax.experimental import pallas as pl
from jax.experimental.pallas import tpu as pltpu
from jax.sharding import Mesh
from jax.sharding import PartitionSpec as P

SWEEPS = 6
TM = ("tm_0", "tm_1")
CHIPS = "tm_0"
ROW = ("tm_1", "space")
GROUPS_TM = ("groups", "tm_0", "tm_1")

frac_order = 0.3
step_length = 0.01
gamma_factor = 0.9086387328532904


def history_weights(count):
    k = np.arange(count + 1, dtype=np.float64) ** (1.0 - frac_order)
    b = k[1:] - k[:-1]
    d = np.concatenate([[1.0], b[1:] - b[:-1]])
    return d / (step_length**frac_order * gamma_factor)


def tables(total, owners):
    half = total // 2
    here = half // owners
    n = np.arange(total)
    d = history_weights(total)
    lag = n[:, None] - n[None, :]
    hist = np.where(lag >= 0, d[np.maximum(lag, 0)], 0.0)
    first = np.where(n < half, d, 0.0)
    angle = 2.0 * math.pi * ((n[:, None] * n[None, :]) % total) / total
    lam = (first[None, :] * np.exp(-1j * angle)).sum(1)
    fwd = np.zeros((owners, 2, here, total))
    inv = np.zeros((total, owners, 2, here))
    lams = np.zeros((owners, 3, here))
    for q in range(owners):
        for j in range(here):
            k = q * here + j
            if k == 0:
                fwd[q, 0, j] = 1.0
                fwd[q, 1, j] = np.cos(angle[half])
                inv[:, q, 0, j] = 1.0 / total
                inv[:, q, 1, j] = np.cos(angle[half]) / total
                lams[q, :, j] = lam[0].real, lam[half].real, 0.0
            else:
                fwd[q, 0, j] = np.cos(angle[k])
                fwd[q, 1, j] = -np.sin(angle[k])
                inv[:, q, 0, j] = 2.0 * np.cos(angle[k]) / total
                inv[:, q, 1, j] = -2.0 * np.sin(angle[k]) / total
                lams[q, :, j] = lam[k].real, lam[k].real, lam[k].imag
    fwd = fwd.reshape(total, total)
    first_mat = np.zeros((2, total, total, 2))
    first_mat[0, :, :, 0] = hist
    first_mat[1, :, :, 0] = -fwd @ hist
    first_mat[1, :, :, 1] = fwd
    flat = inv.reshape(total, total)
    second_mat = np.zeros((total, 2, owners, 2, 2 * here))
    second_mat[:, 0, :, 0] = flat.reshape(total, owners, 2 * here)
    second_mat[:, 1, :, 0] = (hist @ flat).reshape(total, owners, 2 * here)
    second_mat[:, 1, :, 1] = flat.reshape(total, owners, 2 * here)
    f32 = np.float32
    return (
        first_mat.reshape(2 * total, 2 * total).astype(f32),
        second_mat.reshape(2 * total, 2 * total).astype(f32),
        lams.astype(f32),
    )


def neighbour_sum(padded):
    inner = padded[..., 1:-1, :, :]
    result = padded[..., 2:, :, :] + padded[..., :-2, :, :]
    along_y = jnp.pad(inner, [(0, 0)] * (inner.ndim - 2) + [(1, 1), (0, 0)])
    result = result + along_y[..., 2:, :] + along_y[..., :-2, :]
    along_x = jnp.pad(inner, [(0, 0)] * (inner.ndim - 1) + [(1, 1)])
    return result + along_x[..., 2:] + along_x[..., :-2]


def make_sweeps(own, depth, here, lanes, ny):
    cols = own + 2 * depth

    def kernel(*refs):
        pieces, kap, lam, out, start, gain, ping, pong = refs[:-7], *refs[-7:]
        flat = [(ref, c) for ref in pieces for c in range(ref.shape[0])]
        lane = lax.broadcasted_iota(jnp.int32, (here, lanes), 1)
        y = lane % ny
        y_first, y_last = y == 0, y == ny - 1
        z_first, z_last = lane < ny, lane >= lanes - ny
        lam_a, lam_b, lam_i = lam[0], lam[1], lam[2]
        for c in range(cols):
            ref, at = flat[c]
            for h in range(2):
                k = jnp.broadcast_to(kap[2 * c + h : 2 * c + h + 1, :], (here, lanes))
                diag_a = lam_a + 6.0 * k
                diag_b = lam_b + 6.0 * k
                over_a = 1.0 / (diag_a * diag_a + lam_i * lam_i)
                over_b = 1.0 / (diag_b * diag_b + lam_i * lam_i)
                g_a = diag_a * over_a
                g_b = diag_b * over_b
                g_i = -lam_i * over_a
                re = ref[at, h, 0:here, :]
                im = ref[at, h, here : 2 * here, :]
                s_re = g_a * re - g_i * im
                s_im = g_b * im + g_i * re
                start[c, h, 0] = s_re
                start[c, h, 1] = s_im
                ping[c, h, 0] = s_re
                ping[c, h, 1] = s_im
                gain[c, h, 0] = g_a * k
                gain[c, h, 1] = g_b * k
                gain[c, h, 2] = g_i * k

        def around(buf, c, part):
            a, b = buf[c, 0, part], buf[c, 1, part]
            down_a, down_b = pltpu.roll(a, ny, 1), pltpu.roll(b, ny, 1)
            up_a, up_b = pltpu.roll(a, lanes - ny, 1), pltpu.roll(b, lanes - ny, 1)

            def along_y(v):
                return jnp.where(y_first, 0.0, pltpu.roll(v, 1, 1)) + jnp.where(
                    y_last, 0.0, pltpu.roll(v, lanes - 1, 1)
                )

            na = jnp.where(z_first, 0.0, down_a) + jnp.where(z_last, up_b, up_a) + along_y(a)
            nb = jnp.where(z_first, down_a, down_b) + jnp.where(z_last, 0.0, up_b) + along_y(b)
            na = na + buf[c - 1, 0, part] + buf[c + 1, 0, part]
            nb = nb + buf[c - 1, 1, part] + buf[c + 1, 1, part]
            return na, nb

        now, then = ping, pong
        for sweep in range(1, SWEEPS):
            for c in range(sweep, cols - sweep):
                n_re, n_im = around(now, c, 0), around(now, c, 1)
                for h in range(2):
                    h_a, h_b, h_i = gain[c, h, 0], gain[c, h, 1], gain[c, h, 2]
                    then[c, h, 0] = start[c, h, 0] + (h_a * n_re[h] - h_i * n_im[h])
                    then[c, h, 1] = start[c, h, 1] + (h_b * n_im[h] + h_i * n_re[h])
            now, then = then, now
        for c in range(depth, depth + own):
            for part in range(2):
                n = around(now, c, part)
                for h in range(2):
                    sol = now[c, h, part]
                    k = jnp.broadcast_to(kap[2 * c + h : 2 * c + h + 1, :], (here, lanes))
                    row = 2 * (c - depth) + h
                    out[row, 0, here * part : here * (part + 1), :] = sol
                    out[row, 1, here * part : here * (part + 1), :] = k * (6.0 * sol - n[h])

    field = (cols, 2, 2, here, lanes)
    return pl.pallas_call(
        kernel,
        out_shape=jax.ShapeDtypeStruct((2 * own, 2, 2 * here, lanes), jnp.float32),
        in_specs=[pl.BlockSpec(memory_space=pltpu.VMEM)] * 7,
        out_specs=pl.BlockSpec(memory_space=pltpu.VMEM),
        scratch_shapes=[
            pltpu.VMEM(field, jnp.float32),
            pltpu.VMEM((cols, 2, 3, here, lanes), jnp.float32),
            pltpu.VMEM(field, jnp.float32),
            pltpu.VMEM(field, jnp.float32),
        ],
        name="sweeps",
    )


def on_device(iterate, source, diffusivity):
    _, nz, ny, nx = iterate.shape
    lanes = nz * ny
    chips, own = lax.axis_size(CHIPS), lax.axis_size("tm_1")
    cores = lax.axis_size("space")
    total = chips * own
    owners = own * cores
    here = total // 2 // owners
    depth = SWEEPS
    first_mat, second_mat, lams = tables(total, owners)
    core = lax.axis_index("space")
    chip = lax.axis_index(CHIPS)

    u, f = iterate[0], source[0]
    kap_cols = jnp.pad(diffusivity.reshape(lanes, nx).T, ((depth, depth), (0, 0)))
    kap_cols = lax.dynamic_slice_in_dim(kap_cols, chip * own, own + 2 * depth, axis=0)
    edge = jnp.where(core == 0, u[nz - 1], u[0])
    swap = [(0, 1), (1, 0)]
    got = lax.ppermute(jnp.concatenate([edge, kap_cols], axis=0), "space", swap)
    got_edge, kap_other = got[:ny], got[ny:]
    zero = jnp.zeros_like(got_edge)
    before = jnp.where(core == 0, zero, got_edge)
    after = jnp.where(core == 0, got_edge, zero)
    padded = jnp.concatenate([before[None], u, after[None]], axis=0)
    s = f - diffusivity * (6.0 * u - neighbour_sum(padded))
    kap = jnp.where(
        core == 0,
        jnp.stack([kap_cols, kap_other], axis=1),
        jnp.stack([kap_other, kap_cols], axis=1),
    ).reshape(-1, lanes)
    lam = lax.dynamic_index_in_dim(
        jnp.asarray(lams), lax.axis_index(ROW), axis=0, keepdims=False
    )
    lam = jnp.broadcast_to(lam[:, :, None], (3, here, lanes))

    send = jnp.stack([u.reshape(lanes, nx).T, s.reshape(lanes, nx).T], axis=1)
    cells = lax.all_to_all(send, TM, split_axis=0, concat_axis=0, tiled=True)
    high = lax.Precision.HIGHEST
    first = jnp.dot(first_mat, cells.reshape(2 * total, lanes), precision=high)
    hist_u = first[:total]
    spec = first[total:].reshape(owners, 2 * here, lanes)
    residual = cells[:, 1] - hist_u

    spec = lax.all_to_all(spec, ROW, split_axis=0, concat_axis=0, tiled=True)
    spec = spec.reshape(own, cores, 2 * here, lanes)
    rest = depth - own

    def shifted(value, offset):
        pairs = [(i, i + offset) for i in range(chips) if 0 <= i + offset < chips]
        return lax.ppermute(value, CHIPS, pairs)

    left_near = shifted(spec, 1)
    right_near = shifted(spec, -1)
    left_far = shifted(spec[own - rest :], 2)
    right_far = shifted(spec[:rest], -2)
    back = make_sweeps(own, depth, here, lanes, ny)(
        left_far, left_near, spec, right_near, right_far, kap, lam
    )
    back = lax.all_to_all(back, ROW, split_axis=0, concat_axis=0, tiled=True)
    second = jnp.dot(second_mat, back.reshape(2 * total, lanes), precision=high)
    second = second.reshape(total, 2, lanes)
    image = second[:, 1]
    inner_ri = jnp.sum(residual * image)
    inner_ii = jnp.sum(image * image)
    lane = jnp.arange(lanes, dtype=jnp.int32)
    sums = jnp.where(lane == 0, inner_ri, jnp.where(lane == 1, inner_ii, 0.0))
    sums = jnp.broadcast_to(sums[None, None, :], (total, 1, lanes))
    send = jnp.concatenate([second, hist_u[:, None], sums], axis=1)
    times = lax.all_to_all(send, TM, split_axis=0, concat_axis=0, tiled=True)
    sums = jnp.sum(times[:, 3, :], axis=0, keepdims=True)
    sums = sums + lax.ppermute(sums, "space", swap)
    step = sums[0, 0] / sums[0, 1]

    def slab(index):
        return times[:, index].T.reshape(nz, ny, nx)

    new_iterate = u + step * slab(0)
    new_residual = s - slab(2) - step * slab(1)
    return (new_iterate[None], new_residual[None])


def solution(mesh):
    split = Mesh(
        mesh.devices.reshape(mesh.shape["groups"], 32, 4, mesh.shape["space"]),
        ("groups", "tm_0", "tm_1", "space"),
    )
    placed = (
        P(GROUPS_TM, "space", None, None),
        P(GROUPS_TM, "space", None, None),
        P(("groups", "space"), None, None),
    )
    return jax.shard_map(
        on_device,
        mesh=split,
        in_specs=placed,
        out_specs=(P(GROUPS_TM, "space", None, None), P(GROUPS_TM, "space", None, None)),
        check_vma=False,
    )
```

time: 493 us -> 188 us (0.38)
  the two profiles are of different devices: /device:TPU:33 before, /device:TPU:40 now
where the time goes in v1:
time: 188 us; the launch traced here: 185 us
  starting transfers between devices  76.1 us (40%)
  blocking collectives  48.8 us (26%)
  waiting for transfers between devices  44.9 us (24%)
  local copies, waits for them, and re-layouts  6.25 us (3%)
  other arithmetic  3.81 us (2%)
  Pallas kernels  2.62 us (1%)
  between operations  2.23 us (1%)
    all_to_all x1, starting transfers between devices, on_device(): cells = lax.all_to_all(send, TM, split_axis=0, concat_axis=0, tiled=True)  53.2 us
    all_to_all x1, blocking collectives, on_device(): times = lax.all_to_all(send, TM, split_axis=0, concat_axis=0, tiled=True)  48.8 us
    all_to_all x1, waiting for transfers between devices, on_device(): cells = lax.all_to_all(send, TM, split_axis=0, concat_axis=0, tiled=True)  26.9 us
    ppermute x4, starting transfers between devices, shifted(): return lax.ppermute(value, CHIPS, pairs)  9.83 us
    all_to_all x1, waiting for transfers between devices, on_device(): back = lax.all_to_all(back, ROW, split_axis=0, concat_axis=0, tiled=True)  5.81 us
    all_to_all x1, starting transfers between devices, on_device(): spec = lax.all_to_all(spec, ROW, split_axis=0, concat_axis=0, tiled=True)  5.33 us
    ppermute x4, waiting for transfers between devices, shifted(): return lax.ppermute(value, CHIPS, pairs)  4.96 us
    all_to_all x1, waiting for transfers between devices, on_device(): spec = lax.all_to_all(spec, ROW, split_axis=0, concat_axis=0, tiled=True)  4.94 us
  transfers between devices with their start and end apart: 9, of which 6 were waited for; matrix products, arithmetic and copies ran while one was open for 1% of the time, Pallas kernels for 0%

profile of v1, /device:TPU:40, one launch (start us, length us, event | category | flops | bytes accessed | tf_op | source)
XLA Modules:
  0.0 185.5 jit_solution(15234638829824214438)
XLA Ops:
  0.6 1.0 pad_dynamic-slice_fusion
  1.6 0.1 copy.37
  1.7 0.8 copy-done
  2.5 2.1 %collective-permute-start = (f32[32,128]{1,0:T(8,128)S(1)}, f32[32,128]{1,0:T(8,128)S(1)}, u32[]{:S(2)}, u32[]{:S(2)}) collective-permute-start(f32[32,128]{1,0:T(8,128)S(1)} %pad_maximum_fusion.4), channel_id=1, source_target_pairs={{0,1},{1,0},{2,3},{3,2},{4,5},{5,4},{6,7},{7,6},{8,9},{9,8},{10,11... | collective-permute-start | bytes 49160 | tf_op jit(solution)/shard_map/ppermute | solution.py:188
  4.6 1.1 collective-permute-done
  5.7 0.1 fusion.6
  5.8 0.0 copy-start.4
  5.9 0.8 copy.38
  6.6 53.2 %all-to-all-start = ((f32[128,2,128]{2,1,0:T(2,128)}), f32[128,2,128]{2,1,0:T(2,128)S(1)}, u32[]{:S(2)}, u32[]{:S(2)}) async-start(f32[128,2,128]{2,1,0:T(2,128)} %copy.38), calls=%async_computation | async-start | bytes 262144 | tf_op jit(solution)/shard_map/all_to_all | solution.py:206
  59.8 26.9 %all-to-all-done = f32[128,2,128]{2,1,0:T(2,128)S(1)} async-done(((f32[128,2,128]{2,1,0:T(2,128)}), f32[128,2,128]{2,1,0:T(2,128)S(1)}, u32[]{:S(2)}, u32[]{:S(2)}) %all-to-all-start) | async-done | bytes 131104 | tf_op jit(solution)/shard_map/all_to_all | solution.py:206
  86.8 0.4 fusion.11
  87.1 0.6 slice.101
  87.8 5.3 %all-to-all-start.1 = ((f32[8,16,128]{2,1,0:T(8,128)}), f32[8,16,128]{2,1,0:T(8,128)S(1)}, u32[]{:S(2)}, u32[]{:S(2)}) async-start(f32[8,16,128]{2,1,0:T(8,128)} %bitcast.14), calls=%async_computation.1 | async-start | bytes 131072 | tf_op jit(solution)/shard_map/all_to_all | solution.py:213
  93.1 0.7 dynamic-slice_bitcast_fusion
  93.8 4.9 %all-to-all-done.1 = f32[8,16,128]{2,1,0:T(8,128)S(1)} async-done(((f32[8,16,128]{2,1,0:T(8,128)}), f32[8,16,128]{2,1,0:T(8,128)S(1)}, u32[]{:S(2)}, u32[]{:S(2)}) %all-to-all-start.1) | async-done | bytes 65568 | tf_op jit(solution)/shard_map/all_to_all | solution.py:213
  98.7 1.3 collective-permute-start.3
  100.0 4.6 %collective-permute-start.2 = (f32[4,2,16,128]{3,2,1,0:T(8,128)S(1)}, f32[4,2,16,128]{3,2,1,0:T(8,128)S(1)}, u32[]{:S(2)}, u32[]{:S(2)}) collective-permute-start(f32[4,2,16,128]{3,2,1,0:T(8,128)S(1)} %bitcast.71), channel_id=1, source_target_pairs={{0,8},{8,16},{16,24},{24,32},{32,40},{40,48},{48,56},{56,64},{64,7... | collective-permute-start | bytes 196616 | tf_op jit(solution)/shard_map/ppermute | solution.py:219
  104.7 0.0 copy-done.1
  104.7 2.6 %collective-permute-start.1 = (f32[2,2,16,128]{3,2,1,0:T(8,128)S(1)}, f32[2,2,16,128]{3,2,1,0:T(8,128)S(1)}, u32[]{:S(2)}, u32[]{:S(2)}) collective-permute-start(f32[2,2,16,128]{3,2,1,0:T(8,128)S(1)} %bitcast.88), channel_id=1, source_target_pairs={{0,16},{8,24},{16,32},{24,40},{32,48},{40,56},{48,64},{56,72},{64,... | collective-permute-start | bytes 98312 | tf_op jit(solution)/shard_map/ppermute | solution.py:219
  107.3 1.3 collective-permute-start.4
  108.6 0.6 copy.40
  109.3 0.0 collective-permute-done.1.refs_0_
  109.3 4.9 %collective-permute-done.4.refs_4_ = f32[2,2,16,128]{3,2,1,0:T(8,128)S(1)} collective-permute-done((f32[2,2,16,128]{3,2,1,0:T(8,128)S(1)}, f32[2,2,16,128]{3,2,1,0:T(8,128)S(1)}, u32[]{:S(2)}, u32[]{:S(2)}) %collective-permute-start.4) | collective-permute-done | bytes 32800 | tf_op jit(solution)/shard_map/ppermute | solution.py:219
  114.2 0.0 collective-permute-done.3.refs_3_
  114.2 0.0 collective-permute-done.2.refs_1_
  114.2 0.0 copy-start.7
  114.2 0.7 broadcast_in_dim.49.refs_6_
  114.9 0.0 copy-done.6
  114.9 2.6 %sweeps.1 = f32[8,2,16,128]{3,2,1,0:T(8,128)} custom-call(f32[2,2,16,128]{3,2,1,0:T(8,128)} %copy-done.8, f32[4,2,16,128]{3,2,1,0:T(8,128)} %copy-done.7, f32[4,2,16,128]{3,2,1,0:T(8,128)} %bitcast.72, f32[4,2,16,128]{3,2,1,0:T(8,128)} %copy-done.6, f32[2,2,16,128]{3,2,1,0:T(8,128)} %copy-done.9, f32[32,128]{1,0:T(8,128)} %bitcast.86, ...), custom_call_target="tpu_custom_call" | custom-call | tf_op jit(solution)/shard_map/sweeps/pallas_call | solution.py:225
  117.5 3.7 %all-to-all-start.2 = ((f32[8,2,16,128]{3,2,1,0:T(8,128)}), f32[8,2,16,128]{3,2,1,0:T(8,128)S(1)}, u32[]{:S(2)}, u32[]{:S(2)}) async-start(f32[8,2,16,128]{3,2,1,0:T(8,128)} %sweeps.1), calls=%async_computation.2 | async-start | bytes 262144 | tf_op jit(solution)/shard_map/all_to_all | solution.py:228
  121.2 0.1 slice.106
  121.3 5.8 %all-to-all-done.2 = f32[8,2,16,128]{3,2,1,0:T(8,128)S(1)} async-done(((f32[8,2,16,128]{3,2,1,0:T(8,128)}), f32[8,2,16,128]{3,2,1,0:T(8,128)S(1)}, u32[]{:S(2)}, u32[]{:S(2)}) %all-to-all-start.2) | async-done | bytes 131104 | tf_op jit(solution)/shard_map/all_to_all | solution.py:228
  127.1 0.4 fusion.12
  127.5 0.1 slice.107
  127.6 0.6 multiply_reduce_fusion.1
  128.2 1.3 compare_select_fusion.1
  129.6 0.2 pad_maximum_fusion
  129.7 48.8 %all_to_all.20 = f32[128,4,128]{2,1,0:T(4,128)S(1)} all-to-all(f32[128,4,128]{2,1,0:T(4,128)S(1)} %pad_maximum_fusion), channel_id=1, replica_groups=mesh['groups'=2,'tm_0'=32,'tm_1'=4,'space'=2] {'tm_0','tm_1'}, dimensions={0} | all-to-all | bytes 524288 | tf_op jit(solution)/shard_map/all_to_all | solution.py:238
  178.6 0.2 slice_reduce_fusion
  178.7 1.9 %collective-permute-start.5 = (f32[1,128]{1,0:T(1,128)S(1)}, f32[1,128]{1,0:T(1,128)S(1)}, u32[]{:S(2)}, u32[]{:S(2)}) collective-permute-start(f32[1,128]{1,0:T(1,128)S(1)} %bitcast.89), channel_id=1, source_target_pairs={{0,1},{1,0},{2,3},{3,2},{4,5},{5,4},{6,7},{7,6},{8,9},{9,8},{10,11... | collective-permute-start | bytes 1544 | tf_op jit(solution)/shard_map/ppermute | solution.py:240
  180.7 1.1 collective-permute-done.5
  181.8 0.6 fusion.10
  183.7 0.1 fusion.8
  183.9 0.1 copy.45
  184.0 0.1 copy.46
  184.1 0.1 copy.44
  184.2 0.6 add.47
  184.8 0.6 subtract_bitcast_fusion
  (23 shorter events, 0.1 us)
Async XLA Ops:
  0.6 5.1 %copy-start.5 = (f32[1,8,16,128]{3,2,1,0:T(8,128)S(1)}, f32[1,8,16,128]{3,2,1,0:T(8,128)}, u32[]{:S(2)}) copy-start(f32[1,8,16,128]{3,2,1,0:T(8,128)} %param.7) | copy-start | bytes 196612
  1.6 0.8 copy-start
  2.5 3.3 %copy-start.2 = (f32[8,16,128]{2,1,0:T(8,128)S(1)}, f32[8,16,128]{2,1,0:T(8,128)}, u32[]{:S(2)}) copy-start(f32[8,16,128]{2,1,0:T(8,128)} %param.8) | copy-start | bytes 196612
  2.5 3.2 %collective-permute-start = (f32[32,128]{1,0:T(8,128)S(1)}, f32[32,128]{1,0:T(8,128)S(1)}, u32[]{:S(2)}, u32[]{:S(2)}) collective-permute-start(f32[32,128]{1,0:T(8,128)S(1)} %pad_maximum_fusion.4), channel_id=1, source_target_pairs={{0,1},{1,0},{2,3},{3,2},{4,5},{5,4},{6,7},{7,6},{8,9},{9,8},{10,11... | collective-permute-start | bytes 49160 | tf_op jit(solution)/shard_map/ppermute | solution.py:188
  5.8 80.9 %copy-start.4 = (f32[256,256]{1,0:T(8,128)S(1)}, f32[256,256]{1,0:T(8,128)}, u32[]{:S(2)}) copy-start(f32[256,256]{1,0:T(8,128)} %constant.42.clone) | copy-start | bytes 786436
  6.6 80.1 %all-to-all-start = ((f32[128,2,128]{2,1,0:T(2,128)}), f32[128,2,128]{2,1,0:T(2,128)S(1)}, u32[]{:S(2)}, u32[]{:S(2)}) async-start(f32[128,2,128]{2,1,0:T(2,128)} %copy.38), calls=%async_computation | async-start | bytes 262144 | tf_op jit(solution)/shard_map/all_to_all | solution.py:206
  87.8 11.0 %all-to-all-start.1 = ((f32[8,16,128]{2,1,0:T(8,128)}), f32[8,16,128]{2,1,0:T(8,128)S(1)}, u32[]{:S(2)}, u32[]{:S(2)}) async-start(f32[8,16,128]{2,1,0:T(8,128)} %bitcast.14), calls=%async_computation.1 | async-start | bytes 131072 | tf_op jit(solution)/shard_map/all_to_all | solution.py:213
  98.7 5.9 %copy-start.1 = (f32[8,16,128]{2,1,0:T(8,128)}, f32[8,16,128]{2,1,0:T(8,128)S(1)}, u32[]{:S(2)}) copy-start(f32[8,16,128]{2,1,0:T(8,128)S(1)} %all-to-all-done.1) | copy-start | bytes 196612
  98.7 15.5 %collective-permute-start.3 = (f32[4,2,16,128]{3,2,1,0:T(8,128)S(1)}, f32[4,2,16,128]{3,2,1,0:T(8,128)S(1)}, u32[]{:S(2)}, u32[]{:S(2)}) collective-permute-start(f32[4,2,16,128]{3,2,1,0:T(8,128)S(1)} %bitcast.70), channel_id=1, source_target_pairs={{8,0},{16,8},{24,16},{32,24},{40,32},{48,40},{56,48},{64,56},{72,6... | collective-permute-start | bytes 196616 | tf_op jit(solution)/shard_map/ppermute | solution.py:219
  100.0 14.2 %collective-permute-start.2 = (f32[4,2,16,128]{3,2,1,0:T(8,128)S(1)}, f32[4,2,16,128]{3,2,1,0:T(8,128)S(1)}, u32[]{:S(2)}, u32[]{:S(2)}) collective-permute-start(f32[4,2,16,128]{3,2,1,0:T(8,128)S(1)} %bitcast.71), channel_id=1, source_target_pairs={{0,8},{8,16},{16,24},{24,32},{32,40},{40,48},{48,56},{56,64},{64,7... | collective-permute-start | bytes 196616 | tf_op jit(solution)/shard_map/ppermute | solution.py:219
  104.7 4.6 %collective-permute-start.1 = (f32[2,2,16,128]{3,2,1,0:T(8,128)S(1)}, f32[2,2,16,128]{3,2,1,0:T(8,128)S(1)}, u32[]{:S(2)}, u32[]{:S(2)}) collective-permute-start(f32[2,2,16,128]{3,2,1,0:T(8,128)S(1)} %bitcast.88), channel_id=1, source_target_pairs={{0,16},{8,24},{16,32},{24,40},{32,48},{40,56},{48,64},{56,72},{64,... | collective-permute-start | bytes 98312 | tf_op jit(solution)/shard_map/ppermute | solution.py:219
  107.3 6.9 %collective-permute-start.4 = (f32[2,2,16,128]{3,2,1,0:T(8,128)S(1)}, f32[2,2,16,128]{3,2,1,0:T(8,128)S(1)}, u32[]{:S(2)}, u32[]{:S(2)}) collective-permute-start(f32[2,2,16,128]{3,2,1,0:T(8,128)S(1)} %bitcast.87), channel_id=1, source_target_pairs={{16,0},{24,8},{32,16},{40,24},{48,32},{56,40},{64,48},{72,56},{80,... | collective-permute-start | bytes 98312 | tf_op jit(solution)/shard_map/ppermute | solution.py:219
  109.3 5.6 %copy-start.8 = (f32[2,2,16,128]{3,2,1,0:T(8,128)}, f32[2,2,16,128]{3,2,1,0:T(8,128)S(1)}, u32[]{:S(2)}) copy-start(f32[2,2,16,128]{3,2,1,0:T(8,128)S(1)} %collective-permute-done.1.refs_0_) | copy-start | bytes 98308
  114.2 0.7 copy-start.9
  114.2 0.7 copy-start.6
  114.2 0.7 copy-start.7
  117.5 9.6 %copy-start.3 = (f32[256,256]{1,0:T(8,128)S(1)}, f32[256,256]{1,0:T(8,128)}, u32[]{:S(2)}) copy-start(f32[256,256]{1,0:T(8,128)} %constant.43.clone) | copy-start | bytes 786436
  117.5 9.6 %all-to-all-start.2 = ((f32[8,2,16,128]{3,2,1,0:T(8,128)}), f32[8,2,16,128]{3,2,1,0:T(8,128)S(1)}, u32[]{:S(2)}, u32[]{:S(2)}) async-start(f32[8,2,16,128]{3,2,1,0:T(8,128)} %sweeps.1), calls=%async_computation.2 | async-start | bytes 262144 | tf_op jit(solution)/shard_map/all_to_all | solution.py:228
  178.7 3.1 %collective-permute-start.5 = (f32[1,128]{1,0:T(1,128)S(1)}, f32[1,128]{1,0:T(1,128)S(1)}, u32[]{:S(2)}, u32[]{:S(2)}) collective-permute-start(f32[1,128]{1,0:T(1,128)S(1)} %bitcast.89), channel_id=1, source_target_pairs={{0,1},{1,0},{2,3},{3,2},{4,5},{5,4},{6,7},{7,6},{8,9},{9,8},{10,11... | collective-permute-start | bytes 1544 | tf_op jit(solution)/shard_map/ppermute | solution.py:240

commit v2 on v1

v2 whole, which is shorter than its diff:
```python
import math

import jax
import jax.numpy as jnp
import numpy as np
from jax import lax
from jax.experimental import pallas as pl
from jax.experimental.pallas import tpu as pltpu
from jax.sharding import Mesh
from jax.sharding import PartitionSpec as P

SWEEPS = 6
TM = ("blocks", "pair", "tm_1")
ROW = ("pair", "tm_1", "space")
GROUPS_TM = ("groups", "blocks", "pair", "tm_1")
HIGH = lax.Precision.HIGHEST

frac_order = 0.3
step_length = 0.01
gamma_factor = 0.9086387328532904


def history_weights(count):
    k = np.arange(count + 1, dtype=np.float64) ** (1.0 - frac_order)
    b = k[1:] - k[:-1]
    d = np.concatenate([[1.0], b[1:] - b[:-1]])
    return d / (step_length**frac_order * gamma_factor)


def tables(total, owners):
    half = total // 2
    here = half // owners
    n = np.arange(total)
    d = history_weights(total)
    lag = n[:, None] - n[None, :]
    hist = np.where(lag >= 0, d[np.maximum(lag, 0)], 0.0)
    first = np.where(n < half, d, 0.0)
    angle = 2.0 * math.pi * ((n[:, None] * n[None, :]) % total) / total
    lam = (first[None, :] * np.exp(-1j * angle)).sum(1)
    fwd = np.zeros((owners, 2, here, total))
    inv = np.zeros((total, owners, 2, here))
    lams = np.zeros((owners, 2, 2, here))
    for q in range(owners):
        for j in range(here):
            k = q * here + j
            if k == 0:
                fwd[q, 0, j] = 1.0
                fwd[q, 1, j] = np.cos(angle[half])
                inv[:, q, 0, j] = 1.0 / total
                inv[:, q, 1, j] = np.cos(angle[half]) / total
                lams[q, 0, :, j] = lam[0].real, lam[half].real
            else:
                fwd[q, 0, j] = np.cos(angle[k])
                fwd[q, 1, j] = -np.sin(angle[k])
                inv[:, q, 0, j] = 2.0 * np.cos(angle[k]) / total
                inv[:, q, 1, j] = -2.0 * np.sin(angle[k]) / total
                lams[q, 0, :, j] = lam[k].real
                lams[q, 1, :, j] = lam[k].imag
    fwd = fwd.reshape(total, total)
    first_mat = np.zeros((2, total, total, 2))
    first_mat[0, :, :, 0] = hist
    first_mat[1, :, :, 0] = -fwd @ hist
    first_mat[1, :, :, 1] = fwd
    flat = inv.reshape(total, total)
    second_mat = np.zeros((2, total, owners, 2, 2 * here))
    second_mat[0, :, :, 0] = flat.reshape(total, owners, 2 * here)
    second_mat[1, :, :, 0] = (hist @ flat).reshape(total, owners, 2 * here)
    second_mat[1, :, :, 1] = flat.reshape(total, owners, 2 * here)
    f32 = np.float32
    return (
        first_mat.reshape(2 * total, 2 * total).astype(f32),
        second_mat.reshape(2 * total, 2 * total).astype(f32),
        lams.reshape(owners, 2, 2 * here).astype(f32),
    )


def local_call(kernel, name, outs, inputs, scratch=()):
    vmem = pl.BlockSpec(memory_space=pltpu.VMEM)
    return pl.pallas_call(
        kernel,
        out_shape=[jax.ShapeDtypeStruct(shape, jnp.float32) for shape in outs],
        in_specs=[vmem] * inputs,
        out_specs=[vmem] * len(outs),
        scratch_shapes=list(scratch),
        name=name,
    )


def iota(shape, dim):
    return lax.broadcasted_iota(jnp.int32, shape, dim)


def make_entry(nz, ny, nx):
    lanes = nz * ny

    def kernel(u, f, kappa, before, after, s, out):
        row, lane = iota((ny, nx), 0), iota((ny, nx), 1)
        for z in range(nz):
            v = u[z]
            near = (before[...] if z == 0 else u[z - 1]) + (after[...] if z == nz - 1 else u[z + 1])
            near = near + jnp.where(row == 0, 0.0, pltpu.roll(v, 1, 0))
            near = near + jnp.where(row == ny - 1, 0.0, pltpu.roll(v, ny - 1, 0))
            near = near + jnp.where(lane == 0, 0.0, pltpu.roll(v, 1, 1))
            near = near + jnp.where(lane == nx - 1, 0.0, pltpu.roll(v, nx - 1, 1))
            s[z] = f[z] - kappa[z] * (6.0 * v - near)
        out[pl.ds(0, nx, stride=2), :] = u[...].reshape(lanes, nx).T
        out[pl.ds(1, nx, stride=2), :] = s[...].reshape(lanes, nx).T

    return local_call(kernel, "entry", [(nz, ny, nx), (2 * nx, lanes)], 5)


def make_forward(total, lanes):
    def kernel(mat, cells, hist, spec):
        both = jnp.dot(mat[...], cells[...], precision=HIGH, preferred_element_type=jnp.float32)
        hist[...] = both[:total]
        spec[...] = both[total:]

    return local_call(kernel, "forward", [(total, lanes)] * 2, 2)


def make_backward(total, lanes):
    def kernel(mat, back, hist, cells, out):
        both = jnp.dot(mat[...], back[...], precision=HIGH, preferred_element_type=jnp.float32)
        image = both[total:]
        residual = cells[pl.ds(1, total, stride=2), :] - hist[...]
        ri = jnp.sum(residual * image, axis=0, keepdims=True)
        ii = jnp.sum(image * image, axis=0, keepdims=True)
        low = iota((1, lanes), 1) < lanes // 2
        sums = jnp.where(low, ri + pltpu.roll(ri, lanes // 2, 1), ii + pltpu.roll(ii, lanes // 2, 1))
        out[pl.ds(0, total, stride=4), :] = both[:total]
        out[pl.ds(1, total, stride=4), :] = image
        out[pl.ds(2, total, stride=4), :] = hist[...]
        out[pl.ds(3, total, stride=4), :] = jnp.broadcast_to(sums, (total, lanes))

    return local_call(kernel, "backward", [(4 * total, lanes)], 4)


def make_exit(nz, ny, nx):
    lanes = nz * ny

    def kernel(times, sums, u, s, new_u, new_r):
        low = iota((1, lanes), 1) < lanes // 2
        ri = jnp.sum(jnp.where(low, sums[...], 0.0), axis=1, keepdims=True)
        ii = jnp.sum(jnp.where(low, 0.0, sums[...]), axis=1, keepdims=True)
        step = (ri / ii).reshape(1, 1, 1)

        def slab(k):
            return times[pl.ds(k, nx, stride=4), :].T.reshape(nz, ny, nx)

        new_u[...] = u[...] + step * slab(0)
        new_r[...] = s[...] - slab(2) - step * slab(1)

    return local_call(kernel, "exit", [(nz, ny, nx)] * 2, 4)


def make_sweeps(own, depth, rows, lanes, ny):
    cols = own + 2 * depth
    shape = (rows, lanes)

    def kernel(left, mid, right, kap, lam, out, start, same, cross, ping, pong):
        flat = [(ref, c) for ref in (left, mid, right) for c in range(ref.shape[0])]
        lane = iota(shape, 1)
        y = lane % ny
        y_first, y_last = y == 0, y == ny - 1
        z_first, z_last = lane < ny, lane >= lanes - ny
        sign = jnp.where(iota(shape, 0) < rows // 2, -1.0, 1.0)
        lam_r, lam_i = lam[0], lam[1]
        lam_ii = lam_i * lam_i

        def swap(v):
            return pltpu.roll(v, rows // 2, 0)

        for c in range(cols):
            ref, at = flat[c]
            for h in range(2):
                k = jnp.broadcast_to(kap[2 * c + h : 2 * c + h + 1, :], shape)
                diag = lam_r + 6.0 * k
                over = 1.0 / (diag * diag + lam_ii)
                g = diag * over
                g_cross = sign * (-lam_i * over)
                spec = ref[at, h]
                first = g * spec + g_cross * swap(spec)
                start[c, h] = first
                ping[c, h] = first
                same[c, h] = g * k
                cross[c, h] = g_cross * k

        def around(buf, c):
            a, b = buf[c, 0], buf[c, 1]
            down_a, down_b = pltpu.roll(a, ny, 1), pltpu.roll(b, ny, 1)
            up_a, up_b = pltpu.roll(a, lanes - ny, 1), pltpu.roll(b, lanes - ny, 1)

            def along_y(v):
                return jnp.where(y_first, 0.0, pltpu.roll(v, 1, 1)) + jnp.where(
                    y_last, 0.0, pltpu.roll(v, lanes - 1, 1)
                )

            na = jnp.where(z_first, 0.0, down_a) + jnp.where(z_last, up_b, up_a) + along_y(a)
            nb = jnp.where(z_first, down_a, down_b) + jnp.where(z_last, 0.0, up_b) + along_y(b)
            return (
                na + buf[c - 1, 0] + buf[c + 1, 0],
                nb + buf[c - 1, 1] + buf[c + 1, 1],
            )

        now, then = ping, pong
        for sweep in range(1, SWEEPS):
            for c in range(sweep, cols - sweep):
                near = around(now, c)
                for h in range(2):
                    n = near[h]
                    then[c, h] = start[c, h] + (same[c, h] * n + cross[c, h] * swap(n))
            now, then = then, now
        for c in range(depth, depth + own):
            near = around(now, c)
            for h in range(2):
                sol = now[c, h]
                k = jnp.broadcast_to(kap[2 * c + h : 2 * c + h + 1, :], shape)
                row = 2 * (c - depth) + h
                out[row, 0] = sol
                out[row, 1] = k * (6.0 * sol - near[h])

    field = pltpu.VMEM((cols, 2, rows, lanes), jnp.float32)
    return local_call(kernel, "sweeps", [(2 * own, 2, rows, lanes)], 5, [field] * 5)


def on_device(iterate, source, diffusivity):
    _, nz, ny, nx = iterate.shape
    lanes = nz * ny
    blocks, pair = lax.axis_size("blocks"), lax.axis_size("pair")
    own = pair * lax.axis_size("tm_1")
    cores = lax.axis_size("space")
    total = blocks * own
    owners = own * cores
    rows = total // owners
    depth = SWEEPS
    first_mat, second_mat, lams = tables(total, owners)
    core = lax.axis_index("space")
    block = lax.axis_index("blocks")
    swap = [(0, 1), (1, 0)]

    u, f = iterate[0], source[0]
    got = lax.ppermute(jnp.where(core == 0, u[nz - 1], u[0]), "space", swap)
    before = jnp.where(core == 0, 0.0, got)
    after = jnp.where(core == 0, got, 0.0)
    s, send = make_entry(nz, ny, nx)(u, f, diffusivity, before, after)
    cells = lax.all_to_all(
        send.reshape(total, 2, lanes), TM, split_axis=0, concat_axis=0, tiled=True
    ).reshape(2 * total, lanes)

    kap = jnp.pad(diffusivity.reshape(lanes, nx).T, ((depth, depth), (0, 0)))
    kap = lax.dynamic_slice_in_dim(kap, block * own, own + 2 * depth, axis=0)
    kap_other = lax.ppermute(kap, "space", swap)
    kap = jnp.where(
        core == 0, jnp.stack([kap, kap_other], axis=1), jnp.stack([kap_other, kap], axis=1)
    ).reshape(-1, lanes)
    lam = lax.dynamic_index_in_dim(jnp.asarray(lams), lax.axis_index(ROW), axis=0, keepdims=False)
    lam = jnp.broadcast_to(lam[:, :, None], (2, rows, lanes))

    hist_u, spec = make_forward(total, lanes)(first_mat, cells)
    spec = lax.all_to_all(
        spec.reshape(owners, rows, lanes), ROW, split_axis=0, concat_axis=0, tiled=True
    ).reshape(own, cores, rows, lanes)

    def shifted(value, offset):
        pairs = [(i, i + offset) for i in range(blocks) if 0 <= i + offset < blocks]
        return lax.ppermute(value, "blocks", pairs)

    left = shifted(spec[own - depth :], 1)
    right = shifted(spec[:depth], -1)
    (back,) = make_sweeps(own, depth, rows, lanes, ny)(left, spec, right, kap, lam)
    back = lax.all_to_all(back, ROW, split_axis=0, concat_axis=0, tiled=True)
    (send,) = make_backward(total, lanes)(second_mat, back.reshape(2 * total, lanes), hist_u, cells)
    times = lax.all_to_all(
        send.reshape(total, 4, lanes), TM, split_axis=0, concat_axis=0, tiled=True
    )
    sums = jnp.sum(times[:, 3, :], axis=0, keepdims=True)
    sums = sums + lax.ppermute(sums, "space", swap)
    new_iterate, new_residual = make_exit(nz, ny, nx)(
        times.reshape(4 * total, lanes), sums, u, s
    )
    return (new_iterate[None], new_residual[None])


def solution(mesh):
    split = Mesh(
        mesh.devices.reshape(mesh.shape["groups"], 16, 2, 4, mesh.shape["space"]),
        ("groups", "blocks", "pair", "tm_1", "space"),
    )
    placed = (
        P(GROUPS_TM, "space", None, None),
        P(GROUPS_TM, "space", None, None),
        P(("groups", "space"), None, None),
    )
    return jax.shard_map(
        on_device,
        mesh=split,
        in_specs=placed,
        out_specs=(P(GROUPS_TM, "space", None, None), P(GROUPS_TM, "space", None, None)),
        check_vma=False,
    )
```

time: 188 us -> 185 us (0.984)
  blocking collectives: 48.8 us -> 141 us
  starting transfers between devices: 76.1 us -> 15.9 us
  waiting for transfers between devices: 44.9 us -> 10.7 us
  Pallas kernels: 2.62 us -> 9.99 us
  local copies, waits for them, and re-layouts: 6.25 us -> 2.11 us
    all_to_all x1 -> x3, blocking collectives: 48.8 us -> 141 us  [the longest x1 80.2 us: on_device(): lax.all_to_all(send.reshape(total, 2, lanes), TM, split_axis=0, concat_ax...]
    all_to_all x3 -> x1, starting transfers between devices: 62.2 us -> 5.77 us  [on_device(): lax.all_to_all(spec.reshape(owners, rows, lanes), ROW, split_axis=0, conc...]
    all_to_all x3 -> x1, waiting for transfers between devices: 37.7 us -> 2.71 us  [on_device(): lax.all_to_all(spec.reshape(owners, rows, lanes), ROW, split_axis=0, conc...]
    pallas_call x1 -> x5, Pallas kernels: 2.62 us -> 9.99 us  [the longest x1 2.27 us: on_device(): make_sweeps(own, depth, rows, lanes, ny)(left, spec, right, kap, lam)]
    ppermute x5 -> x4, starting transfers between devices: 11.9 us -> 8.16 us  [the longest x2 4.09 us: shifted(): return lax.ppermute(value, 'blocks', pairs)]
    ppermute x5 -> x4, waiting for transfers between devices: 6.11 us -> 6.87 us  [the longest x2 5.48 us: shifted(): return lax.ppermute(value, 'blocks', pairs)]
  transfers between devices with their start and end apart: 9 -> 6, of which waited for: 6 -> 5; matrix products, arithmetic and copies ran while one was open for 1% -> 1% of each run, Pallas kernels for 0% -> 0%
where the time goes in v2:
time: 185 us; the launch traced here: 183 us
  blocking collectives  141 us (76%)
  starting transfers between devices  15.9 us (9%)
  waiting for transfers between devices  10.7 us (6%)
  Pallas kernels  9.99 us (5%)
  other arithmetic  2.66 us (1%)
  local copies, waits for them, and re-layouts  2.11 us (1%)
    all_to_all x1, blocking collectives, on_device(): lax.all_to_all(send.reshape(total, 2, lanes), TM, split_axis=0, concat_ax...  80.2 us
    all_to_all x1, blocking collectives, on_device(): lax.all_to_all(send.reshape(total, 4, lanes), TM, split_axis=0, concat_ax...  49.3 us
    all_to_all x1, blocking collectives, on_device(): back = lax.all_to_all(back, ROW, split_axis=0, concat_axis=0, tiled=True)  11.1 us
    all_to_all x1, starting transfers between devices, on_device(): lax.all_to_all(spec.reshape(owners, rows, lanes), ROW, split_axis=0, conc...  5.77 us
    ppermute x2, waiting for transfers between devices, shifted(): return lax.ppermute(value, 'blocks', pairs)  5.48 us
    ppermute x2, starting transfers between devices, shifted(): return lax.ppermute(value, 'blocks', pairs)  4.09 us
  transfers between devices with their start and end apart: 6, of which 5 were waited for; matrix products, arithmetic and copies ran while one was open for 1% of the time, Pallas kernels for 0%

profile of v2, /device:TPU:40, one launch (start us, length us, event | category | flops | bytes accessed | tf_op | source)
XLA Modules:
  0.0 182.7 jit_solution(535220426855560631)
XLA Ops:
  0.6 0.7 select_bitcast_fusion
  1.4 1.9 %collective-permute-start = (f32[16,128]{1,0:T(8,128)S(1)}, f32[16,128]{1,0:T(8,128)S(1)}, u32[]{:S(2)}, u32[]{:S(2)}) collective-permute-start(f32[16,128]{1,0:T(8,128)S(1)} %select_bitcast_fusion), channel_id=1, source_target_pairs={{0,1},{1,0},{2,3},{3,2},{4,5},{5,4},{6,7},{7,6},{8,9},{9,8},{10,11... | collective-permute-start | bytes 24584 | tf_op jit(solution)/shard_map/ppermute | solution.py:242
  3.3 1.1 collective-permute-done
  4.4 0.6 broadcast_select_fusion
  5.0 1.7 entry.1
  6.8 80.2 %all_to_all.20 = f32[128,2,128]{2,1,0:T(2,128)} all-to-all(f32[128,2,128]{2,1,0:T(2,128)} %bitcast.32), channel_id=1, replica_groups=mesh['groups'=2,'blocks'=16,'pair'=2,'tm_1'=4,'space'=2] {'blocks','pair..., dimensions={0} | all-to-all | bytes 262144 | tf_op jit(solution)/shard_map/all_to_all | solution.py:246
  87.0 2.0 %forward.1 = (f32[128,128]{1,0:T(8,128)}, f32[128,128]{1,0:T(8,128)}) custom-call(f32[256,256]{1,0:T(8,128)} %constant.39.clone.mat, f32[256,128]{1,0:T(8,128)} %bitcast.23), custom_call_target="tpu_custom_call" | custom-call | tf_op jit(solution)/shard_map/forward/pallas_call | solution.py:259
  89.0 0.0 copy-start.2
  89.0 5.8 %all-to-all-start.1 = ((f32[16,8,128]{2,1,0:T(8,128)}), f32[16,8,128]{2,1,0:T(8,128)S(1)}, u32[]{:S(2)}, u32[]{:S(2)}) async-start(f32[16,8,128]{2,1,0:T(8,128)} %bitcast.35), calls=%async_computation.1 | async-start | bytes 131072 | tf_op jit(solution)/shard_map/all_to_all | solution.py:260
  94.8 0.0 copy-done.2
  94.8 0.1 copy.8
  94.9 2.1 %collective-permute-start.3 = (f32[20,128]{1,0:T(8,128)S(1)}, f32[20,128]{1,0:T(8,128)S(1)}, u32[]{:S(2)}, u32[]{:S(2)}) collective-permute-start(f32[20,128]{1,0:T(8,128)S(1)} %pad_dynamic-slice_fusion), channel_id=1, source_target_pairs={{0,1},{1,0},{2,3},{3,2},{4,5},{5,4},{6,7},{7,6},{8,9},{9,8},{10,11... | collective-permute-start | bytes 30728 | tf_op jit(solution)/shard_map/ppermute | solution.py:252
  97.1 0.7 dynamic-slice_bitcast_fusion
  97.8 0.3 collective-permute-done.3
  98.0 2.7 %all-to-all-done.1 = f32[16,8,128]{2,1,0:T(8,128)S(1)} async-done(((f32[16,8,128]{2,1,0:T(8,128)}), f32[16,8,128]{2,1,0:T(8,128)S(1)}, u32[]{:S(2)}, u32[]{:S(2)}) %all-to-all-start.1) | async-done | bytes 65568 | tf_op jit(solution)/shard_map/all_to_all | solution.py:260
  100.7 0.0 copy-start.1
  100.8 0.6 copy-done.1
  101.4 2.8 %collective-permute-start.1 = (f32[6,2,8,128]{3,2,1,0:T(8,128)S(1)}, f32[6,2,8,128]{3,2,1,0:T(8,128)S(1)}, u32[]{:S(2)}, u32[]{:S(2)}) collective-permute-start(f32[6,2,8,128]{3,2,1,0:T(8,128)S(1)} %bitcast.37), channel_id=1, source_target_pairs={{0,16},{16,32},{32,48},{48,64},{64,80},{80,96},{96,112},{112,128},... | collective-permute-start | bytes 147464 | tf_op jit(solution)/shard_map/ppermute | solution.py:266
  104.2 1.3 collective-permute-start.2
  105.5 0.6 maximum_select_fusion
  106.1 0.0 collective-permute-done.1.left
  106.1 0.0 copy-start.3
  106.1 5.5 %collective-permute-done.2.right = f32[6,2,8,128]{3,2,1,0:T(8,128)S(1)} collective-permute-done((f32[6,2,8,128]{3,2,1,0:T(8,128)S(1)}, f32[6,2,8,128]{3,2,1,0:T(8,128)S(1)}, u32[]{:S(2)}, u32[]{:S(2)}) %collective-permute-start.2) | collective-permute-done | bytes 49184 | tf_op jit(solution)/shard_map/ppermute | solution.py:266
  111.6 0.0 copy-start.4
  111.6 0.7 broadcast_in_dim.25.lam
  112.3 0.0 copy-done.3
  112.3 0.0 copy-done.4
  112.3 2.3 %sweeps.1 = f32[16,2,8,128]{3,2,1,0:T(8,128)} custom-call(f32[6,2,8,128]{3,2,1,0:T(8,128)} %copy-done.3, f32[8,2,8,128]{3,2,1,0:T(8,128)} %bitcast.26, f32[6,2,8,128]{3,2,1,0:T(8,128)} %copy-done.4, f32[40,128]{1,0:T(8,128)} %bitcast.33, f32[2,8,128]{2,1,0:T(8,128)} %broadcast_in_dim.25.lam), custom_call_target="tpu_custom_call" | custom-call | tf_op jit(solution)/shard_map/sweeps/pallas_call | solution.py:270
  114.6 11.1 %all_to_all.21 = f32[16,2,8,128]{3,2,1,0:T(8,128)} all-to-all(f32[16,2,8,128]{3,2,1,0:T(8,128)} %sweeps.1), channel_id=1, replica_groups=mesh['groups'=2,'blocks'=16,'pair'=2,'tm_1'=4,'space'=2] {'pair','tm_1',..., dimensions={0} | all-to-all | bytes 262144 | tf_op jit(solution)/shard_map/all_to_all | solution.py:271
  125.6 2.2 %backward.1 = f32[512,128]{1,0:T(8,128)} custom-call(f32[256,256]{1,0:T(8,128)} %constant.40.clone.mat, f32[256,128]{1,0:T(8,128)} %bitcast.27, f32[128,128]{1,0:T(8,128)} %get-tuple-element.10.hist, f32[256,128]{1,0:T(8,128)} %bitcast.24), custom_call_target="tpu_custom_call" | custom-call | tf_op jit(solution)/shard_map/backward/pallas_call | solution.py:272
  127.9 49.3 %all_to_all.22 = f32[128,4,128]{2,1,0:T(4,128)S(1)} all-to-all(f32[128,4,128]{2,1,0:T(4,128)} %bitcast.25), channel_id=1, replica_groups=mesh['groups'=2,'blocks'=16,'pair'=2,'tm_1'=4,'space'=2] {'blocks','pair..., dimensions={0} | all-to-all | bytes 524288 | tf_op jit(solution)/shard_map/all_to_all | solution.py:273
  177.2 0.0 copy-start
  177.2 0.2 slice_reduce_fusion
  177.3 1.9 %collective-permute-start.4 = (f32[1,128]{1,0:T(1,128)S(1)}, f32[1,128]{1,0:T(1,128)S(1)}, u32[]{:S(2)}, u32[]{:S(2)}) collective-permute-start(f32[1,128]{1,0:T(1,128)S(1)} %bitcast.38), channel_id=1, source_target_pairs={{0,1},{1,0},{2,3},{3,2},{4,5},{5,4},{6,7},{7,6},{8,9},{9,8},{10,11... | collective-permute-start | bytes 1544 | tf_op jit(solution)/shard_map/ppermute | solution.py:277
  179.3 1.1 collective-permute-done.4
  180.4 0.5 bitcast_add_fusion.sums
  180.9 0.0 copy-done
  180.9 1.7 exit.1
  (4 shorter events, 0.0 us)
Async XLA Ops:
  1.4 3.1 %collective-permute-start = (f32[16,128]{1,0:T(8,128)S(1)}, f32[16,128]{1,0:T(8,128)S(1)}, u32[]{:S(2)}, u32[]{:S(2)}) collective-permute-start(f32[16,128]{1,0:T(8,128)S(1)} %select_bitcast_fusion), channel_id=1, source_target_pairs={{0,1},{1,0},{2,3},{3,2},{4,5},{5,4},{6,7},{7,6},{8,9},{9,8},{10,11... | collective-permute-start | bytes 24584 | tf_op jit(solution)/shard_map/ppermute | solution.py:242
  89.0 5.8 %copy-start.2 = (f32[8,16,128]{2,1,0:T(8,128)S(1)}, f32[8,16,128]{2,1,0:T(8,128)}, u32[]{:S(2)}) copy-start(f32[8,16,128]{2,1,0:T(8,128)} %kappa.1) | copy-start | bytes 196612
  89.0 11.7 %all-to-all-start.1 = ((f32[16,8,128]{2,1,0:T(8,128)}), f32[16,8,128]{2,1,0:T(8,128)S(1)}, u32[]{:S(2)}, u32[]{:S(2)}) async-start(f32[16,8,128]{2,1,0:T(8,128)} %bitcast.35), calls=%async_computation.1 | async-start | bytes 131072 | tf_op jit(solution)/shard_map/all_to_all | solution.py:260
  94.9 3.1 %collective-permute-start.3 = (f32[20,128]{1,0:T(8,128)S(1)}, f32[20,128]{1,0:T(8,128)S(1)}, u32[]{:S(2)}, u32[]{:S(2)}) collective-permute-start(f32[20,128]{1,0:T(8,128)S(1)} %pad_dynamic-slice_fusion), channel_id=1, source_target_pairs={{0,1},{1,0},{2,3},{3,2},{4,5},{5,4},{6,7},{7,6},{8,9},{9,8},{10,11... | collective-permute-start | bytes 30728 | tf_op jit(solution)/shard_map/ppermute | solution.py:252
  100.7 0.6 copy-start.1
  101.4 4.7 %collective-permute-start.1 = (f32[6,2,8,128]{3,2,1,0:T(8,128)S(1)}, f32[6,2,8,128]{3,2,1,0:T(8,128)S(1)}, u32[]{:S(2)}, u32[]{:S(2)}) collective-permute-start(f32[6,2,8,128]{3,2,1,0:T(8,128)S(1)} %bitcast.37), channel_id=1, source_target_pairs={{0,16},{16,32},{32,48},{48,64},{64,80},{80,96},{96,112},{112,128},... | collective-permute-start | bytes 147464 | tf_op jit(solution)/shard_map/ppermute | solution.py:266
  104.2 7.4 %collective-permute-start.2 = (f32[6,2,8,128]{3,2,1,0:T(8,128)S(1)}, f32[6,2,8,128]{3,2,1,0:T(8,128)S(1)}, u32[]{:S(2)}, u32[]{:S(2)}) collective-permute-start(f32[6,2,8,128]{3,2,1,0:T(8,128)S(1)} %bitcast.36), channel_id=1, source_target_pairs={{16,0},{32,16},{48,32},{64,48},{80,64},{96,80},{112,96},{128,112},... | collective-permute-start | bytes 147464 | tf_op jit(solution)/shard_map/ppermute | solution.py:266
  106.1 6.1 %copy-start.3 = (f32[6,2,8,128]{3,2,1,0:T(8,128)}, f32[6,2,8,128]{3,2,1,0:T(8,128)S(1)}, u32[]{:S(2)}) copy-start(f32[6,2,8,128]{3,2,1,0:T(8,128)S(1)} %collective-permute-done.1.left) | copy-start | bytes 147460
  111.6 0.7 copy-start.4
  177.2 3.8 %copy-start = (f32[128,4,128]{2,1,0:T(4,128)}, f32[128,4,128]{2,1,0:T(4,128)S(1)}, u32[]{:S(2)}) copy-start(f32[128,4,128]{2,1,0:T(4,128)S(1)} %all_to_all.22) | copy-start | bytes 786436
  177.3 3.1 %collective-permute-start.4 = (f32[1,128]{1,0:T(1,128)S(1)}, f32[1,128]{1,0:T(1,128)S(1)}, u32[]{:S(2)}, u32[]{:S(2)}) collective-permute-start(f32[1,128]{1,0:T(1,128)S(1)} %bitcast.38), channel_id=1, source_target_pairs={{0,1},{1,0},{2,3},{3,2},{4,5},{5,4},{6,7},{7,6},{8,9},{9,8},{10,11... | collective-permute-start | bytes 1544 | tf_op jit(solution)/shard_map/ppermute | solution.py:277

commit v3 on v2

--- a/solution.py
+++ b/solution.py
@@ -74,16 +74,22 @@
     )
 
 
-def local_call(kernel, name, outs, inputs, scratch=()):
+def local_call(kernel, name, outs, inputs, scratch=(), keep_out=True):
     vmem = pl.BlockSpec(memory_space=pltpu.VMEM)
-    return pl.pallas_call(
+    made = pltpu.VMEM if keep_out else jax.ShapeDtypeStruct
+    call = pl.pallas_call(
         kernel,
-        out_shape=[jax.ShapeDtypeStruct(shape, jnp.float32) for shape in outs],
+        out_shape=[made(shape, jnp.float32) for shape in outs],
         in_specs=[vmem] * inputs,
         out_specs=[vmem] * len(outs),
         scratch_shapes=list(scratch),
         name=name,
     )
+
+    def placed(*args):
+        return call(*(pltpu.with_memory_space_constraint(a, pltpu.VMEM) for a in args))
+
+    return placed
 
 
 def iota(shape, dim):
@@ -150,7 +156,7 @@
         new_u[...] = u[...] + step * slab(0)
         new_r[...] = s[...] - slab(2) - step * slab(1)
 
-    return local_call(kernel, "exit", [(nz, ny, nx)] * 2, 4)
+    return local_call(kernel, "exit", [(nz, ny, nx)] * 2, 4, keep_out=False)
 
 
 def make_sweeps(own, depth, rows, lanes, ny):
@@ -255,6 +261,7 @@
     ).reshape(-1, lanes)
     lam = lax.dynamic_index_in_dim(jnp.asarray(lams), lax.axis_index(ROW), axis=0, keepdims=False)
     lam = jnp.broadcast_to(lam[:, :, None], (2, rows, lanes))
+    cells, kap, lam = lax.optimization_barrier((cells, kap, lam))
 
     hist_u, spec = make_forward(total, lanes)(first_mat, cells)
     spec = lax.all_to_all(

time: 185 us -> 176 us (0.951)
  blocking collectives: 141 us -> 70.1 us
  starting transfers between devices: 15.9 us -> 63.1 us
  waiting for transfers between devices: 10.7 us -> 32.5 us
  Pallas kernels: 9.99 us -> 3.2 us
    all_to_all x1, blocking collectives: 80.2 us -> 11.4 us  [on_device(): lax.all_to_all(spec.reshape(owners, rows, lanes), ROW, split_axis=0, conc...]
    all_to_all x1, starting transfers between devices: 5.77 us -> 53.3 us  [on_device(): lax.all_to_all(send.reshape(total, 2, lanes), TM, split_axis=0, concat_ax...]
    all_to_all x1, waiting for transfers between devices: 2.71 us -> 23.7 us  [on_device(): lax.all_to_all(send.reshape(total, 2, lanes), TM, split_axis=0, concat_ax...]
    pallas_call x5, Pallas kernels: 9.99 us -> 3.2 us  [placed(): call(*(pltpu.with_memory_space_constraint(a, pltpu.VMEM) for a in args))]
  transfers between devices with their start and end apart: 6 -> 6, of which waited for: 5 -> 6; matrix products, arithmetic and copies ran while one was open for 1% -> 0% of each run, Pallas kernels for 0% -> 0%
where the time goes in v3:
time: 176 us; the launch traced here: 173 us
  blocking collectives  70.1 us (40%)
  starting transfers between devices  63.1 us (36%)
  waiting for transfers between devices  32.5 us (18%)
  Pallas kernels  3.2 us (2%)
  local copies, waits for them, and re-layouts  2.58 us (1%)
    all_to_all x1, starting transfers between devices, on_device(): lax.all_to_all(send.reshape(total, 2, lanes), TM, split_axis=0, concat_ax...  53.3 us
    all_to_all x1, blocking collectives, on_device(): lax.all_to_all(send.reshape(total, 4, lanes), TM, split_axis=0, concat_ax...  49.2 us
    all_to_all x1, waiting for transfers between devices, on_device(): lax.all_to_all(send.reshape(total, 2, lanes), TM, split_axis=0, concat_ax...  23.7 us
    all_to_all x1, blocking collectives, on_device(): lax.all_to_all(spec.reshape(owners, rows, lanes), ROW, split_axis=0, conc...  11.4 us
    all_to_all x1, blocking collectives, on_device(): back = lax.all_to_all(back, ROW, split_axis=0, concat_axis=0, tiled=True)  9.48 us
    ppermute x2, waiting for transfers between devices, shifted(): return lax.ppermute(value, 'blocks', pairs)  6.12 us
    ppermute x2, starting transfers between devices, shifted(): return lax.ppermute(value, 'blocks', pairs)  3.98 us
  transfers between devices with their start and end apart: 6, of which 6 were waited for; matrix products, arithmetic and copies ran while one was open for 0% of the time, Pallas kernels for 0%

profile of v3, /device:TPU:40, one launch (start us, length us, event | category | flops | bytes accessed | tf_op | source)
XLA Modules:
  0.0 173.2 jit_solution(2356847878037967784)
XLA Ops:
  0.6 0.0 copy-start
  0.6 0.8 select_bitcast_fusion
  1.4 1.9 %collective-permute-start = (f32[16,128]{1,0:T(8,128)S(1)}, f32[16,128]{1,0:T(8,128)S(1)}, u32[]{:S(2)}, u32[]{:S(2)}) collective-permute-start(f32[16,128]{1,0:T(8,128)S(1)} %select_bitcast_fusion), channel_id=1, source_target_pairs={{0,1},{1,0},{2,3},{3,2},{4,5},{5,4},{6,7},{7,6},{8,9},{9,8},{10,11... | collective-permute-start | bytes 24584 | tf_op jit(solution)/shard_map/ppermute | solution.py:248
  3.4 1.1 collective-permute-done
  4.5 0.0 copy-done
  4.5 0.0 copy-start.3
  4.5 0.8 copy-done.3
  5.3 0.0 copy-start.5
  5.3 0.8 copy-done.5
  6.2 0.0 copy-start.4
  6.2 0.8 entry.1
  7.0 0.0 copy-start.1
  7.0 53.3 %all-to-all-start = ((f32[128,2,128]{2,1,0:T(2,128)}), f32[128,2,128]{2,1,0:T(2,128)S(1)}, u32[]{:S(2)}, u32[]{:S(2)}) async-start(f32[128,2,128]{2,1,0:T(2,128)} %bitcast.3), calls=%async_computation | async-start | bytes 262144 | tf_op jit(solution)/shard_map/all_to_all | solution.py:252
  60.3 0.0 copy-done.4
  60.3 0.1 copy.8
  60.5 2.0 %collective-permute-start.1 = (f32[20,128]{1,0:T(8,128)S(1)}, f32[20,128]{1,0:T(8,128)S(1)}, u32[]{:S(2)}, u32[]{:S(2)}) collective-permute-start(f32[20,128]{1,0:T(8,128)S(1)} %pad_dynamic-slice_fusion), channel_id=1, source_target_pairs={{0,1},{1,0},{2,3},{3,2},{4,5},{5,4},{6,7},{7,6},{8,9},{9,8},{10,11... | collective-permute-start | bytes 30728 | tf_op jit(solution)/shard_map/ppermute | solution.py:258
  62.4 0.7 dynamic-slice_bitcast_fusion
  63.1 0.4 collective-permute-done.1
  63.6 23.7 %all-to-all-done = f32[128,2,128]{2,1,0:T(2,128)S(1)} async-done(((f32[128,2,128]{2,1,0:T(2,128)}), f32[128,2,128]{2,1,0:T(2,128)S(1)}, u32[]{:S(2)}, u32[]{:S(2)}) %all-to-all-start) | async-done | bytes 131104 | tf_op jit(solution)/shard_map/all_to_all | solution.py:252
  87.3 0.1 broadcast_in_dim.25.lam
  87.3 0.0 copy-done.1
  87.3 0.4 forward.1
  87.7 11.4 %all_to_all.20 = f32[16,8,128]{2,1,0:T(8,128)S(1)} all-to-all(f32[16,8,128]{2,1,0:T(8,128)S(1)} %bitcast.33), channel_id=1, replica_groups=mesh['groups'=2,'blocks'=16,'pair'=2,'tm_1'=4,'space'=2] {'pair','tm_1',..., dimensions={0} | all-to-all | bytes 131072 | tf_op jit(solution)/shard_map/all_to_all | solution.py:267
  99.1 2.7 %collective-permute-start.2 = (f32[6,2,8,128]{3,2,1,0:T(8,128)S(1)}, f32[6,2,8,128]{3,2,1,0:T(8,128)S(1)}, u32[]{:S(2)}, u32[]{:S(2)}) collective-permute-start(f32[6,2,8,128]{3,2,1,0:T(8,128)S(1)} %bitcast.36), channel_id=1, source_target_pairs={{0,16},{16,32},{32,48},{48,64},{64,80},{80,96},{96,112},{112,128},... | collective-permute-start | bytes 147464 | tf_op jit(solution)/shard_map/ppermute | solution.py:273
  101.8 1.3 collective-permute-start.3
  103.1 0.4 collective-permute-done.2.left
  103.6 5.7 %collective-permute-done.3.right = f32[6,2,8,128]{3,2,1,0:T(8,128)S(1)} collective-permute-done((f32[6,2,8,128]{3,2,1,0:T(8,128)S(1)}, f32[6,2,8,128]{3,2,1,0:T(8,128)S(1)}, u32[]{:S(2)}, u32[]{:S(2)}) %collective-permute-start.3) | collective-permute-done | bytes 49184 | tf_op jit(solution)/shard_map/ppermute | solution.py:273
  109.3 0.0 copy-start.2
  109.3 0.8 sweeps.1
  110.0 9.5 %all_to_all.21 = f32[16,2,8,128]{3,2,1,0:T(8,128)S(1)} all-to-all(f32[16,2,8,128]{3,2,1,0:T(8,128)S(1)} %sweeps.1), channel_id=1, replica_groups=mesh['groups'=2,'blocks'=16,'pair'=2,'tm_1'=4,'space'=2] {'pair','tm_1',..., dimensions={0} | all-to-all | bytes 262144 | tf_op jit(solution)/shard_map/all_to_all | solution.py:278
  119.5 0.0 copy-done.2
  119.5 0.5 backward.1
  120.0 49.2 %all_to_all.22 = f32[128,4,128]{2,1,0:T(4,128)S(1)} all-to-all(f32[128,4,128]{2,1,0:T(4,128)S(1)} %bitcast.25), channel_id=1, replica_groups=mesh['groups'=2,'blocks'=16,'pair'=2,'tm_1'=4,'space'=2] {'blocks','pair..., dimensions={0} | all-to-all | bytes 524288 | tf_op jit(solution)/shard_map/all_to_all | solution.py:280
  169.2 0.2 slice_reduce_fusion
  169.3 1.9 %collective-permute-start.4 = (f32[1,128]{1,0:T(1,128)S(1)}, f32[1,128]{1,0:T(1,128)S(1)}, u32[]{:S(2)}, u32[]{:S(2)}) collective-permute-start(f32[1,128]{1,0:T(1,128)S(1)} %bitcast.37), channel_id=1, source_target_pairs={{0,1},{1,0},{2,3},{3,2},{4,5},{5,4},{6,7},{7,6},{8,9},{9,8},{10,11... | collective-permute-start | bytes 1544 | tf_op jit(solution)/shard_map/ppermute | solution.py:284
  171.3 1.1 collective-permute-done.4
  172.4 0.8 exit.1
  (7 shorter events, 0.1 us)
Async XLA Ops:
  0.6 3.9 %copy-start = (f32[1,8,16,128]{3,2,1,0:T(8,128)S(1)}, f32[1,8,16,128]{3,2,1,0:T(8,128)}, u32[]{:S(2)}) copy-start(f32[1,8,16,128]{3,2,1,0:T(8,128)} %param.6) | copy-start | bytes 196612
  1.4 3.1 %collective-permute-start = (f32[16,128]{1,0:T(8,128)S(1)}, f32[16,128]{1,0:T(8,128)S(1)}, u32[]{:S(2)}, u32[]{:S(2)}) collective-permute-start(f32[16,128]{1,0:T(8,128)S(1)} %select_bitcast_fusion), channel_id=1, source_target_pairs={{0,1},{1,0},{2,3},{3,2},{4,5},{5,4},{6,7},{7,6},{8,9},{9,8},{10,11... | collective-permute-start | bytes 24584 | tf_op jit(solution)/shard_map/ppermute | solution.py:248
  4.5 0.8 copy-start.3
  5.3 0.8 copy-start.5
  6.2 54.2 %copy-start.4 = (f32[8,16,128]{2,1,0:T(8,128)S(1)}, f32[8,16,128]{2,1,0:T(8,128)}, u32[]{:S(2)}) copy-start(f32[8,16,128]{2,1,0:T(8,128)} %kappa.1) | copy-start | bytes 196612
  7.0 80.3 %copy-start.1 = (f32[256,256]{1,0:T(8,128)S(1)}, f32[256,256]{1,0:T(8,128)}, u32[]{:S(2)}) copy-start(f32[256,256]{1,0:T(8,128)} %constant.39.clone.mat) | copy-start | bytes 786436
  7.0 80.3 %all-to-all-start = ((f32[128,2,128]{2,1,0:T(2,128)}), f32[128,2,128]{2,1,0:T(2,128)S(1)}, u32[]{:S(2)}, u32[]{:S(2)}) async-start(f32[128,2,128]{2,1,0:T(2,128)} %bitcast.3), calls=%async_computation | async-start | bytes 262144 | tf_op jit(solution)/shard_map/all_to_all | solution.py:252
  60.5 3.1 %collective-permute-start.1 = (f32[20,128]{1,0:T(8,128)S(1)}, f32[20,128]{1,0:T(8,128)S(1)}, u32[]{:S(2)}, u32[]{:S(2)}) collective-permute-start(f32[20,128]{1,0:T(8,128)S(1)} %pad_dynamic-slice_fusion), channel_id=1, source_target_pairs={{0,1},{1,0},{2,3},{3,2},{4,5},{5,4},{6,7},{7,6},{8,9},{9,8},{10,11... | collective-permute-start | bytes 30728 | tf_op jit(solution)/shard_map/ppermute | solution.py:258
  99.1 4.4 %collective-permute-start.2 = (f32[6,2,8,128]{3,2,1,0:T(8,128)S(1)}, f32[6,2,8,128]{3,2,1,0:T(8,128)S(1)}, u32[]{:S(2)}, u32[]{:S(2)}) collective-permute-start(f32[6,2,8,128]{3,2,1,0:T(8,128)S(1)} %bitcast.36), channel_id=1, source_target_pairs={{0,16},{16,32},{32,48},{48,64},{64,80},{80,96},{96,112},{112,128},... | collective-permute-start | bytes 147464 | tf_op jit(solution)/shard_map/ppermute | solution.py:273
  101.8 7.4 %collective-permute-start.3 = (f32[6,2,8,128]{3,2,1,0:T(8,128)S(1)}, f32[6,2,8,128]{3,2,1,0:T(8,128)S(1)}, u32[]{:S(2)}, u32[]{:S(2)}) collective-permute-start(f32[6,2,8,128]{3,2,1,0:T(8,128)S(1)} %bitcast.35), channel_id=1, source_target_pairs={{16,0},{32,16},{48,32},{64,48},{80,64},{96,80},{112,96},{128,112},... | collective-permute-start | bytes 147464 | tf_op jit(solution)/shard_map/ppermute | solution.py:273
  109.3 10.2 %copy-start.2 = (f32[256,256]{1,0:T(8,128)S(1)}, f32[256,256]{1,0:T(8,128)}, u32[]{:S(2)}) copy-start(f32[256,256]{1,0:T(8,128)} %constant.40.clone.mat) | copy-start | bytes 786436
  169.3 3.1 %collective-permute-start.4 = (f32[1,128]{1,0:T(1,128)S(1)}, f32[1,128]{1,0:T(1,128)S(1)}, u32[]{:S(2)}, u32[]{:S(2)}) collective-permute-start(f32[1,128]{1,0:T(1,128)S(1)} %bitcast.37), channel_id=1, source_target_pairs={{0,1},{1,0},{2,3},{3,2},{4,5},{5,4},{6,7},{7,6},{8,9},{9,8},{10,11... | collective-permute-start | bytes 1544 | tf_op jit(solution)/shard_map/ppermute | solution.py:284

commit v4 on v3

--- a/solution.py
+++ b/solution.py
@@ -8,6 +8,7 @@
 from jax.experimental.pallas import tpu as pltpu
 from jax.sharding import Mesh
 from jax.sharding import PartitionSpec as P
+
 
 SWEEPS = 6
 TM = ("blocks", "pair", "tm_1")
@@ -57,10 +58,12 @@
                 lams[q, 0, :, j] = lam[k].real
                 lams[q, 1, :, j] = lam[k].imag
     fwd = fwd.reshape(total, total)
-    first_mat = np.zeros((2, total, total, 2))
-    first_mat[0, :, :, 0] = hist
-    first_mat[1, :, :, 0] = -fwd @ hist
-    first_mat[1, :, :, 1] = fwd
+    first_mat = np.zeros((3 * total, total, 2))
+    first_mat[:total, :, 0] = hist
+    spectra = first_mat[total:].reshape(owners, 2, 2 * here, total, 2)
+    spectra[:, 0, :, :, 0] = (-fwd @ hist).reshape(owners, 2 * here, total)
+    spectra[:, 0, :, :, 1] = fwd.reshape(owners, 2 * here, total)
+    spectra[:, 1, :, :, 0] = fwd.reshape(owners, 2 * here, total)
     flat = inv.reshape(total, total)
     second_mat = np.zeros((2, total, owners, 2, 2 * here))
     second_mat[0, :, :, 0] = flat.reshape(total, owners, 2 * here)
@@ -68,13 +71,13 @@
     second_mat[1, :, :, 1] = flat.reshape(total, owners, 2 * here)
     f32 = np.float32
     return (
-        first_mat.reshape(2 * total, 2 * total).astype(f32),
+        first_mat.reshape(3 * total, 2 * total).astype(f32),
         second_mat.reshape(2 * total, 2 * total).astype(f32),
         lams.reshape(owners, 2, 2 * here).astype(f32),
     )
 
 
-def local_call(kernel, name, outs, inputs, scratch=(), keep_out=True):
+def local_call(kernel, outs, inputs, scratch=(), keep_in=True, keep_out=True):
     vmem = pl.BlockSpec(memory_space=pltpu.VMEM)
     made = pltpu.VMEM if keep_out else jax.ShapeDtypeStruct
     call = pl.pallas_call(
@@ -83,11 +86,12 @@
         in_specs=[vmem] * inputs,
         out_specs=[vmem] * len(outs),
         scratch_shapes=list(scratch),
-        name=name,
     )
 
     def placed(*args):
-        return call(*(pltpu.with_memory_space_constraint(a, pltpu.VMEM) for a in args))
+        if keep_in:
+            args = [pltpu.with_memory_space_constraint(a, pltpu.VMEM) for a in args]
+        return call(*args)
 
     return placed
 
@@ -99,36 +103,63 @@
 def make_entry(nz, ny, nx):
     lanes = nz * ny
 
-    def kernel(u, f, kappa, before, after, s, out):
+    def kernel(u, f, kappa, s, out):
         row, lane = iota((ny, nx), 0), iota((ny, nx), 1)
         for z in range(nz):
             v = u[z]
-            near = (before[...] if z == 0 else u[z - 1]) + (after[...] if z == nz - 1 else u[z + 1])
-            near = near + jnp.where(row == 0, 0.0, pltpu.roll(v, 1, 0))
+            near = jnp.where(row == 0, 0.0, pltpu.roll(v, 1, 0))
             near = near + jnp.where(row == ny - 1, 0.0, pltpu.roll(v, ny - 1, 0))
             near = near + jnp.where(lane == 0, 0.0, pltpu.roll(v, 1, 1))
             near = near + jnp.where(lane == nx - 1, 0.0, pltpu.roll(v, nx - 1, 1))
+            if z > 0:
+                near = near + u[z - 1]
+            if z < nz - 1:
+                near = near + u[z + 1]
             s[z] = f[z] - kappa[z] * (6.0 * v - near)
         out[pl.ds(0, nx, stride=2), :] = u[...].reshape(lanes, nx).T
         out[pl.ds(1, nx, stride=2), :] = s[...].reshape(lanes, nx).T
 
-    return local_call(kernel, "entry", [(nz, ny, nx), (2 * nx, lanes)], 5)
-
-
-def make_forward(total, lanes):
-    def kernel(mat, cells, hist, spec):
-        both = jnp.dot(mat[...], cells[...], precision=HIGH, preferred_element_type=jnp.float32)
-        hist[...] = both[:total]
-        spec[...] = both[total:]
-
-    return local_call(kernel, "forward", [(total, lanes)] * 2, 2)
+    return local_call(kernel, [(nz, ny, nx), (2 * nx, lanes)], 3, keep_in=False)
+
+
+def make_forward(total, lanes, ny):
+    def kernel(mat, cells, masks, hist, spec, edge):
+        out = jnp.dot(mat[...], cells[...], precision=HIGH, preferred_element_type=jnp.float32)
+        hist[...] = out[:total]
+        spec[...] = out[total:]
+        u = cells[pl.ds(0, total, stride=2), :]
+        edge[...] = masks[0:1, :] * pltpu.roll(u, ny, 1) + masks[1:2, :] * pltpu.roll(
+            u, lanes - ny, 1
+        )
+
+    return local_call(kernel, [(total, lanes), (2 * total, lanes), (total, lanes)], 3)
+
+
+def make_border(own, depth, rows, lanes, ny):
+    def kernel(spec, kap, out, to_right, to_left):
+        lane = iota((rows, lanes), 1)
+        first, last = lane < ny, lane >= lanes - ny
+        for c in range(own):
+            for h in range(2):
+                at = 2 * (depth + c) + h
+                k = jnp.broadcast_to(kap[at : at + 1, :], (rows, lanes))
+                other = pltpu.roll(spec[c, 1 - h, rows:, :], ny if h else lanes - ny, 1)
+                value = spec[c, h, :rows, :] + jnp.where(first if h else last, k * other, 0.0)
+                out[c, h] = value
+                if c >= own - depth:
+                    to_right[c - (own - depth), h] = value
+                if c < depth:
+                    to_left[c, h] = value
+
+    shapes = [(count, 2, rows, lanes) for count in (own, depth, depth)]
+    return local_call(kernel, shapes, 2)
 
 
 def make_backward(total, lanes):
-    def kernel(mat, back, hist, cells, out):
+    def kernel(mat, back, hist, cells, edge, kap, out):
         both = jnp.dot(mat[...], back[...], precision=HIGH, preferred_element_type=jnp.float32)
         image = both[total:]
-        residual = cells[pl.ds(1, total, stride=2), :] - hist[...]
+        residual = cells[pl.ds(1, total, stride=2), :] - hist[...] + kap[...] * edge[...]
         ri = jnp.sum(residual * image, axis=0, keepdims=True)
         ii = jnp.sum(image * image, axis=0, keepdims=True)
         low = iota((1, lanes), 1) < lanes // 2
@@ -138,13 +169,13 @@
         out[pl.ds(2, total, stride=4), :] = hist[...]
         out[pl.ds(3, total, stride=4), :] = jnp.broadcast_to(sums, (total, lanes))
 
-    return local_call(kernel, "backward", [(4 * total, lanes)], 4)
+    return local_call(kernel, [(4 * total, lanes)], 6)
 
 
 def make_exit(nz, ny, nx):
     lanes = nz * ny
 
-    def kernel(times, sums, u, s, new_u, new_r):
+    def kernel(times, sums, u, s, low_plane, high_plane, new_u, new_r):
         low = iota((1, lanes), 1) < lanes // 2
         ri = jnp.sum(jnp.where(low, sums[...], 0.0), axis=1, keepdims=True)
         ii = jnp.sum(jnp.where(low, 0.0, sums[...]), axis=1, keepdims=True)
@@ -154,9 +185,12 @@
             return times[pl.ds(k, nx, stride=4), :].T.reshape(nz, ny, nx)
 
         new_u[...] = u[...] + step * slab(0)
-        new_r[...] = s[...] - slab(2) - step * slab(1)
-
-    return local_call(kernel, "exit", [(nz, ny, nx)] * 2, 4, keep_out=False)
+        plane = s[...] - slab(2) - step * slab(1)
+        new_r[...] = plane
+        new_r[0] = plane[0] + low_plane[...]
+        new_r[nz - 1] = plane[nz - 1] + high_plane[...]
+
+    return local_call(kernel, [(nz, ny, nx)] * 2, 6, keep_out=False)
 
 
 def make_sweeps(own, depth, rows, lanes, ny):
@@ -226,7 +260,7 @@
                 out[row, 1] = k * (6.0 * sol - near[h])
 
     field = pltpu.VMEM((cols, 2, rows, lanes), jnp.float32)
-    return local_call(kernel, "sweeps", [(2 * own, 2, rows, lanes)], 5, [field] * 5)
+    return local_call(kernel, [(2 * own, 2, rows, lanes)], 5, [field] * 5)
 
 
 def on_device(iterate, source, diffusivity):
@@ -245,45 +279,65 @@
     swap = [(0, 1), (1, 0)]
 
     u, f = iterate[0], source[0]
-    got = lax.ppermute(jnp.where(core == 0, u[nz - 1], u[0]), "space", swap)
-    before = jnp.where(core == 0, 0.0, got)
-    after = jnp.where(core == 0, got, 0.0)
-    s, send = make_entry(nz, ny, nx)(u, f, diffusivity, before, after)
+    s, send = make_entry(nz, ny, nx)(u, f, diffusivity)
+    send, u, diffusivity = lax.optimization_barrier((send, u, diffusivity))
     cells = lax.all_to_all(
         send.reshape(total, 2, lanes), TM, split_axis=0, concat_axis=0, tiled=True
     ).reshape(2 * total, lanes)
 
     kap = jnp.pad(diffusivity.reshape(lanes, nx).T, ((depth, depth), (0, 0)))
     kap = lax.dynamic_slice_in_dim(kap, block * own, own + 2 * depth, axis=0)
-    kap_other = lax.ppermute(kap, "space", swap)
+    my_kap = lax.dynamic_slice_in_dim(kap, depth + lax.axis_index(TM[1:]), 1, axis=0)
+    edge = jnp.where(core == 0, u[nz - 1], u[0])
+    got = lax.ppermute(jnp.concatenate([edge, kap], axis=0), "space", swap)
+    got_edge, kap_other = got[:ny], got[ny:]
     kap = jnp.where(
         core == 0, jnp.stack([kap, kap_other], axis=1), jnp.stack([kap_other, kap], axis=1)
     ).reshape(-1, lanes)
+    low_plane = jnp.where(core == 0, 0.0, diffusivity[0] * got_edge)
+    high_plane = jnp.where(core == 0, diffusivity[nz - 1] * got_edge, 0.0)
+    lane = jnp.arange(lanes, dtype=jnp.int32)
+    masks = jnp.where(
+        core == 0,
+        jnp.stack([lane < ny, lane < 0]),
+        jnp.stack([lane < 0, lane >= lanes - ny]),
+    ).astype(jnp.float32)
     lam = lax.dynamic_index_in_dim(jnp.asarray(lams), lax.axis_index(ROW), axis=0, keepdims=False)
     lam = jnp.broadcast_to(lam[:, :, None], (2, rows, lanes))
-    cells, kap, lam = lax.optimization_barrier((cells, kap, lam))
-
-    hist_u, spec = make_forward(total, lanes)(first_mat, cells)
+    cells, kap, my_kap, low_plane, high_plane, masks, lam = lax.optimization_barrier(
+        (cells, kap, my_kap, low_plane, high_plane, masks, lam)
+    )
+
+    hist_u, spec, edge_u = make_forward(total, lanes, ny)(first_mat, cells, masks)
     spec = lax.all_to_all(
-        spec.reshape(owners, rows, lanes), ROW, split_axis=0, concat_axis=0, tiled=True
-    ).reshape(own, cores, rows, lanes)
+        spec.reshape(owners, 2 * rows, lanes), ROW, split_axis=0, concat_axis=0, tiled=True
+    )
+    spec, to_right, to_left = make_border(own, depth, rows, lanes, ny)(
+        spec.reshape(own, cores, 2 * rows, lanes), kap
+    )
+
+    to_right, to_left, edge_u = lax.optimization_barrier((to_right, to_left, edge_u))
 
     def shifted(value, offset):
         pairs = [(i, i + offset) for i in range(blocks) if 0 <= i + offset < blocks]
         return lax.ppermute(value, "blocks", pairs)
 
-    left = shifted(spec[own - depth :], 1)
-    right = shifted(spec[:depth], -1)
+    left = shifted(to_right, 1)
+    right = shifted(to_left, -1)
+    edge_u = lax.ppermute(edge_u, "space", swap)
+    left, right, edge_u = lax.optimization_barrier((left, right, edge_u))
     (back,) = make_sweeps(own, depth, rows, lanes, ny)(left, spec, right, kap, lam)
     back = lax.all_to_all(back, ROW, split_axis=0, concat_axis=0, tiled=True)
-    (send,) = make_backward(total, lanes)(second_mat, back.reshape(2 * total, lanes), hist_u, cells)
+    (send,) = make_backward(total, lanes)(
+        second_mat, back.reshape(2 * total, lanes), hist_u, cells, edge_u, my_kap
+    )
     times = lax.all_to_all(
         send.reshape(total, 4, lanes), TM, split_axis=0, concat_axis=0, tiled=True
     )
     sums = jnp.sum(times[:, 3, :], axis=0, keepdims=True)
     sums = sums + lax.ppermute(sums, "space", swap)
     new_iterate, new_residual = make_exit(nz, ny, nx)(
-        times.reshape(4 * total, lanes), sums, u, s
+        times.reshape(4 * total, lanes), sums, u, s, low_plane, high_plane
     )
     return (new_iterate[None], new_residual[None])
 

time: 176 us -> 174 us (0.989)
    pallas_call x5 -> x6, Pallas kernels: 3.2 us -> 4.28 us  [placed(): return call(*args)]
  transfers between devices with their start and end apart: 6 -> 6, of which waited for: 6 -> 5; matrix products, arithmetic and copies ran while one was open for 0% -> 1% of each run, Pallas kernels for 0% -> 0%
where the time goes in v4:
time: 174 us; the launch traced here: 171 us
  blocking collectives  70.2 us (40%)
  starting transfers between devices  63.1 us (36%)
  waiting for transfers between devices  31.7 us (18%)
  Pallas kernels  4.28 us (2%)
    all_to_all x1, starting transfers between devices, on_device(): lax.all_to_all(send.reshape(total, 2, lanes), TM, split_axis=0, concat_ax...  53.3 us
    all_to_all x1, blocking collectives, on_device(): lax.all_to_all(send.reshape(total, 4, lanes), TM, split_axis=0, concat_ax...  49.2 us
    all_to_all x1, waiting for transfers between devices, on_device(): lax.all_to_all(send.reshape(total, 2, lanes), TM, split_axis=0, concat_ax...  23.8 us
    all_to_all x1, blocking collectives, on_device(): lax.all_to_all(spec.reshape(owners, 2 * rows, lanes), ROW, split_axis=0,...  11.5 us
    all_to_all x1, blocking collectives, on_device(): back = lax.all_to_all(back, ROW, split_axis=0, concat_axis=0, tiled=True)  9.48 us
    ppermute x2, waiting for transfers between devices, shifted(): return lax.ppermute(value, 'blocks', pairs)  6.42 us
    pallas_call x6, Pallas kernels, placed(): return call(*args)  4.28 us
    ppermute x2, starting transfers between devices, shifted(): return lax.ppermute(value, 'blocks', pairs)  3.96 us
  transfers between devices with their start and end apart: 6, of which 5 were waited for; matrix products, arithmetic and copies ran while one was open for 1% of the time, Pallas kernels for 0%

profile of v4, /device:TPU:40, one launch (start us, length us, event | category | flops | bytes accessed | tf_op | source)
XLA Modules:
  0.0 171.2 jit_solution(11257555806842960185)
XLA Ops:
  0.6 1.7 %shard_map.77 = (f32[8,16,128]{2,1,0:T(8,128)S(1)}, f32[256,128]{1,0:T(8,128)}) custom-call(f32[8,16,128]{2,1,0:T(8,128)} %bitcast.38, f32[8,16,128]{2,1,0:T(8,128)} %bitcast.48, f32[8,16,128]{2,1,0:T(8,128)} %kappa.1), custom_call_target="tpu_custom_call" | custom-call | tf_op jit(solution)/shard_map/pallas_call | solution.py:94
  2.4 0.0 copy-start.3
  2.4 0.0 copy-start.1
  2.4 53.3 %all-to-all-start = ((f32[128,2,128]{2,1,0:T(2,128)}), f32[128,2,128]{2,1,0:T(2,128)S(1)}, u32[]{:S(2)}, u32[]{:S(2)}) async-start(f32[128,2,128]{2,1,0:T(2,128)} %bitcast.2), calls=%async_computation | async-start | bytes 262144 | tf_op jit(solution)/shard_map/all_to_all | solution.py:284
  55.7 0.0 copy-start
  55.7 0.0 copy-done.3
  55.7 0.1 copy.9
  55.8 0.0 copy-done.1
  55.9 2.0 %collective-permute-start = (f32[36,128]{1,0:T(8,128)S(1)}, f32[36,128]{1,0:T(8,128)S(1)}, u32[]{:S(2)}, u32[]{:S(2)}) collective-permute-start(f32[36,128]{1,0:T(8,128)S(1)} %pad_maximum_fusion), channel_id=1, source_target_pairs={{0,1},{1,0},{2,3},{3,2},{4,5},{5,4},{6,7},{7,6},{8,9},{9,8},{10,11... | collective-permute-start | bytes 55304 | tf_op jit(solution)/shard_map/ppermute | solution.py:292
  57.9 0.7 dynamic-slice_bitcast_fusion
  58.6 0.4 collective-permute-done
  59.0 23.8 %all-to-all-done = f32[128,2,128]{2,1,0:T(2,128)S(1)} async-done(((f32[128,2,128]{2,1,0:T(2,128)}), f32[128,2,128]{2,1,0:T(2,128)S(1)}, u32[]{:S(2)}, u32[]{:S(2)}) %all-to-all-start) | async-done | bytes 131104 | tf_op jit(solution)/shard_map/all_to_all | solution.py:284
  82.8 0.1 broadcast_in_dim.25.lam
  82.9 0.0 copy-done
  82.9 0.5 shard_map.78
  83.3 11.5 %all_to_all.20 = f32[16,16,128]{2,1,0:T(8,128)S(1)} all-to-all(f32[16,16,128]{2,1,0:T(8,128)S(1)} %bitcast.43), channel_id=1, replica_groups=mesh['groups'=2,'blocks'=16,'pair'=2,'tm_1'=4,'space'=2] {'pair','tm_1',..., dimensions={0} | all-to-all | bytes 262144 | tf_op jit(solution)/shard_map/all_to_all | solution.py:312
  94.8 0.1 shard_map.79
  94.9 2.0 %collective-permute-start.3 = (f32[128,128]{1,0:T(8,128)S(1)}, f32[128,128]{1,0:T(8,128)S(1)}, u32[]{:S(2)}, u32[]{:S(2)}) collective-permute-start(f32[128,128]{1,0:T(8,128)S(1)} %get-tuple-element.41), channel_id=1, source_target_pairs={{0,1},{1,0},{2,3},{3,2},{4,5},{5,4},{6,7},{7,6},{8,9},{9,8},{10,11... | collective-permute-start | bytes 196616 | tf_op jit(solution)/shard_map/ppermute | solution.py:327
  96.9 2.7 %collective-permute-start.1 = (f32[6,2,8,128]{3,2,1,0:T(8,128)S(1)}, f32[6,2,8,128]{3,2,1,0:T(8,128)S(1)}, u32[]{:S(2)}, u32[]{:S(2)}) collective-permute-start(f32[6,2,8,128]{3,2,1,0:T(8,128)S(1)} %get-tuple-element.39), channel_id=1, source_target_pairs={{0,16},{16,32},{32,48},{48,64},{64,80},{80,96},{96,112},{112,128},... | collective-permute-start | bytes 147464 | tf_op jit(solution)/shard_map/ppermute | solution.py:323
  99.5 1.3 collective-permute-start.2
  100.8 0.4 collective-permute-done.1.left
  101.3 6.0 %collective-permute-done.2.right = f32[6,2,8,128]{3,2,1,0:T(8,128)S(1)} collective-permute-done((f32[6,2,8,128]{3,2,1,0:T(8,128)S(1)}, f32[6,2,8,128]{3,2,1,0:T(8,128)S(1)}, u32[]{:S(2)}, u32[]{:S(2)}) %collective-permute-start.2) | collective-permute-done | bytes 49184 | tf_op jit(solution)/shard_map/ppermute | solution.py:323
  107.3 0.0 collective-permute-done.3.edge
  107.3 0.0 copy-start.2
  107.3 0.8 shard_map.80
  108.0 9.5 %all_to_all.21 = f32[16,2,8,128]{3,2,1,0:T(8,128)S(1)} all-to-all(f32[16,2,8,128]{3,2,1,0:T(8,128)S(1)} %shard_map.80), channel_id=1, replica_groups=mesh['groups'=2,'blocks'=16,'pair'=2,'tm_1'=4,'space'=2] {'pair','tm_1',..., dimensions={0} | all-to-all | bytes 262144 | tf_op jit(solution)/shard_map/all_to_all | solution.py:330
  117.5 0.0 copy-done.2
  117.5 0.5 shard_map.81
  118.0 49.2 %all_to_all.22 = f32[128,4,128]{2,1,0:T(4,128)S(1)} all-to-all(f32[128,4,128]{2,1,0:T(4,128)S(1)} %bitcast.35), channel_id=1, replica_groups=mesh['groups'=2,'blocks'=16,'pair'=2,'tm_1'=4,'space'=2] {'blocks','pair..., dimensions={0} | all-to-all | bytes 524288 | tf_op jit(solution)/shard_map/all_to_all | solution.py:334
  167.2 0.2 slice_reduce_fusion
  167.4 1.9 %collective-permute-start.4 = (f32[1,128]{1,0:T(1,128)S(1)}, f32[1,128]{1,0:T(1,128)S(1)}, u32[]{:S(2)}, u32[]{:S(2)}) collective-permute-start(f32[1,128]{1,0:T(1,128)S(1)} %bitcast.49), channel_id=1, source_target_pairs={{0,1},{1,0},{2,3},{3,2},{4,5},{5,4},{6,7},{7,6},{8,9},{9,8},{10,11... | collective-permute-start | bytes 1544 | tf_op jit(solution)/shard_map/ppermute | solution.py:338
  169.3 1.1 collective-permute-done.4
  170.4 0.8 shard_map.82
  (12 shorter events, 0.1 us)
Async XLA Ops:
  2.4 53.3 %copy-start.3 = (f32[8,16,128]{2,1,0:T(8,128)S(1)}, f32[8,16,128]{2,1,0:T(8,128)}, u32[]{:S(2)}) copy-start(f32[8,16,128]{2,1,0:T(8,128)} %kappa.1) | copy-start | bytes 196612
  2.4 53.4 %copy-start.1 = (f32[1,8,16,128]{3,2,1,0:T(8,128)S(1)}, f32[1,8,16,128]{3,2,1,0:T(8,128)}, u32[]{:S(2)}) copy-start(f32[1,8,16,128]{3,2,1,0:T(8,128)} %param.6) | copy-start | bytes 196612
  2.4 80.4 %all-to-all-start = ((f32[128,2,128]{2,1,0:T(2,128)}), f32[128,2,128]{2,1,0:T(2,128)S(1)}, u32[]{:S(2)}, u32[]{:S(2)}) async-start(f32[128,2,128]{2,1,0:T(2,128)} %bitcast.2), calls=%async_computation | async-start | bytes 262144 | tf_op jit(solution)/shard_map/all_to_all | solution.py:284
  55.7 27.2 %copy-start = (f32[384,256]{1,0:T(8,128)S(1)}, f32[384,256]{1,0:T(8,128)}, u32[]{:S(2)}) copy-start(f32[384,256]{1,0:T(8,128)} %constant.63.clone.mat) | copy-start | bytes 1179652
  55.9 3.1 %collective-permute-start = (f32[36,128]{1,0:T(8,128)S(1)}, f32[36,128]{1,0:T(8,128)S(1)}, u32[]{:S(2)}, u32[]{:S(2)}) collective-permute-start(f32[36,128]{1,0:T(8,128)S(1)} %pad_maximum_fusion), channel_id=1, source_target_pairs={{0,1},{1,0},{2,3},{3,2},{4,5},{5,4},{6,7},{7,6},{8,9},{9,8},{10,11... | collective-permute-start | bytes 55304 | tf_op jit(solution)/shard_map/ppermute | solution.py:292
  94.9 12.4 %collective-permute-start.3 = (f32[128,128]{1,0:T(8,128)S(1)}, f32[128,128]{1,0:T(8,128)S(1)}, u32[]{:S(2)}, u32[]{:S(2)}) collective-permute-start(f32[128,128]{1,0:T(8,128)S(1)} %get-tuple-element.41), channel_id=1, source_target_pairs={{0,1},{1,0},{2,3},{3,2},{4,5},{5,4},{6,7},{7,6},{8,9},{9,8},{10,11... | collective-permute-start | bytes 196616 | tf_op jit(solution)/shard_map/ppermute | solution.py:327
  96.9 4.4 %collective-permute-start.1 = (f32[6,2,8,128]{3,2,1,0:T(8,128)S(1)}, f32[6,2,8,128]{3,2,1,0:T(8,128)S(1)}, u32[]{:S(2)}, u32[]{:S(2)}) collective-permute-start(f32[6,2,8,128]{3,2,1,0:T(8,128)S(1)} %get-tuple-element.39), channel_id=1, source_target_pairs={{0,16},{16,32},{32,48},{48,64},{64,80},{80,96},{96,112},{112,128},... | collective-permute-start | bytes 147464 | tf_op jit(solution)/shard_map/ppermute | solution.py:323
  99.5 7.7 %collective-permute-start.2 = (f32[6,2,8,128]{3,2,1,0:T(8,128)S(1)}, f32[6,2,8,128]{3,2,1,0:T(8,128)S(1)}, u32[]{:S(2)}, u32[]{:S(2)}) collective-permute-start(f32[6,2,8,128]{3,2,1,0:T(8,128)S(1)} %get-tuple-element.40), channel_id=1, source_target_pairs={{16,0},{32,16},{48,32},{64,48},{80,64},{96,80},{112,96},{128,112},... | collective-permute-start | bytes 147464 | tf_op jit(solution)/shard_map/ppermute | solution.py:323
  107.3 10.2 %copy-start.2 = (f32[256,256]{1,0:T(8,128)S(1)}, f32[256,256]{1,0:T(8,128)}, u32[]{:S(2)}) copy-start(f32[256,256]{1,0:T(8,128)} %constant.64.clone.mat) | copy-start | bytes 786436
  167.4 3.1 %collective-permute-start.4 = (f32[1,128]{1,0:T(1,128)S(1)}, f32[1,128]{1,0:T(1,128)S(1)}, u32[]{:S(2)}, u32[]{:S(2)}) collective-permute-start(f32[1,128]{1,0:T(1,128)S(1)} %bitcast.49), channel_id=1, source_target_pairs={{0,1},{1,0},{2,3},{3,2},{4,5},{5,4},{6,7},{7,6},{8,9},{9,8},{10,11... | collective-permute-start | bytes 1544 | tf_op jit(solution)/shard_map/ppermute | solution.py:338

commit v5 on v4

--- a/solution.py
+++ b/solution.py
@@ -58,21 +58,21 @@
                 lams[q, 0, :, j] = lam[k].real
                 lams[q, 1, :, j] = lam[k].imag
     fwd = fwd.reshape(total, total)
-    first_mat = np.zeros((3 * total, total, 2))
-    first_mat[:total, :, 0] = hist
-    spectra = first_mat[total:].reshape(owners, 2, 2 * here, total, 2)
+    first_mat = np.zeros((2 * total, total, 2))
+    spectra = first_mat.reshape(owners, 2, 2 * here, total, 2)
     spectra[:, 0, :, :, 0] = (-fwd @ hist).reshape(owners, 2 * here, total)
     spectra[:, 0, :, :, 1] = fwd.reshape(owners, 2 * here, total)
     spectra[:, 1, :, :, 0] = fwd.reshape(owners, 2 * here, total)
-    flat = inv.reshape(total, total)
-    second_mat = np.zeros((2, total, owners, 2, 2 * here))
-    second_mat[0, :, :, 0] = flat.reshape(total, owners, 2 * here)
-    second_mat[1, :, :, 0] = (hist @ flat).reshape(total, owners, 2 * here)
-    second_mat[1, :, :, 1] = flat.reshape(total, owners, 2 * here)
+    flat = inv.reshape(total, owners, 2 * here)
+    second_mat = np.zeros((3, total, owners, 3, 2 * here))
+    second_mat[0, :, :, 0] = flat
+    second_mat[1, :, :, 0] = (hist @ inv.reshape(total, total)).reshape(flat.shape)
+    second_mat[1, :, :, 1] = flat
+    second_mat[2, :, :, 2] = flat
     f32 = np.float32
     return (
-        first_mat.reshape(3 * total, 2 * total).astype(f32),
-        second_mat.reshape(2 * total, 2 * total).astype(f32),
+        first_mat.reshape(2 * total, 2 * total).astype(f32),
+        second_mat.reshape(3 * total, 3 * total).astype(f32),
         lams.reshape(owners, 2, 2 * here).astype(f32),
     )
 
@@ -103,7 +103,7 @@
 def make_entry(nz, ny, nx):
     lanes = nz * ny
 
-    def kernel(u, f, kappa, s, out):
+    def kernel(u, f, kappa, out, s):
         row, lane = iota((ny, nx), 0), iota((ny, nx), 1)
         for z in range(nz):
             v = u[z]
@@ -119,20 +119,17 @@
         out[pl.ds(0, nx, stride=2), :] = u[...].reshape(lanes, nx).T
         out[pl.ds(1, nx, stride=2), :] = s[...].reshape(lanes, nx).T
 
-    return local_call(kernel, [(nz, ny, nx), (2 * nx, lanes)], 3, keep_in=False)
-
-
-def make_forward(total, lanes, ny):
-    def kernel(mat, cells, masks, hist, spec, edge):
-        out = jnp.dot(mat[...], cells[...], precision=HIGH, preferred_element_type=jnp.float32)
-        hist[...] = out[:total]
-        spec[...] = out[total:]
-        u = cells[pl.ds(0, total, stride=2), :]
-        edge[...] = masks[0:1, :] * pltpu.roll(u, ny, 1) + masks[1:2, :] * pltpu.roll(
-            u, lanes - ny, 1
+    scratch = [pltpu.VMEM((nz, ny, nx), jnp.float32)]
+    return local_call(kernel, [(2 * nx, lanes)], 3, scratch, keep_in=False)
+
+
+def make_forward(total, lanes):
+    def kernel(mat, cells, spec):
+        spec[...] = jnp.dot(
+            mat[...], cells[...], precision=HIGH, preferred_element_type=jnp.float32
         )
 
-    return local_call(kernel, [(total, lanes), (2 * total, lanes), (total, lanes)], 3)
+    return local_call(kernel, [(2 * total, lanes)], 2)
 
 
 def make_border(own, depth, rows, lanes, ny):
@@ -156,41 +153,42 @@
 
 
 def make_backward(total, lanes):
-    def kernel(mat, back, hist, cells, edge, kap, out):
-        both = jnp.dot(mat[...], back[...], precision=HIGH, preferred_element_type=jnp.float32)
-        image = both[total:]
-        residual = cells[pl.ds(1, total, stride=2), :] - hist[...] + kap[...] * edge[...]
-        ri = jnp.sum(residual * image, axis=0, keepdims=True)
+    def kernel(mat, back, out):
+        fields = jnp.concatenate(
+            [back[:, 3 * h : 3 * h + 3].reshape(3 * total, lanes) for h in range(2)], axis=1
+        )
+        every = jnp.dot(mat[...], fields, precision=HIGH, preferred_element_type=jnp.float32)
+        image = every[total : 2 * total]
+        ri = jnp.sum(every[2 * total :] * image, axis=0, keepdims=True)
         ii = jnp.sum(image * image, axis=0, keepdims=True)
+        ri = ri[:, :lanes] + ri[:, lanes:]
+        ii = ii[:, :lanes] + ii[:, lanes:]
         low = iota((1, lanes), 1) < lanes // 2
         sums = jnp.where(low, ri + pltpu.roll(ri, lanes // 2, 1), ii + pltpu.roll(ii, lanes // 2, 1))
-        out[pl.ds(0, total, stride=4), :] = both[:total]
-        out[pl.ds(1, total, stride=4), :] = image
-        out[pl.ds(2, total, stride=4), :] = hist[...]
+        for k in range(3):
+            out[pl.ds(k, total, stride=4), :] = every[k * total : (k + 1) * total, :lanes]
         out[pl.ds(3, total, stride=4), :] = jnp.broadcast_to(sums, (total, lanes))
 
-    return local_call(kernel, [(4 * total, lanes)], 6)
+    return local_call(kernel, [(4 * total, lanes)], 2)
 
 
 def make_exit(nz, ny, nx):
     lanes = nz * ny
 
-    def kernel(times, sums, u, s, low_plane, high_plane, new_u, new_r):
+    def kernel(times, u, new_u, new_r):
         low = iota((1, lanes), 1) < lanes // 2
-        ri = jnp.sum(jnp.where(low, sums[...], 0.0), axis=1, keepdims=True)
-        ii = jnp.sum(jnp.where(low, 0.0, sums[...]), axis=1, keepdims=True)
+        row = jnp.sum(times[pl.ds(3, nx, stride=4), :], axis=0, keepdims=True)
+        ri = jnp.sum(jnp.where(low, row, 0.0), axis=1, keepdims=True)
+        ii = jnp.sum(jnp.where(low, 0.0, row), axis=1, keepdims=True)
         step = (ri / ii).reshape(1, 1, 1)
 
         def slab(k):
             return times[pl.ds(k, nx, stride=4), :].T.reshape(nz, ny, nx)
 
         new_u[...] = u[...] + step * slab(0)
-        plane = s[...] - slab(2) - step * slab(1)
-        new_r[...] = plane
-        new_r[0] = plane[0] + low_plane[...]
-        new_r[nz - 1] = plane[nz - 1] + high_plane[...]
-
-    return local_call(kernel, [(nz, ny, nx)] * 2, 6, keep_out=False)
+        new_r[...] = slab(2) - step * slab(1)
+
+    return local_call(kernel, [(nz, ny, nx)] * 2, 2, keep_out=False)
 
 
 def make_sweeps(own, depth, rows, lanes, ny):
@@ -255,12 +253,15 @@
             for h in range(2):
                 sol = now[c, h]
                 k = jnp.broadcast_to(kap[2 * c + h : 2 * c + h + 1, :], shape)
-                row = 2 * (c - depth) + h
-                out[row, 0] = sol
-                out[row, 1] = k * (6.0 * sol - near[h])
+                stiff = k * (6.0 * sol - near[h])
+                for core in range(2):
+                    row, at = 2 * (c - depth) + core, 0 if core == h else 3
+                    out[row, at] = sol
+                    out[row, at + 1] = stiff
+                    out[row, at + 2] = mid[c - depth, h]
 
     field = pltpu.VMEM((cols, 2, rows, lanes), jnp.float32)
-    return local_call(kernel, [(2 * own, 2, rows, lanes)], 5, [field] * 5)
+    return local_call(kernel, [(2 * own, 6, rows, lanes)], 5, [field] * 5)
 
 
 def on_device(iterate, source, diffusivity):
@@ -279,44 +280,29 @@
     swap = [(0, 1), (1, 0)]
 
     u, f = iterate[0], source[0]
-    s, send = make_entry(nz, ny, nx)(u, f, diffusivity)
-    send, u, diffusivity = lax.optimization_barrier((send, u, diffusivity))
+    (send,) = make_entry(nz, ny, nx)(u, f, diffusivity)
+    send, diffusivity = lax.optimization_barrier((send, diffusivity))
     cells = lax.all_to_all(
         send.reshape(total, 2, lanes), TM, split_axis=0, concat_axis=0, tiled=True
     ).reshape(2 * total, lanes)
 
     kap = jnp.pad(diffusivity.reshape(lanes, nx).T, ((depth, depth), (0, 0)))
     kap = lax.dynamic_slice_in_dim(kap, block * own, own + 2 * depth, axis=0)
-    my_kap = lax.dynamic_slice_in_dim(kap, depth + lax.axis_index(TM[1:]), 1, axis=0)
-    edge = jnp.where(core == 0, u[nz - 1], u[0])
-    got = lax.ppermute(jnp.concatenate([edge, kap], axis=0), "space", swap)
-    got_edge, kap_other = got[:ny], got[ny:]
+    kap_other = lax.ppermute(kap, "space", swap)
     kap = jnp.where(
         core == 0, jnp.stack([kap, kap_other], axis=1), jnp.stack([kap_other, kap], axis=1)
     ).reshape(-1, lanes)
-    low_plane = jnp.where(core == 0, 0.0, diffusivity[0] * got_edge)
-    high_plane = jnp.where(core == 0, diffusivity[nz - 1] * got_edge, 0.0)
-    lane = jnp.arange(lanes, dtype=jnp.int32)
-    masks = jnp.where(
-        core == 0,
-        jnp.stack([lane < ny, lane < 0]),
-        jnp.stack([lane < 0, lane >= lanes - ny]),
-    ).astype(jnp.float32)
     lam = lax.dynamic_index_in_dim(jnp.asarray(lams), lax.axis_index(ROW), axis=0, keepdims=False)
     lam = jnp.broadcast_to(lam[:, :, None], (2, rows, lanes))
-    cells, kap, my_kap, low_plane, high_plane, masks, lam = lax.optimization_barrier(
-        (cells, kap, my_kap, low_plane, high_plane, masks, lam)
-    )
-
-    hist_u, spec, edge_u = make_forward(total, lanes, ny)(first_mat, cells, masks)
+    cells, kap, lam = lax.optimization_barrier((cells, kap, lam))
+
+    (spec,) = make_forward(total, lanes)(first_mat, cells)
     spec = lax.all_to_all(
         spec.reshape(owners, 2 * rows, lanes), ROW, split_axis=0, concat_axis=0, tiled=True
     )
     spec, to_right, to_left = make_border(own, depth, rows, lanes, ny)(
         spec.reshape(own, cores, 2 * rows, lanes), kap
     )
-
-    to_right, to_left, edge_u = lax.optimization_barrier((to_right, to_left, edge_u))
 
     def shifted(value, offset):
         pairs = [(i, i + offset) for i in range(blocks) if 0 <= i + offset < blocks]
@@ -324,21 +310,13 @@
 
     left = shifted(to_right, 1)
     right = shifted(to_left, -1)
-    edge_u = lax.ppermute(edge_u, "space", swap)
-    left, right, edge_u = lax.optimization_barrier((left, right, edge_u))
     (back,) = make_sweeps(own, depth, rows, lanes, ny)(left, spec, right, kap, lam)
     back = lax.all_to_all(back, ROW, split_axis=0, concat_axis=0, tiled=True)
-    (send,) = make_backward(total, lanes)(
-        second_mat, back.reshape(2 * total, lanes), hist_u, cells, edge_u, my_kap
-    )
+    (send,) = make_backward(total, lanes)(second_mat, back)
     times = lax.all_to_all(
         send.reshape(total, 4, lanes), TM, split_axis=0, concat_axis=0, tiled=True
     )
-    sums = jnp.sum(times[:, 3, :], axis=0, keepdims=True)
-    sums = sums + lax.ppermute(sums, "space", swap)
-    new_iterate, new_residual = make_exit(nz, ny, nx)(
-        times.reshape(4 * total, lanes), sums, u, s, low_plane, high_plane
-    )
+    new_iterate, new_residual = make_exit(nz, ny, nx)(times.reshape(4 * total, lanes), u)
     return (new_iterate[None], new_residual[None])
 
 

time: 174 us -> 171 us (0.983)
  starting transfers between devices: 63.1 us -> 59.3 us
  blocking collectives: 70.2 us -> 73.3 us
    ppermute x3 -> x1, starting transfers between devices: 5.84 us -> 1.95 us  [on_device(): kap_other = lax.ppermute(kap, 'space', swap)]
    all_to_all x1, blocking collectives: 9.48 us -> 12.2 us  [on_device(): back = lax.all_to_all(back, ROW, split_axis=0, concat_axis=0, tiled=True)]
  transfers between devices with their start and end apart: 6 -> 4, of which waited for: 5 -> 4; matrix products, arithmetic and copies ran while one was open for 1% -> 1% of each run, Pallas kernels for 0% -> 0%
where the time goes in v5:
time: 171 us; the launch traced here: 169 us
  blocking collectives  73.3 us (43%)
  starting transfers between devices  59.3 us (35%)
  waiting for transfers between devices  30.2 us (18%)
  Pallas kernels  4.64 us (3%)
    all_to_all x1, starting transfers between devices, on_device(): lax.all_to_all(send.reshape(total, 2, lanes), TM, split_axis=0, concat_ax...  53.3 us
    all_to_all x1, blocking collectives, on_device(): lax.all_to_all(send.reshape(total, 4, lanes), TM, split_axis=0, concat_ax...  49.4 us
    all_to_all x1, waiting for transfers between devices, on_device(): lax.all_to_all(send.reshape(total, 2, lanes), TM, split_axis=0, concat_ax...  23.6 us
    all_to_all x1, blocking collectives, on_device(): back = lax.all_to_all(back, ROW, split_axis=0, concat_axis=0, tiled=True)  12.2 us
    all_to_all x1, blocking collectives, on_device(): lax.all_to_all(spec.reshape(owners, 2 * rows, lanes), ROW, split_axis=0,...  11.7 us
    ppermute x2, waiting for transfers between devices, shifted(): return lax.ppermute(value, 'blocks', pairs)  6.12 us
    pallas_call x6, Pallas kernels, placed(): return call(*args)  4.64 us
    ppermute x2, starting transfers between devices, shifted(): return lax.ppermute(value, 'blocks', pairs)  4 us
  transfers between devices with their start and end apart: 4, of which 4 were waited for; matrix products, arithmetic and copies ran while one was open for 1% of the time, Pallas kernels for 0%

profile of v5, /device:TPU:40, one launch (start us, length us, event | category | flops | bytes accessed | tf_op | source)
XLA Modules:
  0.0 169.1 jit_solution(13849174489418694629)
XLA Ops:
  0.6 0.0 copy-start.3
  0.6 1.8 %shard_map.77 = f32[256,128]{1,0:T(8,128)} custom-call(f32[8,16,128]{2,1,0:T(8,128)} %bitcast.20, f32[8,16,128]{2,1,0:T(8,128)} %bitcast.26, f32[8,16,128]{2,1,0:T(8,128)} %kappa.1), custom_call_target="tpu_custom_call" | custom-call | tf_op jit(solution)/shard_map/pallas_call | solution.py:94
  2.4 0.0 copy-start.2
  2.4 53.3 %all-to-all-start = ((f32[128,2,128]{2,1,0:T(2,128)}), f32[128,2,128]{2,1,0:T(2,128)S(1)}, u32[]{:S(2)}, u32[]{:S(2)}) async-start(f32[128,2,128]{2,1,0:T(2,128)} %bitcast.2), calls=%async_computation | async-start | bytes 262144 | tf_op jit(solution)/shard_map/all_to_all | solution.py:285
  55.7 0.0 copy-done.3
  55.7 0.1 copy.8
  55.8 2.0 %collective-permute-start = (f32[20,128]{1,0:T(8,128)S(1)}, f32[20,128]{1,0:T(8,128)S(1)}, u32[]{:S(2)}, u32[]{:S(2)}) collective-permute-start(f32[20,128]{1,0:T(8,128)S(1)} %pad_dynamic-slice_fusion), channel_id=1, source_target_pairs={{0,1},{1,0},{2,3},{3,2},{4,5},{5,4},{6,7},{7,6},{8,9},{9,8},{10,11... | collective-permute-start | bytes 30728 | tf_op jit(solution)/shard_map/ppermute | solution.py:291
  57.8 0.7 dynamic-slice_bitcast_fusion
  58.5 0.4 collective-permute-done
  59.0 23.6 %all-to-all-done = f32[128,2,128]{2,1,0:T(2,128)S(1)} async-done(((f32[128,2,128]{2,1,0:T(2,128)}), f32[128,2,128]{2,1,0:T(2,128)S(1)}, u32[]{:S(2)}, u32[]{:S(2)}) %all-to-all-start) | async-done | bytes 131104 | tf_op jit(solution)/shard_map/all_to_all | solution.py:285
  82.6 0.1 broadcast_in_dim.15.lam
  82.7 0.0 copy-done.2
  82.7 0.4 shard_map.78
  83.1 11.7 %all_to_all.20 = f32[16,16,128]{2,1,0:T(8,128)S(1)} all-to-all(f32[16,16,128]{2,1,0:T(8,128)S(1)} %bitcast.19), channel_id=1, replica_groups=mesh['groups'=2,'blocks'=16,'pair'=2,'tm_1'=4,'space'=2] {'pair','tm_1',..., dimensions={0} | all-to-all | bytes 262144 | tf_op jit(solution)/shard_map/all_to_all | solution.py:300
  94.8 0.1 shard_map.79
  94.8 2.7 %collective-permute-start.1 = (f32[6,2,8,128]{3,2,1,0:T(8,128)S(1)}, f32[6,2,8,128]{3,2,1,0:T(8,128)S(1)}, u32[]{:S(2)}, u32[]{:S(2)}) collective-permute-start(f32[6,2,8,128]{3,2,1,0:T(8,128)S(1)} %get-tuple-element.16), channel_id=1, source_target_pairs={{0,16},{16,32},{32,48},{48,64},{64,80},{80,96},{96,112},{112,128},... | collective-permute-start | bytes 147464 | tf_op jit(solution)/shard_map/ppermute | solution.py:309
  97.5 1.3 collective-permute-start.2
  98.9 0.4 collective-permute-done.1.left
  99.3 5.7 %collective-permute-done.2.right = f32[6,2,8,128]{3,2,1,0:T(8,128)S(1)} collective-permute-done((f32[6,2,8,128]{3,2,1,0:T(8,128)S(1)}, f32[6,2,8,128]{3,2,1,0:T(8,128)S(1)}, u32[]{:S(2)}, u32[]{:S(2)}) %collective-permute-start.2) | collective-permute-done | bytes 49184 | tf_op jit(solution)/shard_map/ppermute | solution.py:309
  105.0 0.0 copy-start
  105.0 0.8 shard_map.80
  105.7 12.2 %all_to_all.21.back = f32[16,6,8,128]{3,2,1,0:T(8,128)S(1)} all-to-all(f32[16,6,8,128]{3,2,1,0:T(8,128)S(1)} %shard_map.80), channel_id=1, replica_groups=mesh['groups'=2,'blocks'=16,'pair'=2,'tm_1'=4,'space'=2] {'pair','tm_1',..., dimensions={0} | all-to-all | bytes 786432 | tf_op jit(solution)/shard_map/all_to_all | solution.py:314
  118.0 0.0 copy-done
  118.0 0.9 shard_map.81
  118.9 0.0 copy-start.1
  118.9 49.4 %all_to_all.22 = f32[128,4,128]{2,1,0:T(4,128)S(1)} all-to-all(f32[128,4,128]{2,1,0:T(4,128)S(1)} %bitcast.15), channel_id=1, replica_groups=mesh['groups'=2,'blocks'=16,'pair'=2,'tm_1'=4,'space'=2] {'blocks','pair..., dimensions={0} | all-to-all | bytes 524288 | tf_op jit(solution)/shard_map/all_to_all | solution.py:316
  168.3 0.0 copy-done.1
  168.3 0.8 shard_map.82
  (4 shorter events, 0.1 us)
Async XLA Ops:
  0.6 55.1 %copy-start.3 = (f32[8,16,128]{2,1,0:T(8,128)S(1)}, f32[8,16,128]{2,1,0:T(8,128)}, u32[]{:S(2)}) copy-start(f32[8,16,128]{2,1,0:T(8,128)} %kappa.1) | copy-start | bytes 196612
  2.4 80.3 %copy-start.2 = (f32[256,256]{1,0:T(8,128)S(1)}, f32[256,256]{1,0:T(8,128)}, u32[]{:S(2)}) copy-start(f32[256,256]{1,0:T(8,128)} %constant.38.clone.mat) | copy-start | bytes 786436
  2.4 80.2 %all-to-all-start = ((f32[128,2,128]{2,1,0:T(2,128)}), f32[128,2,128]{2,1,0:T(2,128)S(1)}, u32[]{:S(2)}, u32[]{:S(2)}) async-start(f32[128,2,128]{2,1,0:T(2,128)} %bitcast.2), calls=%async_computation | async-start | bytes 262144 | tf_op jit(solution)/shard_map/all_to_all | solution.py:285
  55.8 3.1 %collective-permute-start = (f32[20,128]{1,0:T(8,128)S(1)}, f32[20,128]{1,0:T(8,128)S(1)}, u32[]{:S(2)}, u32[]{:S(2)}) collective-permute-start(f32[20,128]{1,0:T(8,128)S(1)} %pad_dynamic-slice_fusion), channel_id=1, source_target_pairs={{0,1},{1,0},{2,3},{3,2},{4,5},{5,4},{6,7},{7,6},{8,9},{9,8},{10,11... | collective-permute-start | bytes 30728 | tf_op jit(solution)/shard_map/ppermute | solution.py:291
  94.8 4.4 %collective-permute-start.1 = (f32[6,2,8,128]{3,2,1,0:T(8,128)S(1)}, f32[6,2,8,128]{3,2,1,0:T(8,128)S(1)}, u32[]{:S(2)}, u32[]{:S(2)}) collective-permute-start(f32[6,2,8,128]{3,2,1,0:T(8,128)S(1)} %get-tuple-element.16), channel_id=1, source_target_pairs={{0,16},{16,32},{32,48},{48,64},{64,80},{80,96},{96,112},{112,128},... | collective-permute-start | bytes 147464 | tf_op jit(solution)/shard_map/ppermute | solution.py:309
  97.5 7.4 %collective-permute-start.2 = (f32[6,2,8,128]{3,2,1,0:T(8,128)S(1)}, f32[6,2,8,128]{3,2,1,0:T(8,128)S(1)}, u32[]{:S(2)}, u32[]{:S(2)}) collective-permute-start(f32[6,2,8,128]{3,2,1,0:T(8,128)S(1)} %get-tuple-element.18), channel_id=1, source_target_pairs={{16,0},{32,16},{48,32},{64,48},{80,64},{96,80},{112,96},{128,112},... | collective-permute-start | bytes 147464 | tf_op jit(solution)/shard_map/ppermute | solution.py:309
  105.0 13.0 %copy-start = (f32[384,384]{1,0:T(8,128)S(1)}, f32[384,384]{1,0:T(8,128)}, u32[]{:S(2)}) copy-start(f32[384,384]{1,0:T(8,128)} %constant.39.clone.mat) | copy-start | bytes 1769476
  118.9 49.4 %copy-start.1 = (f32[1,8,16,128]{3,2,1,0:T(8,128)S(1)}, f32[1,8,16,128]{3,2,1,0:T(8,128)}, u32[]{:S(2)}) copy-start(f32[1,8,16,128]{3,2,1,0:T(8,128)} %param.6) | copy-start | bytes 196612

commit v6 on v5

--- a/solution.py
+++ b/solution.py
@@ -28,7 +28,7 @@
     return d / (step_length**frac_order * gamma_factor)
 
 
-def tables(total, owners):
+def tables(total, owners, own):
     half = total // 2
     here = half // owners
     n = np.arange(total)
@@ -69,6 +69,7 @@
     second_mat[1, :, :, 0] = (hist @ inv.reshape(total, total)).reshape(flat.shape)
     second_mat[1, :, :, 1] = flat
     second_mat[2, :, :, 2] = flat
+    second_mat = second_mat.reshape(3, total // own, own, 3 * total).transpose(2, 0, 1, 3)
     f32 = np.float32
     return (
         first_mat.reshape(2 * total, 2 * total).astype(f32),
@@ -152,38 +153,61 @@
     return local_call(kernel, shapes, 2)
 
 
-def make_backward(total, lanes):
+def make_backward(total, own, lanes):
+    blocks = total // own
+    pad = 3 * blocks + 8
+
     def kernel(mat, back, out):
         fields = jnp.concatenate(
             [back[:, 3 * h : 3 * h + 3].reshape(3 * total, lanes) for h in range(2)], axis=1
         )
         every = jnp.dot(mat[...], fields, precision=HIGH, preferred_element_type=jnp.float32)
-        image = every[total : 2 * total]
-        ri = jnp.sum(every[2 * total :] * image, axis=0, keepdims=True)
-        ii = jnp.sum(image * image, axis=0, keepdims=True)
-        ri = ri[:, :lanes] + ri[:, lanes:]
-        ii = ii[:, :lanes] + ii[:, lanes:]
+        ri = ii = 0.0
+        for c in range(own):
+            at = 3 * blocks * c
+            image = every[at + blocks : at + 2 * blocks]
+            ri = ri + every[at + 2 * blocks : at + 3 * blocks] * image
+            ii = ii + image * image
+            out[pad * c : pad * c + 3 * blocks, :] = every[at : at + 3 * blocks, :lanes]
+        ri = jnp.sum(ri[:, :lanes] + ri[:, lanes:], axis=0, keepdims=True)
+        ii = jnp.sum(ii[:, :lanes] + ii[:, lanes:], axis=0, keepdims=True)
         low = iota((1, lanes), 1) < lanes // 2
         sums = jnp.where(low, ri + pltpu.roll(ri, lanes // 2, 1), ii + pltpu.roll(ii, lanes // 2, 1))
-        for k in range(3):
-            out[pl.ds(k, total, stride=4), :] = every[k * total : (k + 1) * total, :lanes]
-        out[pl.ds(3, total, stride=4), :] = jnp.broadcast_to(sums, (total, lanes))
-
-    return local_call(kernel, [(4 * total, lanes)], 2)
-
-
-def make_exit(nz, ny, nx):
+        for c in range(own):
+            out[pad * c + 3 * blocks : pad * (c + 1), :] = jnp.broadcast_to(sums, (8, lanes))
+
+    return local_call(kernel, [(own * pad, lanes)], 2)
+
+
+def make_turn(blocks, own, lanes):
+    pad, rows = 3 * blocks + 8, 3 * own + 1
+
+    def kernel(near, out):
+        sums = 0.0
+        for c in range(own):
+            for k in range(3):
+                at = pad * c + blocks * k
+                out[pl.ds(own * k + c, blocks, stride=rows), :] = near[at : at + blocks, :]
+            sums = sums + near[pad * c + 3 * blocks : pad * c + 3 * blocks + 1, :]
+        out[pl.ds(3 * own, blocks, stride=rows), :] = jnp.broadcast_to(sums, (blocks, lanes))
+
+    return local_call(kernel, [(blocks * rows, lanes)], 1)
+
+
+def make_exit(nz, ny, nx, blocks, own):
     lanes = nz * ny
+    rows = 3 * own + 1
 
     def kernel(times, u, new_u, new_r):
         low = iota((1, lanes), 1) < lanes // 2
-        row = jnp.sum(times[pl.ds(3, nx, stride=4), :], axis=0, keepdims=True)
+        row = jnp.sum(times[pl.ds(3 * own, blocks, stride=rows), :], axis=0, keepdims=True)
         ri = jnp.sum(jnp.where(low, row, 0.0), axis=1, keepdims=True)
         ii = jnp.sum(jnp.where(low, 0.0, row), axis=1, keepdims=True)
         step = (ri / ii).reshape(1, 1, 1)
 
         def slab(k):
-            return times[pl.ds(k, nx, stride=4), :].T.reshape(nz, ny, nx)
+            parts = [times[rows * b + own * k : rows * b + own * (k + 1), :] for b in range(blocks)]
+            return jnp.concatenate(parts, axis=0).T.reshape(nz, ny, nx)
 
         new_u[...] = u[...] + step * slab(0)
         new_r[...] = slab(2) - step * slab(1)
@@ -274,7 +298,7 @@
     owners = own * cores
     rows = total // owners
     depth = SWEEPS
-    first_mat, second_mat, lams = tables(total, owners)
+    first_mat, second_mat, lams = tables(total, owners, own)
     core = lax.axis_index("space")
     block = lax.axis_index("blocks")
     swap = [(0, 1), (1, 0)]
@@ -312,11 +336,15 @@
     right = shifted(to_left, -1)
     (back,) = make_sweeps(own, depth, rows, lanes, ny)(left, spec, right, kap, lam)
     back = lax.all_to_all(back, ROW, split_axis=0, concat_axis=0, tiled=True)
-    (send,) = make_backward(total, lanes)(second_mat, back)
+    (near,) = make_backward(total, own, lanes)(second_mat, back)
+    near = lax.all_to_all(
+        near.reshape(own, -1, lanes), TM[1:], split_axis=0, concat_axis=0, tiled=True
+    )
+    (far,) = make_turn(blocks, own, lanes)(near.reshape(-1, lanes))
     times = lax.all_to_all(
-        send.reshape(total, 4, lanes), TM, split_axis=0, concat_axis=0, tiled=True
-    )
-    new_iterate, new_residual = make_exit(nz, ny, nx)(times.reshape(4 * total, lanes), u)
+        far.reshape(blocks, 3 * own + 1, 1, lanes), "blocks", split_axis=0, concat_axis=0, tiled=True
+    )
+    new_iterate, new_residual = make_exit(nz, ny, nx, blocks, own)(times.reshape(-1, lanes), u)
     return (new_iterate[None], new_residual[None])
 
 

time: 171 us -> 166 us (0.971)
  blocking collectives: 73.3 us -> 69.8 us
    all_to_all x1 -> x2, blocking collectives: 49.4 us -> 46 us  [the longest x1 36.4 us: on_device(): lax.all_to_all(far.reshape(blocks, 3 * own + 1, 1, lanes), 'blocks', spli...]
    pallas_call x6 -> x7, Pallas kernels: 4.64 us -> 4.64 us  [placed(): return call(*args)]
where the time goes in v6:
time: 166 us
  blocking collectives  69.8 us (42%)
  starting transfers between devices  59.3 us (36%)
  waiting for transfers between devices  30.2 us (18%)
  Pallas kernels  4.64 us (3%)
    all_to_all x1, starting transfers between devices, on_device(): lax.all_to_all(send.reshape(total, 2, lanes), TM, split_axis=0, concat_ax...  53.3 us
    all_to_all x1, blocking collectives, on_device(): lax.all_to_all(far.reshape(blocks, 3 * own + 1, 1, lanes), 'blocks', spli...  36.4 us
    all_to_all x1, waiting for transfers between devices, on_device(): lax.all_to_all(send.reshape(total, 2, lanes), TM, split_axis=0, concat_ax...  23.6 us
    all_to_all x1, blocking collectives, on_device(): back = lax.all_to_all(back, ROW, split_axis=0, concat_axis=0, tiled=True)  12.2 us
    all_to_all x1, blocking collectives, on_device(): lax.all_to_all(spec.reshape(owners, 2 * rows, lanes), ROW, split_axis=0,...  11.7 us
    all_to_all x1, blocking collectives, on_device(): lax.all_to_all(near.reshape(own, -1, lanes), TM[1:], split_axis=0, concat...  9.58 us
    ppermute x2, waiting for transfers between devices, shifted(): return lax.ppermute(value, 'blocks', pairs)  6.12 us
    pallas_call x7, Pallas kernels, placed(): return call(*args)  4.64 us
  transfers between devices with their start and end apart: 4, of which 4 were waited for; matrix products, arithmetic and copies ran while one was open for 1% of the time, Pallas kernels for 0%

profile of v6, /device:TPU:40, one launch (start us, length us, event | category | flops | bytes accessed | tf_op | source)
XLA Modules:
  0.0 165.6 jit_solution(10063078132726393443)
XLA Ops:
  0.6 0.0 copy-start.3
  0.6 1.8 %shard_map.77 = f32[256,128]{1,0:T(8,128)} custom-call(f32[8,16,128]{2,1,0:T(8,128)} %bitcast.24, f32[8,16,128]{2,1,0:T(8,128)} %bitcast.30, f32[8,16,128]{2,1,0:T(8,128)} %kappa.1), custom_call_target="tpu_custom_call" | custom-call | tf_op jit(solution)/shard_map/pallas_call | solution.py:95
  2.4 0.0 copy-start.1
  2.4 53.3 %all-to-all-start = ((f32[128,2,128]{2,1,0:T(2,128)}), f32[128,2,128]{2,1,0:T(2,128)S(1)}, u32[]{:S(2)}, u32[]{:S(2)}) async-start(f32[128,2,128]{2,1,0:T(2,128)} %bitcast.2), calls=%async_computation | async-start | bytes 262144 | tf_op jit(solution)/shard_map/all_to_all | solution.py:309
  55.7 0.0 copy-done.3
  55.7 0.1 copy.10
  55.8 2.0 %collective-permute-start = (f32[20,128]{1,0:T(8,128)S(1)}, f32[20,128]{1,0:T(8,128)S(1)}, u32[]{:S(2)}, u32[]{:S(2)}) collective-permute-start(f32[20,128]{1,0:T(8,128)S(1)} %pad_dynamic-slice_fusion), channel_id=1, source_target_pairs={{0,1},{1,0},{2,3},{3,2},{4,5},{5,4},{6,7},{7,6},{8,9},{9,8},{10,11... | collective-permute-start | bytes 30728 | tf_op jit(solution)/shard_map/ppermute | solution.py:315
  57.8 0.7 dynamic-slice_bitcast_fusion
  58.5 0.4 collective-permute-done
  59.0 23.6 %all-to-all-done = f32[128,2,128]{2,1,0:T(2,128)S(1)} async-done(((f32[128,2,128]{2,1,0:T(2,128)}), f32[128,2,128]{2,1,0:T(2,128)S(1)}, u32[]{:S(2)}, u32[]{:S(2)}) %all-to-all-start) | async-done | bytes 131104 | tf_op jit(solution)/shard_map/all_to_all | solution.py:309
  82.6 0.1 broadcast_in_dim.15.lam
  82.7 0.0 copy-done.1
  82.7 0.4 shard_map.78
  83.1 11.7 %all_to_all.25 = f32[16,16,128]{2,1,0:T(8,128)S(1)} all-to-all(f32[16,16,128]{2,1,0:T(8,128)S(1)} %bitcast.23), channel_id=1, replica_groups=mesh['groups'=2,'blocks'=16,'pair'=2,'tm_1'=4,'space'=2] {'pair','tm_1',..., dimensions={0} | all-to-all | bytes 262144 | tf_op jit(solution)/shard_map/all_to_all | solution.py:324
  94.8 0.1 shard_map.79
  94.8 2.7 %collective-permute-start.1 = (f32[6,2,8,128]{3,2,1,0:T(8,128)S(1)}, f32[6,2,8,128]{3,2,1,0:T(8,128)S(1)}, u32[]{:S(2)}, u32[]{:S(2)}) collective-permute-start(f32[6,2,8,128]{3,2,1,0:T(8,128)S(1)} %get-tuple-element.16), channel_id=1, source_target_pairs={{0,16},{16,32},{32,48},{48,64},{64,80},{80,96},{96,112},{112,128},... | collective-permute-start | bytes 147464 | tf_op jit(solution)/shard_map/ppermute | solution.py:333
  97.5 1.3 collective-permute-start.2
  98.9 0.4 collective-permute-done.1.left
  99.3 5.7 %collective-permute-done.2.right = f32[6,2,8,128]{3,2,1,0:T(8,128)S(1)} collective-permute-done((f32[6,2,8,128]{3,2,1,0:T(8,128)S(1)}, f32[6,2,8,128]{3,2,1,0:T(8,128)S(1)}, u32[]{:S(2)}, u32[]{:S(2)}) %collective-permute-start.2) | collective-permute-done | bytes 49184 | tf_op jit(solution)/shard_map/ppermute | solution.py:333
  105.0 0.0 copy-start
  105.0 0.8 shard_map.80
  105.7 12.2 %all_to_all.26.back = f32[16,6,8,128]{3,2,1,0:T(8,128)S(1)} all-to-all(f32[16,6,8,128]{3,2,1,0:T(8,128)S(1)} %shard_map.80), channel_id=1, replica_groups=mesh['groups'=2,'blocks'=16,'pair'=2,'tm_1'=4,'space'=2] {'pair','tm_1',..., dimensions={0} | all-to-all | bytes 786432 | tf_op jit(solution)/shard_map/all_to_all | solution.py:338
  118.0 0.0 copy-done
  118.0 0.9 shard_map.81
  118.9 9.6 %all_to_all.27 = f32[8,56,128]{2,1,0:T(8,128)S(1)} all-to-all(f32[8,56,128]{2,1,0:T(8,128)S(1)} %bitcast.17), channel_id=1, replica_groups=mesh['groups'=2,'blocks'=16,'pair'=2,'tm_1'=4,'space'=2] {'pair','tm_1'}, dimensions={0} | all-to-all | bytes 458752 | tf_op jit(solution)/shard_map/all_to_all | solution.py:340
  128.5 0.0 copy-start.2
  128.5 36.4 %all_to_all.28 = f32[16,25,1,128]{3,2,1,0:T(1,128)S(1)} all-to-all(f32[16,25,1,128]{3,2,1,0:T(1,128)S(1)} %bitcast.20), channel_id=1, replica_groups=mesh['groups'=2,'blocks'=16,'pair'=2,'tm_1'=4,'space'=2] {'blocks'}, dimensions={0} | all-to-all | bytes 409600 | tf_op jit(solution)/shard_map/all_to_all | solution.py:344
  164.9 0.0 copy-done.2
  164.9 0.8 shard_map.83
  (5 shorter events, 0.1 us)
Async XLA Ops:
  0.6 55.1 %copy-start.3 = (f32[8,16,128]{2,1,0:T(8,128)S(1)}, f32[8,16,128]{2,1,0:T(8,128)}, u32[]{:S(2)}) copy-start(f32[8,16,128]{2,1,0:T(8,128)} %kappa.1) | copy-start | bytes 196612
  2.4 80.3 %copy-start.1 = (f32[256,256]{1,0:T(8,128)S(1)}, f32[256,256]{1,0:T(8,128)}, u32[]{:S(2)}) copy-start(f32[256,256]{1,0:T(8,128)} %constant.38.clone.mat) | copy-start | bytes 786436
  2.4 80.2 %all-to-all-start = ((f32[128,2,128]{2,1,0:T(2,128)}), f32[128,2,128]{2,1,0:T(2,128)S(1)}, u32[]{:S(2)}, u32[]{:S(2)}) async-start(f32[128,2,128]{2,1,0:T(2,128)} %bitcast.2), calls=%async_computation | async-start | bytes 262144 | tf_op jit(solution)/shard_map/all_to_all | solution.py:309
  55.8 3.1 %collective-permute-start = (f32[20,128]{1,0:T(8,128)S(1)}, f32[20,128]{1,0:T(8,128)S(1)}, u32[]{:S(2)}, u32[]{:S(2)}) collective-permute-start(f32[20,128]{1,0:T(8,128)S(1)} %pad_dynamic-slice_fusion), channel_id=1, source_target_pairs={{0,1},{1,0},{2,3},{3,2},{4,5},{5,4},{6,7},{7,6},{8,9},{9,8},{10,11... | collective-permute-start | bytes 30728 | tf_op jit(solution)/shard_map/ppermute | solution.py:315
  94.8 4.4 %collective-permute-start.1 = (f32[6,2,8,128]{3,2,1,0:T(8,128)S(1)}, f32[6,2,8,128]{3,2,1,0:T(8,128)S(1)}, u32[]{:S(2)}, u32[]{:S(2)}) collective-permute-start(f32[6,2,8,128]{3,2,1,0:T(8,128)S(1)} %get-tuple-element.16), channel_id=1, source_target_pairs={{0,16},{16,32},{32,48},{48,64},{64,80},{80,96},{96,112},{112,128},... | collective-permute-start | bytes 147464 | tf_op jit(solution)/shard_map/ppermute | solution.py:333
  97.5 7.4 %collective-permute-start.2 = (f32[6,2,8,128]{3,2,1,0:T(8,128)S(1)}, f32[6,2,8,128]{3,2,1,0:T(8,128)S(1)}, u32[]{:S(2)}, u32[]{:S(2)}) collective-permute-start(f32[6,2,8,128]{3,2,1,0:T(8,128)S(1)} %get-tuple-element.18), channel_id=1, source_target_pairs={{16,0},{32,16},{48,32},{64,48},{80,64},{96,80},{112,96},{128,112},... | collective-permute-start | bytes 147464 | tf_op jit(solution)/shard_map/ppermute | solution.py:333
  105.0 13.0 %copy-start = (f32[384,384]{1,0:T(8,128)S(1)}, f32[384,384]{1,0:T(8,128)}, u32[]{:S(2)}) copy-start(f32[384,384]{1,0:T(8,128)} %constant.39.clone.mat) | copy-start | bytes 1769476
  128.5 36.4 %copy-start.2 = (f32[1,8,16,128]{3,2,1,0:T(8,128)S(1)}, f32[1,8,16,128]{3,2,1,0:T(8,128)}, u32[]{:S(2)}) copy-start(f32[1,8,16,128]{3,2,1,0:T(8,128)} %param.6) | copy-start | bytes 196612

commit v7 on v6

--- a/solution.py
+++ b/solution.py
@@ -8,7 +8,6 @@
 from jax.experimental.pallas import tpu as pltpu
 from jax.sharding import Mesh
 from jax.sharding import PartitionSpec as P
-
 
 SWEEPS = 6
 TM = ("blocks", "pair", "tm_1")
@@ -78,7 +77,7 @@
     )
 
 
-def local_call(kernel, outs, inputs, scratch=(), keep_in=True, keep_out=True):
+def local_call(kernel, name, outs, inputs, scratch=(), keep_in=True, keep_out=True):
     vmem = pl.BlockSpec(memory_space=pltpu.VMEM)
     made = pltpu.VMEM if keep_out else jax.ShapeDtypeStruct
     call = pl.pallas_call(
@@ -87,6 +86,7 @@
         in_specs=[vmem] * inputs,
         out_specs=[vmem] * len(outs),
         scratch_shapes=list(scratch),
+        name=name,
     )
 
     def placed(*args):
@@ -121,28 +121,57 @@
         out[pl.ds(1, nx, stride=2), :] = s[...].reshape(lanes, nx).T
 
     scratch = [pltpu.VMEM((nz, ny, nx), jnp.float32)]
-    return local_call(kernel, [(2 * nx, lanes)], 3, scratch, keep_in=False)
-
-
-def make_forward(total, lanes):
-    def kernel(mat, cells, spec):
-        spec[...] = jnp.dot(
+    return local_call(kernel, "entry", [(2 * nx, lanes)], 3, scratch, keep_in=False)
+
+
+def make_forward(total, owners, lanes, ny):
+    rows = total // owners
+
+    def kernel(mat, cells, info, out, both):
+        both[...] = jnp.dot(
             mat[...], cells[...], precision=HIGH, preferred_element_type=jnp.float32
         )
-
-    return local_call(kernel, [(2 * total, lanes)], 2)
+        lane = iota((owners, lanes), 1)
+        lower = info[3:4, :]
+        edge = jnp.zeros((owners, lanes), jnp.float32)
+        for j in range(rows):
+            x = both[pl.ds(rows + j, owners, stride=2 * rows), :]
+            at = ny * (rows - 1 - j)
+            moved = lower * pltpu.roll(x, (at + ny) % lanes, 1) + (1.0 - lower) * (
+                pltpu.roll(x, at, 1) if at else x
+            )
+            edge = jnp.where((lane >= at) & (lane < at + ny), moved, edge)
+        for q in range(owners):
+            out[12 * q : 12 * q + rows, :] = both[2 * rows * q : 2 * rows * q + rows, :]
+        out[pl.ds(rows, owners, stride=12), :] = edge
+        for m in range(3):
+            row = jnp.broadcast_to(info[m : m + 1, :], (owners, lanes))
+            out[pl.ds(rows + 1 + m, owners, stride=12), :] = row
+
+    scratch = [pltpu.VMEM((2 * total, lanes), jnp.float32)]
+    return local_call(kernel, "forward", [(12 * owners, lanes)], 3, scratch)
 
 
 def make_border(own, depth, rows, lanes, ny):
-    def kernel(spec, kap, out, to_right, to_left):
+    def kernel(spec, out, to_right, to_left, kap):
         lane = iota((rows, lanes), 1)
         first, last = lane < ny, lane >= lanes - ny
+        for c in range(own):
+            for h in range(2):
+                for m in range(3):
+                    if c + own * m < own + 2 * depth:
+                        at = 2 * (c + own * m) + h
+                        line = 12 * (2 * c + h) + rows + 1 + m
+                        kap[at : at + 1, :] = spec[line : line + 1, :]
         for c in range(own):
             for h in range(2):
                 at = 2 * (depth + c) + h
                 k = jnp.broadcast_to(kap[at : at + 1, :], (rows, lanes))
-                other = pltpu.roll(spec[c, 1 - h, rows:, :], ny if h else lanes - ny, 1)
-                value = spec[c, h, :rows, :] + jnp.where(first if h else last, k * other, 0.0)
+                line = 12 * (2 * c + 1 - h) + rows
+                edge = jnp.broadcast_to(spec[line : line + 1, :], (rows, lanes))
+                other = pltpu.roll(edge, ny if h else 0, 1, stride=ny, stride_axis=0)
+                line = 12 * (2 * c + h)
+                value = spec[line : line + rows, :] + jnp.where(first if h else last, k * other, 0.0)
                 out[c, h] = value
                 if c >= own - depth:
                     to_right[c - (own - depth), h] = value
@@ -150,7 +179,7 @@
                     to_left[c, h] = value
 
     shapes = [(count, 2, rows, lanes) for count in (own, depth, depth)]
-    return local_call(kernel, shapes, 2)
+    return local_call(kernel, "border", shapes + [(2 * (own + 2 * depth), lanes)], 1)
 
 
 def make_backward(total, own, lanes):
@@ -176,7 +205,7 @@
         for c in range(own):
             out[pad * c + 3 * blocks : pad * (c + 1), :] = jnp.broadcast_to(sums, (8, lanes))
 
-    return local_call(kernel, [(own * pad, lanes)], 2)
+    return local_call(kernel, "backward", [(own * pad, lanes)], 2)
 
 
 def make_turn(blocks, own, lanes):
@@ -191,7 +220,7 @@
             sums = sums + near[pad * c + 3 * blocks : pad * c + 3 * blocks + 1, :]
         out[pl.ds(3 * own, blocks, stride=rows), :] = jnp.broadcast_to(sums, (blocks, lanes))
 
-    return local_call(kernel, [(blocks * rows, lanes)], 1)
+    return local_call(kernel, "turn", [(blocks * rows, lanes)], 1)
 
 
 def make_exit(nz, ny, nx, blocks, own):
@@ -212,7 +241,7 @@
         new_u[...] = u[...] + step * slab(0)
         new_r[...] = slab(2) - step * slab(1)
 
-    return local_call(kernel, [(nz, ny, nx)] * 2, 2, keep_out=False)
+    return local_call(kernel, "exit", [(nz, ny, nx)] * 2, 2, keep_out=False)
 
 
 def make_sweeps(own, depth, rows, lanes, ny):
@@ -285,7 +314,7 @@
                     out[row, at + 2] = mid[c - depth, h]
 
     field = pltpu.VMEM((cols, 2, rows, lanes), jnp.float32)
-    return local_call(kernel, [(2 * own, 6, rows, lanes)], 5, [field] * 5)
+    return local_call(kernel, "sweeps", [(2 * own, 6, rows, lanes)], 5, [field] * 5)
 
 
 def on_device(iterate, source, diffusivity):
@@ -301,32 +330,32 @@
     first_mat, second_mat, lams = tables(total, owners, own)
     core = lax.axis_index("space")
     block = lax.axis_index("blocks")
-    swap = [(0, 1), (1, 0)]
 
     u, f = iterate[0], source[0]
     (send,) = make_entry(nz, ny, nx)(u, f, diffusivity)
-    send, diffusivity = lax.optimization_barrier((send, diffusivity))
+    start = block * own + lax.axis_index(TM[1:])
+    owner = lax.axis_index(ROW)
+    lower = jnp.where(core == 0, 1.0, 0.0)
+    send, start, owner, lower = lax.optimization_barrier((send, start, owner, lower))
     cells = lax.all_to_all(
         send.reshape(total, 2, lanes), TM, split_axis=0, concat_axis=0, tiled=True
     ).reshape(2 * total, lanes)
 
-    kap = jnp.pad(diffusivity.reshape(lanes, nx).T, ((depth, depth), (0, 0)))
-    kap = lax.dynamic_slice_in_dim(kap, block * own, own + 2 * depth, axis=0)
-    kap_other = lax.ppermute(kap, "space", swap)
-    kap = jnp.where(
-        core == 0, jnp.stack([kap, kap_other], axis=1), jnp.stack([kap_other, kap], axis=1)
-    ).reshape(-1, lanes)
-    lam = lax.dynamic_index_in_dim(jnp.asarray(lams), lax.axis_index(ROW), axis=0, keepdims=False)
+    cells, kappa, start, lower = lax.optimization_barrier((cells, diffusivity, start, lower))
+    columns = jnp.pad(kappa.reshape(lanes, nx).T, ((depth, 2 * own), (0, 0)))
+    columns = lax.dynamic_slice_in_dim(columns, start, 2 * own + 1, axis=0)
+    lower = jnp.broadcast_to(lower, (1, lanes))
+    info = jnp.concatenate([columns[0:1], columns[own : own + 1], columns[2 * own :], lower], axis=0)
+    (spec,) = make_forward(total, owners, lanes, ny)(first_mat, cells, info)
+    spec = lax.all_to_all(
+        spec.reshape(owners, 12, 1, lanes), ROW, split_axis=0, concat_axis=0, tiled=True
+    )
+    spec, to_right, to_left, kap = make_border(own, depth, rows, lanes, ny)(spec.reshape(-1, lanes))
+    to_right, to_left, lams, owner = lax.optimization_barrier(
+        (to_right, to_left, jnp.asarray(lams), owner)
+    )
+    lam = lax.dynamic_index_in_dim(lams, owner, axis=0, keepdims=False)
     lam = jnp.broadcast_to(lam[:, :, None], (2, rows, lanes))
-    cells, kap, lam = lax.optimization_barrier((cells, kap, lam))
-
-    (spec,) = make_forward(total, lanes)(first_mat, cells)
-    spec = lax.all_to_all(
-        spec.reshape(owners, 2 * rows, lanes), ROW, split_axis=0, concat_axis=0, tiled=True
-    )
-    spec, to_right, to_left = make_border(own, depth, rows, lanes, ny)(
-        spec.reshape(own, cores, 2 * rows, lanes), kap
-    )
 
     def shifted(value, offset):
         pairs = [(i, i + offset) for i in range(blocks) if 0 <= i + offset < blocks]

time: 166 us -> 165 us (level)
  blocking collectives: 69.8 us -> 150 us
  starting transfers between devices: 59.3 us -> 3.96 us
  waiting for transfers between devices: 30.2 us -> 5.43 us
    all_to_all x1 -> x2, blocking collectives: 11.7 us -> 91.3 us  [the longest x1 80 us: on_device(): lax.all_to_all(send.reshape(total, 2, lanes), TM, split_axis=0, concat_ax...]
    all_to_all x1 -> x0, starting transfers between devices: 53.3 us -> none  [on_device(): lax.all_to_all(send.reshape(total, 2, lanes), TM, split_axis=0, concat_ax...]
    all_to_all x1 -> x0, waiting for transfers between devices: 23.6 us -> none  [on_device(): lax.all_to_all(send.reshape(total, 2, lanes), TM, split_axis=0, concat_ax...]
    ppermute x1 -> x0, starting transfers between devices: 1.95 us -> none  [on_device(): kap_other = lax.ppermute(kap, 'space', swap)]
  transfers between devices with their start and end apart: 4 -> 2, of which waited for: 4 -> 1; matrix products, arithmetic and copies ran while one was open for 1% -> 0% of each run, Pallas kernels for 0% -> 0%
where the time goes in v7:
time: 165 us
  blocking collectives  150 us (91%)
  waiting for transfers between devices  5.43 us (3%)
  Pallas kernels  4.11 us (2%)
  starting transfers between devices  3.96 us (2%)
    all_to_all x1, blocking collectives, on_device(): lax.all_to_all(send.reshape(total, 2, lanes), TM, split_axis=0, concat_ax...  80 us
    all_to_all x1, blocking collectives, on_device(): lax.all_to_all(far.reshape(blocks, 3 * own + 1, 1, lanes), 'blocks', spli...  36.4 us
    all_to_all x1, blocking collectives, on_device(): back = lax.all_to_all(back, ROW, split_axis=0, concat_axis=0, tiled=True)  12.2 us
    all_to_all x1, blocking collectives, on_device(): lax.all_to_all(spec.reshape(owners, 12, 1, lanes), ROW, split_axis=0, con...  11.3 us
    all_to_all x1, blocking collectives, on_device(): lax.all_to_all(near.reshape(own, -1, lanes), TM[1:], split_axis=0, concat...  9.58 us
    ppermute x2, waiting for transfers between devices, shifted(): return lax.ppermute(value, 'blocks', pairs)  5.43 us
    pallas_call x7, Pallas kernels, placed(): return call(*args)  4.11 us
    ppermute x2, starting transfers between devices, shifted(): return lax.ppermute(value, 'blocks', pairs)  3.96 us
  transfers between devices with their start and end apart: 2, of which 1 were waited for; matrix products, arithmetic and copies ran while one was open for 0% of the time, Pallas kernels for 0%

profile of v7, /device:TPU:40, one launch (start us, length us, event | category | flops | bytes accessed | tf_op | source)
XLA Modules:
  0.0 164.8 jit_solution(2394512896705825431)
XLA Ops:
  0.6 0.0 copy-start.3
  0.7 1.1 entry.1
  1.8 0.0 copy-start.2
  1.8 80.0 %all_to_all.25 = f32[128,2,128]{2,1,0:T(2,128)S(1)} all-to-all(f32[128,2,128]{2,1,0:T(2,128)S(1)} %bitcast.21), channel_id=1, replica_groups=mesh['groups'=2,'blocks'=16,'pair'=2,'tm_1'=4,'space'=2] {'blocks','pair..., dimensions={0} | all-to-all | bytes 262144 | tf_op jit(solution)/shard_map/all_to_all | solution.py:340
  81.8 0.0 copy-done.3
  81.8 0.1 copy.10
  81.9 0.1 pad.8.clone
  82.0 0.1 maximum_maximum_fusion.info
  82.1 0.0 copy-done.2
  82.1 0.5 forward.1
  82.5 11.3 %all_to_all.26 = f32[16,12,1,128]{3,2,1,0:T(1,128)S(1)} all-to-all(f32[16,12,1,128]{3,2,1,0:T(1,128)S(1)} %bitcast.24), channel_id=1, replica_groups=mesh['groups'=2,'blocks'=16,'pair'=2,'tm_1'=4,'space'=2] {'pair','tm_1',..., dimensions={0} | all-to-all | bytes 196608 | tf_op jit(solution)/shard_map/all_to_all | solution.py:350
  93.9 0.1 border.1
  94.0 2.7 %collective-permute-start = (f32[6,2,8,128]{3,2,1,0:T(8,128)S(1)}, f32[6,2,8,128]{3,2,1,0:T(8,128)S(1)}, u32[]{:S(2)}, u32[]{:S(2)}) collective-permute-start(f32[6,2,8,128]{3,2,1,0:T(8,128)S(1)} %get-tuple-element.30), channel_id=1, source_target_pairs={{0,16},{16,32},{32,48},{48,64},{64,80},{80,96},{96,112},{112,128},... | collective-permute-start | bytes 147464 | tf_op jit(solution)/shard_map/ppermute | solution.py:362
  96.6 1.3 collective-permute-start.1
  97.9 0.7 dynamic-slice_bitcast_fusion
  98.6 0.0 collective-permute-done.left
  98.6 5.4 %collective-permute-done.1.right = f32[6,2,8,128]{3,2,1,0:T(8,128)S(1)} collective-permute-done((f32[6,2,8,128]{3,2,1,0:T(8,128)S(1)}, f32[6,2,8,128]{3,2,1,0:T(8,128)S(1)}, u32[]{:S(2)}, u32[]{:S(2)}) %collective-permute-start.1) | collective-permute-done | bytes 49184 | tf_op jit(solution)/shard_map/ppermute | solution.py:362
  104.1 0.1 broadcast_in_dim.19.lam
  104.1 0.0 copy-start
  104.1 0.8 sweeps.1
  104.9 12.2 %all_to_all.27.back = f32[16,6,8,128]{3,2,1,0:T(8,128)S(1)} all-to-all(f32[16,6,8,128]{3,2,1,0:T(8,128)S(1)} %sweeps.1), channel_id=1, replica_groups=mesh['groups'=2,'blocks'=16,'pair'=2,'tm_1'=4,'space'=2] {'pair','tm_1',..., dimensions={0} | all-to-all | bytes 786432 | tf_op jit(solution)/shard_map/all_to_all | solution.py:367
  117.1 0.0 copy-done
  117.1 0.9 backward.1
  118.0 9.6 %all_to_all.28 = f32[8,56,128]{2,1,0:T(8,128)S(1)} all-to-all(f32[8,56,128]{2,1,0:T(8,128)S(1)} %bitcast.17), channel_id=1, replica_groups=mesh['groups'=2,'blocks'=16,'pair'=2,'tm_1'=4,'space'=2] {'pair','tm_1'}, dimensions={0} | all-to-all | bytes 458752 | tf_op jit(solution)/shard_map/all_to_all | solution.py:369
  127.6 0.0 copy-start.1
  127.6 36.4 %all_to_all.29 = f32[16,25,1,128]{3,2,1,0:T(1,128)S(1)} all-to-all(f32[16,25,1,128]{3,2,1,0:T(1,128)S(1)} %bitcast.20), channel_id=1, replica_groups=mesh['groups'=2,'blocks'=16,'pair'=2,'tm_1'=4,'space'=2] {'blocks'}, dimensions={0} | all-to-all | bytes 409600 | tf_op jit(solution)/shard_map/all_to_all | solution.py:373
  164.1 0.0 copy-done.1
  164.1 0.8 exit.1
  (2 shorter events, 0.0 us)
Async XLA Ops:
  0.6 81.1 %copy-start.3 = (f32[8,16,128]{2,1,0:T(8,128)S(1)}, f32[8,16,128]{2,1,0:T(8,128)}, u32[]{:S(2)}) copy-start(f32[8,16,128]{2,1,0:T(8,128)} %kappa.1) | copy-start | bytes 196612
  1.8 80.3 %copy-start.2 = (f32[256,256]{1,0:T(8,128)S(1)}, f32[256,256]{1,0:T(8,128)}, u32[]{:S(2)}) copy-start(f32[256,256]{1,0:T(8,128)} %constant.42.clone.mat) | copy-start | bytes 786436
  94.0 4.7 %collective-permute-start = (f32[6,2,8,128]{3,2,1,0:T(8,128)S(1)}, f32[6,2,8,128]{3,2,1,0:T(8,128)S(1)}, u32[]{:S(2)}, u32[]{:S(2)}) collective-permute-start(f32[6,2,8,128]{3,2,1,0:T(8,128)S(1)} %get-tuple-element.30), channel_id=1, source_target_pairs={{0,16},{16,32},{32,48},{48,64},{64,80},{80,96},{96,112},{112,128},... | collective-permute-start | bytes 147464 | tf_op jit(solution)/shard_map/ppermute | solution.py:362
  96.6 7.4 %collective-permute-start.1 = (f32[6,2,8,128]{3,2,1,0:T(8,128)S(1)}, f32[6,2,8,128]{3,2,1,0:T(8,128)S(1)}, u32[]{:S(2)}, u32[]{:S(2)}) collective-permute-start(f32[6,2,8,128]{3,2,1,0:T(8,128)S(1)} %get-tuple-element.32), channel_id=1, source_target_pairs={{16,0},{32,16},{48,32},{64,48},{80,64},{96,80},{112,96},{128,112},... | collective-permute-start | bytes 147464 | tf_op jit(solution)/shard_map/ppermute | solution.py:362
  104.1 13.0 %copy-start = (f32[384,384]{1,0:T(8,128)S(1)}, f32[384,384]{1,0:T(8,128)}, u32[]{:S(2)}) copy-start(f32[384,384]{1,0:T(8,128)} %constant.44.clone.mat) | copy-start | bytes 1769476
  127.6 36.4 %copy-start.1 = (f32[1,8,16,128]{3,2,1,0:T(8,128)S(1)}, f32[1,8,16,128]{3,2,1,0:T(8,128)}, u32[]{:S(2)}) copy-start(f32[1,8,16,128]{3,2,1,0:T(8,128)} %param.6) | copy-start | bytes 196612

commit v8 on v7

--- a/solution.py
+++ b/solution.py
@@ -62,17 +62,13 @@
     spectra[:, 0, :, :, 0] = (-fwd @ hist).reshape(owners, 2 * here, total)
     spectra[:, 0, :, :, 1] = fwd.reshape(owners, 2 * here, total)
     spectra[:, 1, :, :, 0] = fwd.reshape(owners, 2 * here, total)
-    flat = inv.reshape(total, owners, 2 * here)
-    second_mat = np.zeros((3, total, owners, 3, 2 * here))
-    second_mat[0, :, :, 0] = flat
-    second_mat[1, :, :, 0] = (hist @ inv.reshape(total, total)).reshape(flat.shape)
-    second_mat[1, :, :, 1] = flat
-    second_mat[2, :, :, 2] = flat
-    second_mat = second_mat.reshape(3, total // own, own, 3 * total).transpose(2, 0, 1, 3)
+    flat = inv.reshape(total, total)
+    second_mat = np.stack([hist @ flat, flat]).reshape(2, total // own, own, total)
+    second_mat = second_mat.transpose(0, 2, 1, 3)
     f32 = np.float32
     return (
         first_mat.reshape(2 * total, 2 * total).astype(f32),
-        second_mat.reshape(3 * total, 3 * total).astype(f32),
+        second_mat.reshape(2 * total, total).astype(f32),
         lams.reshape(owners, 2, 2 * here).astype(f32),
     )
 
@@ -187,17 +183,22 @@
     pad = 3 * blocks + 8
 
     def kernel(mat, back, out):
-        fields = jnp.concatenate(
-            [back[:, 3 * h : 3 * h + 3].reshape(3 * total, lanes) for h in range(2)], axis=1
-        )
-        every = jnp.dot(mat[...], fields, precision=HIGH, preferred_element_type=jnp.float32)
-        ri = ii = 0.0
-        for c in range(own):
-            at = 3 * blocks * c
-            image = every[at + blocks : at + 2 * blocks]
-            ri = ri + every[at + 2 * blocks : at + 3 * blocks] * image
-            ii = ii + image * image
-            out[pad * c : pad * c + 3 * blocks, :] = every[at : at + 3 * blocks, :lanes]
+        def fields(k):
+            return jnp.concatenate([back[:, 3 * h + k].reshape(total, lanes) for h in range(2)], 1)
+
+        def product(m, x):
+            return jnp.dot(m, x, precision=HIGH, preferred_element_type=jnp.float32)
+
+        first = product(mat[...], fields(0))
+        rest = product(mat[total:, :], jnp.concatenate([fields(1), fields(2)], axis=1))
+        correction = first[total:]
+        image = first[:total] + rest[:, : 2 * lanes]
+        residual = rest[:, 2 * lanes :]
+        ri, ii = residual * image, image * image
+        for c in range(own):
+            for k, field in enumerate((correction, image, residual)):
+                at = pad * c + blocks * k
+                out[at : at + blocks, :] = field[blocks * c : blocks * (c + 1), :lanes]
         ri = jnp.sum(ri[:, :lanes] + ri[:, lanes:], axis=0, keepdims=True)
         ii = jnp.sum(ii[:, :lanes] + ii[:, lanes:], axis=0, keepdims=True)
         low = iota((1, lanes), 1) < lanes // 2

time: 165 us -> 165 us (level)
  no operation moved by 1% of the time
where the time goes in v8:
time: 165 us
  blocking collectives  150 us (91%)
  waiting for transfers between devices  5.43 us (3%)
  starting transfers between devices  3.96 us (2%)
  Pallas kernels  3.88 us (2%)
    all_to_all x1, blocking collectives, on_device(): lax.all_to_all(send.reshape(total, 2, lanes), TM, split_axis=0, concat_ax...  80 us
    all_to_all x1, blocking collectives, on_device(): lax.all_to_all(far.reshape(blocks, 3 * own + 1, 1, lanes), 'blocks', spli...  36.4 us
    all_to_all x1, blocking collectives, on_device(): back = lax.all_to_all(back, ROW, split_axis=0, concat_axis=0, tiled=True)  12.4 us
    all_to_all x1, blocking collectives, on_device(): lax.all_to_all(spec.reshape(owners, 12, 1, lanes), ROW, split_axis=0, con...  11.3 us
    all_to_all x1, blocking collectives, on_device(): lax.all_to_all(near.reshape(own, -1, lanes), TM[1:], split_axis=0, concat...  9.58 us
    ppermute x2, waiting for transfers between devices, shifted(): return lax.ppermute(value, 'blocks', pairs)  5.43 us
    ppermute x2, starting transfers between devices, shifted(): return lax.ppermute(value, 'blocks', pairs)  3.96 us
    pallas_call x7, Pallas kernels, placed(): return call(*args)  3.88 us
  transfers between devices with their start and end apart: 2, of which 1 were waited for; matrix products, arithmetic and copies ran while one was open for 0% of the time, Pallas kernels for 0%

profile of v8, /device:TPU:40, one launch (start us, length us, event | category | flops | bytes accessed | tf_op | source)
XLA Modules:
  0.0 164.7 jit_solution(3313590236489810769)
XLA Ops:
  0.6 0.0 copy-start.3
  0.7 1.1 entry.1
  1.8 0.0 copy-start.1
  1.8 80.0 %all_to_all.25 = f32[128,2,128]{2,1,0:T(2,128)S(1)} all-to-all(f32[128,2,128]{2,1,0:T(2,128)S(1)} %bitcast.21), channel_id=1, replica_groups=mesh['groups'=2,'blocks'=16,'pair'=2,'tm_1'=4,'space'=2] {'blocks','pair..., dimensions={0} | all-to-all | bytes 262144 | tf_op jit(solution)/shard_map/all_to_all | solution.py:341
  81.8 0.0 copy-done.3
  81.8 0.1 copy.10
  81.9 0.1 pad.8.clone
  82.0 0.1 maximum_maximum_fusion.info
  82.1 0.0 copy-done.1
  82.1 0.5 forward.1
  82.5 11.3 %all_to_all.26 = f32[16,12,1,128]{3,2,1,0:T(1,128)S(1)} all-to-all(f32[16,12,1,128]{3,2,1,0:T(1,128)S(1)} %bitcast.24), channel_id=1, replica_groups=mesh['groups'=2,'blocks'=16,'pair'=2,'tm_1'=4,'space'=2] {'pair','tm_1',..., dimensions={0} | all-to-all | bytes 196608 | tf_op jit(solution)/shard_map/all_to_all | solution.py:351
  93.9 0.1 border.1
  94.0 2.7 %collective-permute-start = (f32[6,2,8,128]{3,2,1,0:T(8,128)S(1)}, f32[6,2,8,128]{3,2,1,0:T(8,128)S(1)}, u32[]{:S(2)}, u32[]{:S(2)}) collective-permute-start(f32[6,2,8,128]{3,2,1,0:T(8,128)S(1)} %get-tuple-element.30), channel_id=1, source_target_pairs={{0,16},{16,32},{32,48},{48,64},{64,80},{80,96},{96,112},{112,128},... | collective-permute-start | bytes 147464 | tf_op jit(solution)/shard_map/ppermute | solution.py:363
  96.6 1.3 collective-permute-start.1
  97.9 0.7 dynamic-slice_bitcast_fusion
  98.6 0.0 collective-permute-done.left
  98.6 5.4 %collective-permute-done.1.right = f32[6,2,8,128]{3,2,1,0:T(8,128)S(1)} collective-permute-done((f32[6,2,8,128]{3,2,1,0:T(8,128)S(1)}, f32[6,2,8,128]{3,2,1,0:T(8,128)S(1)}, u32[]{:S(2)}, u32[]{:S(2)}) %collective-permute-start.1) | collective-permute-done | bytes 49184 | tf_op jit(solution)/shard_map/ppermute | solution.py:363
  104.1 0.1 broadcast_in_dim.19.lam
  104.1 0.8 sweeps.1
  104.9 0.0 copy-start.2
  104.9 12.4 %all_to_all.27.back = f32[16,6,8,128]{3,2,1,0:T(8,128)S(1)} all-to-all(f32[16,6,8,128]{3,2,1,0:T(8,128)S(1)} %sweeps.1), channel_id=1, replica_groups=mesh['groups'=2,'blocks'=16,'pair'=2,'tm_1'=4,'space'=2] {'pair','tm_1',..., dimensions={0} | all-to-all | bytes 786432 | tf_op jit(solution)/shard_map/all_to_all | solution.py:368
  117.3 0.0 copy-done.2
  117.3 0.6 backward.1
  117.9 9.6 %all_to_all.28 = f32[8,56,128]{2,1,0:T(8,128)S(1)} all-to-all(f32[8,56,128]{2,1,0:T(8,128)S(1)} %bitcast.17), channel_id=1, replica_groups=mesh['groups'=2,'blocks'=16,'pair'=2,'tm_1'=4,'space'=2] {'pair','tm_1'}, dimensions={0} | all-to-all | bytes 458752 | tf_op jit(solution)/shard_map/all_to_all | solution.py:370
  127.5 0.0 copy-start
  127.5 36.4 %all_to_all.29 = f32[16,25,1,128]{3,2,1,0:T(1,128)S(1)} all-to-all(f32[16,25,1,128]{3,2,1,0:T(1,128)S(1)} %bitcast.20), channel_id=1, replica_groups=mesh['groups'=2,'blocks'=16,'pair'=2,'tm_1'=4,'space'=2] {'blocks'}, dimensions={0} | all-to-all | bytes 409600 | tf_op jit(solution)/shard_map/all_to_all | solution.py:374
  164.0 0.0 copy-done
  164.0 0.8 exit.1
  (2 shorter events, 0.0 us)
Async XLA Ops:
  0.6 81.1 %copy-start.3 = (f32[8,16,128]{2,1,0:T(8,128)S(1)}, f32[8,16,128]{2,1,0:T(8,128)}, u32[]{:S(2)}) copy-start(f32[8,16,128]{2,1,0:T(8,128)} %kappa.1) | copy-start | bytes 196612
  1.8 80.3 %copy-start.1 = (f32[256,256]{1,0:T(8,128)S(1)}, f32[256,256]{1,0:T(8,128)}, u32[]{:S(2)}) copy-start(f32[256,256]{1,0:T(8,128)} %constant.42.clone.mat) | copy-start | bytes 786436
  94.0 4.7 %collective-permute-start = (f32[6,2,8,128]{3,2,1,0:T(8,128)S(1)}, f32[6,2,8,128]{3,2,1,0:T(8,128)S(1)}, u32[]{:S(2)}, u32[]{:S(2)}) collective-permute-start(f32[6,2,8,128]{3,2,1,0:T(8,128)S(1)} %get-tuple-element.30), channel_id=1, source_target_pairs={{0,16},{16,32},{32,48},{48,64},{64,80},{80,96},{96,112},{112,128},... | collective-permute-start | bytes 147464 | tf_op jit(solution)/shard_map/ppermute | solution.py:363
  96.6 7.4 %collective-permute-start.1 = (f32[6,2,8,128]{3,2,1,0:T(8,128)S(1)}, f32[6,2,8,128]{3,2,1,0:T(8,128)S(1)}, u32[]{:S(2)}, u32[]{:S(2)}) collective-permute-start(f32[6,2,8,128]{3,2,1,0:T(8,128)S(1)} %get-tuple-element.32), channel_id=1, source_target_pairs={{16,0},{32,16},{48,32},{64,48},{80,64},{96,80},{112,96},{128,112},... | collective-permute-start | bytes 147464 | tf_op jit(solution)/shard_map/ppermute | solution.py:363
  104.9 12.4 %copy-start.2 = (f32[256,128]{1,0:T(8,128)S(1)}, f32[256,128]{1,0:T(8,128)}, u32[]{:S(2)}) copy-start(f32[256,128]{1,0:T(8,128)} %constant.44.clone.mat) | copy-start | bytes 393220
  127.5 36.4 %copy-start = (f32[1,8,16,128]{3,2,1,0:T(8,128)S(1)}, f32[1,8,16,128]{3,2,1,0:T(8,128)}, u32[]{:S(2)}) copy-start(f32[1,8,16,128]{3,2,1,0:T(8,128)} %param.6) | copy-start | bytes 196612

commit v9 on v8

--- a/solution.py
+++ b/solution.py
@@ -8,6 +8,7 @@
 from jax.experimental.pallas import tpu as pltpu
 from jax.sharding import Mesh
 from jax.sharding import PartitionSpec as P
+
 
 SWEEPS = 6
 TM = ("blocks", "pair", "tm_1")
@@ -73,7 +74,7 @@
     )
 
 
-def local_call(kernel, name, outs, inputs, scratch=(), keep_in=True, keep_out=True):
+def local_call(kernel, outs, inputs, scratch=(), keep_in=True, keep_out=True):
     vmem = pl.BlockSpec(memory_space=pltpu.VMEM)
     made = pltpu.VMEM if keep_out else jax.ShapeDtypeStruct
     call = pl.pallas_call(
@@ -82,7 +83,6 @@
         in_specs=[vmem] * inputs,
         out_specs=[vmem] * len(outs),
         scratch_shapes=list(scratch),
-        name=name,
     )
 
     def placed(*args):
@@ -117,7 +117,7 @@
         out[pl.ds(1, nx, stride=2), :] = s[...].reshape(lanes, nx).T
 
     scratch = [pltpu.VMEM((nz, ny, nx), jnp.float32)]
-    return local_call(kernel, "entry", [(2 * nx, lanes)], 3, scratch, keep_in=False)
+    return local_call(kernel, [(2 * nx, lanes)], 3, scratch, keep_in=False)
 
 
 def make_forward(total, owners, lanes, ny):
@@ -145,7 +145,7 @@
             out[pl.ds(rows + 1 + m, owners, stride=12), :] = row
 
     scratch = [pltpu.VMEM((2 * total, lanes), jnp.float32)]
-    return local_call(kernel, "forward", [(12 * owners, lanes)], 3, scratch)
+    return local_call(kernel, [(12 * owners, lanes)], 3, scratch)
 
 
 def make_border(own, depth, rows, lanes, ny):
@@ -175,7 +175,7 @@
                     to_left[c, h] = value
 
     shapes = [(count, 2, rows, lanes) for count in (own, depth, depth)]
-    return local_call(kernel, "border", shapes + [(2 * (own + 2 * depth), lanes)], 1)
+    return local_call(kernel, shapes + [(2 * (own + 2 * depth), lanes)], 1)
 
 
 def make_backward(total, own, lanes):
@@ -206,7 +206,7 @@
         for c in range(own):
             out[pad * c + 3 * blocks : pad * (c + 1), :] = jnp.broadcast_to(sums, (8, lanes))
 
-    return local_call(kernel, "backward", [(own * pad, lanes)], 2)
+    return local_call(kernel, [(own * pad, lanes)], 2)
 
 
 def make_turn(blocks, own, lanes):
@@ -221,7 +221,7 @@
             sums = sums + near[pad * c + 3 * blocks : pad * c + 3 * blocks + 1, :]
         out[pl.ds(3 * own, blocks, stride=rows), :] = jnp.broadcast_to(sums, (blocks, lanes))
 
-    return local_call(kernel, "turn", [(blocks * rows, lanes)], 1)
+    return local_call(kernel, [(blocks * rows, lanes)], 1)
 
 
 def make_exit(nz, ny, nx, blocks, own):
@@ -242,7 +242,7 @@
         new_u[...] = u[...] + step * slab(0)
         new_r[...] = slab(2) - step * slab(1)
 
-    return local_call(kernel, "exit", [(nz, ny, nx)] * 2, 2, keep_out=False)
+    return local_call(kernel, [(nz, ny, nx)] * 2, 2, keep_out=False)
 
 
 def make_sweeps(own, depth, rows, lanes, ny):
@@ -315,7 +315,7 @@
                     out[row, at + 2] = mid[c - depth, h]
 
     field = pltpu.VMEM((cols, 2, rows, lanes), jnp.float32)
-    return local_call(kernel, "sweeps", [(2 * own, 6, rows, lanes)], 5, [field] * 5)
+    return local_call(kernel, [(2 * own, 6, rows, lanes)], 5, [field] * 5)
 
 
 def on_device(iterate, source, diffusivity):
@@ -362,8 +362,8 @@
         pairs = [(i, i + offset) for i in range(blocks) if 0 <= i + offset < blocks]
         return lax.ppermute(value, "blocks", pairs)
 
+    right = shifted(to_left, -1)
     left = shifted(to_right, 1)
-    right = shifted(to_left, -1)
     (back,) = make_sweeps(own, depth, rows, lanes, ny)(left, spec, right, kap, lam)
     back = lax.all_to_all(back, ROW, split_axis=0, concat_axis=0, tiled=True)
     (near,) = make_backward(total, own, lanes)(second_mat, back)

time: 165 us -> 165 us (level)
  no operation moved by 1% of the time
where the time goes in v9:
time: 165 us
  blocking collectives  150 us (91%)
  waiting for transfers between devices  5.43 us (3%)
  starting transfers between devices  3.96 us (2%)
  Pallas kernels  3.88 us (2%)
    all_to_all x1, blocking collectives, on_device(): lax.all_to_all(send.reshape(total, 2, lanes), TM, split_axis=0, concat_ax...  80 us
    all_to_all x1, blocking collectives, on_device(): lax.all_to_all(far.reshape(blocks, 3 * own + 1, 1, lanes), 'blocks', spli...  36.4 us
    all_to_all x1, blocking collectives, on_device(): back = lax.all_to_all(back, ROW, split_axis=0, concat_axis=0, tiled=True)  12.4 us
    all_to_all x1, blocking collectives, on_device(): lax.all_to_all(spec.reshape(owners, 12, 1, lanes), ROW, split_axis=0, con...  11.3 us
    all_to_all x1, blocking collectives, on_device(): lax.all_to_all(near.reshape(own, -1, lanes), TM[1:], split_axis=0, concat...  9.58 us
    ppermute x2, waiting for transfers between devices, shifted(): return lax.ppermute(value, 'blocks', pairs)  5.43 us
    ppermute x2, starting transfers between devices, shifted(): return lax.ppermute(value, 'blocks', pairs)  3.96 us
    pallas_call x7, Pallas kernels, placed(): return call(*args)  3.88 us
  transfers between devices with their start and end apart: 2, of which 1 were waited for; matrix products, arithmetic and copies ran while one was open for 0% of the time, Pallas kernels for 0%

profile of v9, /device:TPU:40, one launch (start us, length us, event | category | flops | bytes accessed | tf_op | source)
XLA Modules:
  0.0 164.7 jit_solution(3313590236489810769)
XLA Ops:
  0.6 0.0 copy-start.3
  0.7 1.1 shard_map.77
  1.8 0.0 copy-start.1
  1.8 80.0 %all_to_all.25 = f32[128,2,128]{2,1,0:T(2,128)S(1)} all-to-all(f32[128,2,128]{2,1,0:T(2,128)S(1)} %bitcast.21), channel_id=1, replica_groups=mesh['groups'=2,'blocks'=16,'pair'=2,'tm_1'=4,'space'=2] {'blocks','pair..., dimensions={0} | all-to-all | bytes 262144 | tf_op jit(solution)/shard_map/all_to_all | solution.py:341
  81.8 0.0 copy-done.3
  81.8 0.1 copy.10
  81.9 0.1 pad.8.clone
  82.0 0.1 maximum_maximum_fusion.info
  82.1 0.0 copy-done.1
  82.1 0.5 shard_map.78
  82.5 11.3 %all_to_all.26 = f32[16,12,1,128]{3,2,1,0:T(1,128)S(1)} all-to-all(f32[16,12,1,128]{3,2,1,0:T(1,128)S(1)} %bitcast.24), channel_id=1, replica_groups=mesh['groups'=2,'blocks'=16,'pair'=2,'tm_1'=4,'space'=2] {'pair','tm_1',..., dimensions={0} | all-to-all | bytes 196608 | tf_op jit(solution)/shard_map/all_to_all | solution.py:351
  93.9 0.1 shard_map.79
  94.0 2.7 %collective-permute-start = (f32[6,2,8,128]{3,2,1,0:T(8,128)S(1)}, f32[6,2,8,128]{3,2,1,0:T(8,128)S(1)}, u32[]{:S(2)}, u32[]{:S(2)}) collective-permute-start(f32[6,2,8,128]{3,2,1,0:T(8,128)S(1)} %get-tuple-element.30), channel_id=1, source_target_pairs={{0,16},{16,32},{32,48},{48,64},{64,80},{80,96},{96,112},{112,128},... | collective-permute-start | bytes 147464 | tf_op jit(solution)/shard_map/ppermute | solution.py:363
  96.6 1.3 collective-permute-start.1
  97.9 0.7 dynamic-slice_bitcast_fusion
  98.6 0.0 collective-permute-done.left
  98.6 5.4 %collective-permute-done.1.right = f32[6,2,8,128]{3,2,1,0:T(8,128)S(1)} collective-permute-done((f32[6,2,8,128]{3,2,1,0:T(8,128)S(1)}, f32[6,2,8,128]{3,2,1,0:T(8,128)S(1)}, u32[]{:S(2)}, u32[]{:S(2)}) %collective-permute-start.1) | collective-permute-done | bytes 49184 | tf_op jit(solution)/shard_map/ppermute | solution.py:363
  104.1 0.1 broadcast_in_dim.19.lam
  104.1 0.8 shard_map.80
  104.9 0.0 copy-start.2
  104.9 12.4 %all_to_all.27.back = f32[16,6,8,128]{3,2,1,0:T(8,128)S(1)} all-to-all(f32[16,6,8,128]{3,2,1,0:T(8,128)S(1)} %shard_map.80), channel_id=1, replica_groups=mesh['groups'=2,'blocks'=16,'pair'=2,'tm_1'=4,'space'=2] {'pair','tm_1',..., dimensions={0} | all-to-all | bytes 786432 | tf_op jit(solution)/shard_map/all_to_all | solution.py:368
  117.3 0.0 copy-done.2
  117.3 0.6 shard_map.81
  117.9 9.6 %all_to_all.28 = f32[8,56,128]{2,1,0:T(8,128)S(1)} all-to-all(f32[8,56,128]{2,1,0:T(8,128)S(1)} %bitcast.17), channel_id=1, replica_groups=mesh['groups'=2,'blocks'=16,'pair'=2,'tm_1'=4,'space'=2] {'pair','tm_1'}, dimensions={0} | all-to-all | bytes 458752 | tf_op jit(solution)/shard_map/all_to_all | solution.py:370
  127.5 0.0 copy-start
  127.5 36.4 %all_to_all.29 = f32[16,25,1,128]{3,2,1,0:T(1,128)S(1)} all-to-all(f32[16,25,1,128]{3,2,1,0:T(1,128)S(1)} %bitcast.20), channel_id=1, replica_groups=mesh['groups'=2,'blocks'=16,'pair'=2,'tm_1'=4,'space'=2] {'blocks'}, dimensions={0} | all-to-all | bytes 409600 | tf_op jit(solution)/shard_map/all_to_all | solution.py:374
  164.0 0.0 copy-done
  164.0 0.8 shard_map.83
  (2 shorter events, 0.0 us)
Async XLA Ops:
  0.6 81.1 %copy-start.3 = (f32[8,16,128]{2,1,0:T(8,128)S(1)}, f32[8,16,128]{2,1,0:T(8,128)}, u32[]{:S(2)}) copy-start(f32[8,16,128]{2,1,0:T(8,128)} %kappa.1) | copy-start | bytes 196612
  1.8 80.3 %copy-start.1 = (f32[256,256]{1,0:T(8,128)S(1)}, f32[256,256]{1,0:T(8,128)}, u32[]{:S(2)}) copy-start(f32[256,256]{1,0:T(8,128)} %constant.42.clone.mat) | copy-start | bytes 786436
  94.0 4.7 %collective-permute-start = (f32[6,2,8,128]{3,2,1,0:T(8,128)S(1)}, f32[6,2,8,128]{3,2,1,0:T(8,128)S(1)}, u32[]{:S(2)}, u32[]{:S(2)}) collective-permute-start(f32[6,2,8,128]{3,2,1,0:T(8,128)S(1)} %get-tuple-element.30), channel_id=1, source_target_pairs={{0,16},{16,32},{32,48},{48,64},{64,80},{80,96},{96,112},{112,128},... | collective-permute-start | bytes 147464 | tf_op jit(solution)/shard_map/ppermute | solution.py:363
  96.6 7.4 %collective-permute-start.1 = (f32[6,2,8,128]{3,2,1,0:T(8,128)S(1)}, f32[6,2,8,128]{3,2,1,0:T(8,128)S(1)}, u32[]{:S(2)}, u32[]{:S(2)}) collective-permute-start(f32[6,2,8,128]{3,2,1,0:T(8,128)S(1)} %get-tuple-element.32), channel_id=1, source_target_pairs={{16,0},{32,16},{48,32},{64,48},{80,64},{96,80},{112,96},{128,112},... | collective-permute-start | bytes 147464 | tf_op jit(solution)/shard_map/ppermute | solution.py:363
  104.9 12.4 %copy-start.2 = (f32[256,128]{1,0:T(8,128)S(1)}, f32[256,128]{1,0:T(8,128)}, u32[]{:S(2)}) copy-start(f32[256,128]{1,0:T(8,128)} %constant.44.clone.mat) | copy-start | bytes 393220
  127.5 36.4 %copy-start = (f32[1,8,16,128]{3,2,1,0:T(8,128)S(1)}, f32[1,8,16,128]{3,2,1,0:T(8,128)}, u32[]{:S(2)}) copy-start(f32[1,8,16,128]{3,2,1,0:T(8,128)} %param.6) | copy-start | bytes 196612

commit v10 on v8

--- a/solution.py
+++ b/solution.py
@@ -138,14 +138,16 @@
             )
             edge = jnp.where((lane >= at) & (lane < at + ny), moved, edge)
         for q in range(owners):
-            out[12 * q : 12 * q + rows, :] = both[2 * rows * q : 2 * rows * q + rows, :]
-        out[pl.ds(rows, owners, stride=12), :] = edge
+            out[16 * q : 16 * q + rows, :] = both[2 * rows * q : 2 * rows * q + rows, :]
+        out[pl.ds(rows, owners, stride=16), :] = edge
         for m in range(3):
             row = jnp.broadcast_to(info[m : m + 1, :], (owners, lanes))
-            out[pl.ds(rows + 1 + m, owners, stride=12), :] = row
+            out[pl.ds(rows + 1 + m, owners, stride=16), :] = row
+        for m in range(rows + 4, 16):
+            out[pl.ds(m, owners, stride=16), :] = edge
 
     scratch = [pltpu.VMEM((2 * total, lanes), jnp.float32)]
-    return local_call(kernel, "forward", [(12 * owners, lanes)], 3, scratch)
+    return local_call(kernel, "forward", [(16 * owners, lanes)], 3, scratch)
 
 
 def make_border(own, depth, rows, lanes, ny):
@@ -157,16 +159,16 @@
                 for m in range(3):
                     if c + own * m < own + 2 * depth:
                         at = 2 * (c + own * m) + h
-                        line = 12 * (2 * c + h) + rows + 1 + m
+                        line = 16 * (2 * c + h) + rows + 1 + m
                         kap[at : at + 1, :] = spec[line : line + 1, :]
         for c in range(own):
             for h in range(2):
                 at = 2 * (depth + c) + h
                 k = jnp.broadcast_to(kap[at : at + 1, :], (rows, lanes))
-                line = 12 * (2 * c + 1 - h) + rows
+                line = 16 * (2 * c + 1 - h) + rows
                 edge = jnp.broadcast_to(spec[line : line + 1, :], (rows, lanes))
                 other = pltpu.roll(edge, ny if h else 0, 1, stride=ny, stride_axis=0)
-                line = 12 * (2 * c + h)
+                line = 16 * (2 * c + h)
                 value = spec[line : line + rows, :] + jnp.where(first if h else last, k * other, 0.0)
                 out[c, h] = value
                 if c >= own - depth:
@@ -349,7 +351,7 @@
     info = jnp.concatenate([columns[0:1], columns[own : own + 1], columns[2 * own :], lower], axis=0)
     (spec,) = make_forward(total, owners, lanes, ny)(first_mat, cells, info)
     spec = lax.all_to_all(
-        spec.reshape(owners, 12, 1, lanes), ROW, split_axis=0, concat_axis=0, tiled=True
+        spec.reshape(owners, 16, lanes), ROW, split_axis=0, concat_axis=0, tiled=True
     )
     spec, to_right, to_left, kap = make_border(own, depth, rows, lanes, ny)(spec.reshape(-1, lanes))
     to_right, to_left, lams, owner = lax.optimization_barrier(

time: 165 us -> 165 us (level)
  no operation moved by 1% of the time
where the time goes in v10:
time: 165 us
  blocking collectives  150 us (91%)
  waiting for transfers between devices  5.44 us (3%)
  starting transfers between devices  3.96 us (2%)
  Pallas kernels  3.88 us (2%)
    all_to_all x1, blocking collectives, on_device(): lax.all_to_all(send.reshape(total, 2, lanes), TM, split_axis=0, concat_ax...  80 us
    all_to_all x1, blocking collectives, on_device(): lax.all_to_all(far.reshape(blocks, 3 * own + 1, 1, lanes), 'blocks', spli...  36.3 us
    all_to_all x1, blocking collectives, on_device(): back = lax.all_to_all(back, ROW, split_axis=0, concat_axis=0, tiled=True)  12.4 us
    all_to_all x1, blocking collectives, on_device(): lax.all_to_all(spec.reshape(owners, 16, lanes), ROW, split_axis=0, concat...  11.7 us
    all_to_all x1, blocking collectives, on_device(): lax.all_to_all(near.reshape(own, -1, lanes), TM[1:], split_axis=0, concat...  9.58 us
    ppermute x2, waiting for transfers between devices, shifted(): return lax.ppermute(value, 'blocks', pairs)  5.44 us
    ppermute x2, starting transfers between devices, shifted(): return lax.ppermute(value, 'blocks', pairs)  3.96 us
    pallas_call x7, Pallas kernels, placed(): return call(*args)  3.88 us
  transfers between devices with their start and end apart: 2, of which 1 were waited for; matrix products, arithmetic and copies ran while one was open for 0% of the time, Pallas kernels for 0%

profile of v10, /device:TPU:40, one launch (start us, length us, event | category | flops | bytes accessed | tf_op | source)
XLA Modules:
  0.0 165.0 jit_solution(5843625101882625647)
XLA Ops:
  0.6 0.0 copy-start.3
  0.7 1.1 entry.1
  1.8 0.0 copy-start
  1.8 80.0 %all_to_all.25 = f32[128,2,128]{2,1,0:T(2,128)S(1)} all-to-all(f32[128,2,128]{2,1,0:T(2,128)S(1)} %bitcast.22), channel_id=1, replica_groups=mesh['groups'=2,'blocks'=16,'pair'=2,'tm_1'=4,'space'=2] {'blocks','pair..., dimensions={0} | all-to-all | bytes 262144 | tf_op jit(solution)/shard_map/all_to_all | solution.py:343
  81.8 0.0 copy-done.3
  81.8 0.1 copy.10
  81.9 0.1 pad.8.clone
  82.0 0.1 maximum_maximum_fusion.info
  82.1 0.0 copy-done
  82.1 0.5 forward.1
  82.6 11.7 %all_to_all.26 = f32[16,16,128]{2,1,0:T(8,128)S(1)} all-to-all(f32[16,16,128]{2,1,0:T(8,128)S(1)} %bitcast.24), channel_id=1, replica_groups=mesh['groups'=2,'blocks'=16,'pair'=2,'tm_1'=4,'space'=2] {'pair','tm_1',..., dimensions={0} | all-to-all | bytes 262144 | tf_op jit(solution)/shard_map/all_to_all | solution.py:353
  94.2 0.1 border.1
  94.3 2.7 %collective-permute-start = (f32[6,2,8,128]{3,2,1,0:T(8,128)S(1)}, f32[6,2,8,128]{3,2,1,0:T(8,128)S(1)}, u32[]{:S(2)}, u32[]{:S(2)}) collective-permute-start(f32[6,2,8,128]{3,2,1,0:T(8,128)S(1)} %get-tuple-element.30), channel_id=1, source_target_pairs={{0,16},{16,32},{32,48},{48,64},{64,80},{80,96},{96,112},{112,128},... | collective-permute-start | bytes 147464 | tf_op jit(solution)/shard_map/ppermute | solution.py:365
  97.0 1.3 collective-permute-start.1
  98.3 0.7 dynamic-slice_bitcast_fusion
  99.0 0.0 collective-permute-done.left
  99.0 5.4 %collective-permute-done.1.right = f32[6,2,8,128]{3,2,1,0:T(8,128)S(1)} collective-permute-done((f32[6,2,8,128]{3,2,1,0:T(8,128)S(1)}, f32[6,2,8,128]{3,2,1,0:T(8,128)S(1)}, u32[]{:S(2)}, u32[]{:S(2)}) %collective-permute-start.1) | collective-permute-done | bytes 49184 | tf_op jit(solution)/shard_map/ppermute | solution.py:365
  104.4 0.1 broadcast_in_dim.19.lam
  104.5 0.8 sweeps.1
  105.3 0.0 copy-start.2
  105.3 12.4 %all_to_all.27.back = f32[16,6,8,128]{3,2,1,0:T(8,128)S(1)} all-to-all(f32[16,6,8,128]{3,2,1,0:T(8,128)S(1)} %sweeps.1), channel_id=1, replica_groups=mesh['groups'=2,'blocks'=16,'pair'=2,'tm_1'=4,'space'=2] {'pair','tm_1',..., dimensions={0} | all-to-all | bytes 786432 | tf_op jit(solution)/shard_map/all_to_all | solution.py:370
  117.6 0.0 copy-done.2
  117.6 0.6 backward.1
  118.3 9.6 %all_to_all.28 = f32[8,56,128]{2,1,0:T(8,128)S(1)} all-to-all(f32[8,56,128]{2,1,0:T(8,128)S(1)} %bitcast.17), channel_id=1, replica_groups=mesh['groups'=2,'blocks'=16,'pair'=2,'tm_1'=4,'space'=2] {'pair','tm_1'}, dimensions={0} | all-to-all | bytes 458752 | tf_op jit(solution)/shard_map/all_to_all | solution.py:372
  127.9 0.0 copy-start.1
  127.9 36.3 %all_to_all.29 = f32[16,25,1,128]{3,2,1,0:T(1,128)S(1)} all-to-all(f32[16,25,1,128]{3,2,1,0:T(1,128)S(1)} %bitcast.20), channel_id=1, replica_groups=mesh['groups'=2,'blocks'=16,'pair'=2,'tm_1'=4,'space'=2] {'blocks'}, dimensions={0} | all-to-all | bytes 409600 | tf_op jit(solution)/shard_map/all_to_all | solution.py:376
  164.2 0.0 copy-done.1
  164.2 0.8 exit.1
  (2 shorter events, 0.0 us)
Async XLA Ops:
  0.6 81.1 %copy-start.3 = (f32[8,16,128]{2,1,0:T(8,128)S(1)}, f32[8,16,128]{2,1,0:T(8,128)}, u32[]{:S(2)}) copy-start(f32[8,16,128]{2,1,0:T(8,128)} %kappa.1) | copy-start | bytes 196612
  1.8 80.3 %copy-start = (f32[256,256]{1,0:T(8,128)S(1)}, f32[256,256]{1,0:T(8,128)}, u32[]{:S(2)}) copy-start(f32[256,256]{1,0:T(8,128)} %constant.42.clone.mat) | copy-start | bytes 786436
  94.3 4.7 %collective-permute-start = (f32[6,2,8,128]{3,2,1,0:T(8,128)S(1)}, f32[6,2,8,128]{3,2,1,0:T(8,128)S(1)}, u32[]{:S(2)}, u32[]{:S(2)}) collective-permute-start(f32[6,2,8,128]{3,2,1,0:T(8,128)S(1)} %get-tuple-element.30), channel_id=1, source_target_pairs={{0,16},{16,32},{32,48},{48,64},{64,80},{80,96},{96,112},{112,128},... | collective-permute-start | bytes 147464 | tf_op jit(solution)/shard_map/ppermute | solution.py:365
  97.0 7.4 %collective-permute-start.1 = (f32[6,2,8,128]{3,2,1,0:T(8,128)S(1)}, f32[6,2,8,128]{3,2,1,0:T(8,128)S(1)}, u32[]{:S(2)}, u32[]{:S(2)}) collective-permute-start(f32[6,2,8,128]{3,2,1,0:T(8,128)S(1)} %get-tuple-element.32), channel_id=1, source_target_pairs={{16,0},{32,16},{48,32},{64,48},{80,64},{96,80},{112,96},{128,112},... | collective-permute-start | bytes 147464 | tf_op jit(solution)/shard_map/ppermute | solution.py:365
  105.3 12.4 %copy-start.2 = (f32[256,128]{1,0:T(8,128)S(1)}, f32[256,128]{1,0:T(8,128)}, u32[]{:S(2)}) copy-start(f32[256,128]{1,0:T(8,128)} %constant.44.clone.mat) | copy-start | bytes 393220
  127.9 36.3 %copy-start.1 = (f32[1,8,16,128]{3,2,1,0:T(8,128)S(1)}, f32[1,8,16,128]{3,2,1,0:T(8,128)}, u32[]{:S(2)}) copy-start(f32[1,8,16,128]{3,2,1,0:T(8,128)} %param.6) | copy-start | bytes 196612
